TPU v7x, 768 devices: a whole 4x8x12 slice. The times are simulated.
768 devices in a mesh: dom: 64 (over x, y, core), sub: 12 (over z).
Axes of the slice: x: 4, y: 8, z: 12, core: 2. Of those that a mesh axis runs over, the one named last changes fastest.
Arguments:
- displacement: float32 [3, 1036800], P(None, ('dom', 'sub')), may hold values from -0.01 to 0.01
- velocity: float32 [3, 1036800], P(None, ('dom', 'sub')), may hold values from -3 to 3
- energy: float32 [27, 36864], P(None, ('dom', 'sub')), may hold values from 0.5 to 18, as said below
- mass_density: float32 [125, 36864], P(None, ('dom', 'sub')), may hold values from 0.5 to 4
- live_mask: int32 [36864], P(('dom', 'sub')), may hold values from 0 to 1, as said below
- time_step: float32 [], replicated, may hold values from 0.004 to 0.008
Outputs:
- new_velocity: float32 [3, 1036800], P(None, ('dom', 'sub'))
- energy_rate: float32 [27, 36864], P(None, ('dom', 'sub'))
- mesh_velocity: float32 [3, 1036800], P(None, ('dom', 'sub'))
Inputs may be any that keep to these rules, and one draw needn't show every extreme that they name: `energy`: internal energies are positive. `live_mask`: at most 36 element slots of one device are live, and some device has exactly 36.
All inputs are finite; a program needn't handle non-finite values.
Results may differ from a plain program's by a relative error of at most 0.0003.
Values sent between devices are 32-bit elements; how exact they have to be, the bound alone decides.
No kernel may reach another device: no remote copies, remote signals or barrier semaphores. Data moves between devices by JAX's collectives and lax.ppermute only.
A program may use at most 32 MiB of HBM per device.

v0:
```python
import functools
import math

import jax
import jax.numpy as jnp
import numpy as np
from jax import lax
from jax.sharding import Mesh
from jax.sharding import PartitionSpec as P

EX = 1
EY = 8
EZ = 6
CG_ITERS = 2
RELAX_PASSES = 2
DOM = ("dom_0", "dom_1", "dom_2")
DOM_SUB = ("dom_0", "dom_1", "dom_2", "sub")


highest = lax.Precision.HIGHEST
adiabatic = 5.0 / 3.0
viscosity = 0.3
mesh_step = 0.01


def from_behind(shard, axis, by):
    size = lax.axis_size(axis)
    pairs = [(i, i + by) for i in range(size) if 0 <= i + by < size]
    return lax.ppermute(shard, axis, pairs)


def over_axes(shard, axes):
    return functools.reduce(lax.psum, axes, shard)


def outer_triple(first, second, third):
    product = (
        first[:, None, None, :, None, None]
        * second[None, :, None, None, :, None]
        * third[None, None, :, None, None, :]
    )
    return product.reshape(
        first.shape[0] * second.shape[0] * third.shape[0],
        first.shape[1] * second.shape[1] * third.shape[1],
    )


def basis_tables():
    root_term = math.sqrt(10.0 / 7.0)
    gauss_roots = np.array(
        [
            -math.sqrt(5.0 + 2.0 * root_term) / 3.0,
            -math.sqrt(5.0 - 2.0 * root_term) / 3.0,
            0.0,
            math.sqrt(5.0 - 2.0 * root_term) / 3.0,
            math.sqrt(5.0 + 2.0 * root_term) / 3.0,
        ]
    )
    outer_weight = (322.0 - 13.0 * math.sqrt(70.0)) / 900.0
    middle_weight = (322.0 + 13.0 * math.sqrt(70.0)) / 900.0
    weights = (
        np.array([outer_weight, middle_weight, 128.0 / 225.0, middle_weight, outer_weight]) / 2.0
    )
    points = (1.0 + gauss_roots) / 2.0
    lobatto = [0.0, (1.0 - 1.0 / math.sqrt(5.0)) / 2.0, (1.0 + 1.0 / math.sqrt(5.0)) / 2.0, 1.0]
    values = np.ones((5, 4))
    slopes = np.zeros((5, 4))
    for node_index in range(4):
        for other_index in range(4):
            if other_index != node_index:
                values[:, node_index] *= (points - lobatto[other_index]) / (
                    lobatto[node_index] - lobatto[other_index]
                )
        for other_index in range(4):
            if other_index != node_index:
                factor_term = np.ones(5) / (lobatto[node_index] - lobatto[other_index])
                for third_index in range(4):
                    if third_index != node_index and third_index != other_index:
                        factor_term = (
                            factor_term
                            * (points - lobatto[third_index])
                            / (lobatto[node_index] - lobatto[third_index])
                        )
                slopes[:, node_index] += factor_term
    bernstein = np.stack([(1.0 - points) ** 2, 2.0 * points * (1.0 - points), points**2], axis=1)
    vel_basis = outer_triple(values, values, values)
    grad_table = np.concatenate(
        [
            outer_triple(slopes, values, values),
            outer_triple(values, slopes, values),
            outer_triple(values, values, slopes),
        ],
        axis=0,
    )
    energy_basis = outer_triple(bernstein, bernstein, bernstein)
    quad_weight = (
        weights[:, None, None] * weights[None, :, None] * weights[None, None, :]
    ).reshape(125)
    tables = (
        jnp.asarray(vel_basis, jnp.float32),
        jnp.asarray(grad_table, jnp.float32),
        jnp.asarray(energy_basis, jnp.float32),
        jnp.asarray(quad_weight, jnp.float32),
    )
    return (tables, lobatto)


def product_dot(left, right):
    return jnp.dot(left, right, precision=highest, preferred_element_type=jnp.float32)


def nodal_gradient(grad_table, nodal_values):
    element_count = nodal_values.shape[1] // 3
    shaped = product_dot(grad_table, nodal_values).reshape(3, 125, 3, element_count)
    return [
        [shaped[direction, :, component, :] for direction in range(3)] for component in range(3)
    ]


def cofactors(matrix):
    return [
        [
            matrix[(row_index + 1) % 3][(col_index + 1) % 3]
            * matrix[(row_index + 2) % 3][(col_index + 2) % 3]
            - matrix[(row_index + 1) % 3][(col_index + 2) % 3]
            * matrix[(row_index + 2) % 3][(col_index + 1) % 3]
            for col_index in range(3)
        ]
        for row_index in range(3)
    ]


def project(grad_table, fields):
    element_count = fields[0][0].shape[1]
    stacked = jnp.stack(
        [
            jnp.stack([fields[component][direction] for component in range(3)], axis=1)
            for direction in range(3)
        ],
        axis=0,
    )
    return product_dot(grad_table.T, stacked.reshape(375, 3 * element_count))


def lagrange_rates(coords, speeds, energy, mass_density, live_values, tables):
    vel_basis, grad_table, energy_basis, quad_weight = tables
    jacobian = nodal_gradient(grad_table, coords)
    velocity_grad = nodal_gradient(grad_table, speeds)
    cofactor = cofactors(jacobian)
    volume = (
        jacobian[0][0] * cofactor[0][0]
        + jacobian[0][1] * cofactor[0][1]
        + jacobian[0][2] * cofactor[0][2]
    )
    density = mass_density / volume
    pressure = (adiabatic - 1.0) * density * product_dot(energy_basis, energy)
    spatial = [
        [
            (
                velocity_grad[component][0] * cofactor[direction][0]
                + velocity_grad[component][1] * cofactor[direction][1]
                + velocity_grad[component][2] * cofactor[direction][2]
            )
            / volume
            for direction in range(3)
        ]
        for component in range(3)
    ]
    stress = [
        [
            viscosity * density * (spatial[component][direction] + spatial[direction][component])
            - (pressure if component == direction else 0.0)
            for direction in range(3)
        ]
        for component in range(3)
    ]
    weight = quad_weight[:, None] * live_values[None, :]
    flux_terms = [
        [
            weight
            * (
                stress[component][0] * cofactor[0][direction]
                + stress[component][1] * cofactor[1][direction]
                + stress[component][2] * cofactor[2][direction]
            )
            for direction in range(3)
        ]
        for component in range(3)
    ]
    node_force = -project(grad_table, flux_terms)
    power_density = stress[0][0] * spatial[0][0]
    for component in range(3):
        for direction in range(3):
            if component + direction > 0:
                power_density = (
                    power_density + stress[component][direction] * spatial[component][direction]
                )
    power_density = weight * volume * power_density
    lumped = product_dot(energy_basis.T, quad_weight[:, None] * mass_density)
    return (node_force, product_dot(energy_basis.T, power_density) / lumped)


def mass_apply(nodal_values, mass_weight, vel_basis):
    element_count = mass_weight.shape[1]
    at_points = (
        product_dot(vel_basis, nodal_values).reshape(125, 3, element_count)
        * mass_weight[:, None, :]
    )
    return product_dot(vel_basis.T, at_points.reshape(125, 3 * element_count))


def shape_gradient(coords, live_values, tables):
    vel_basis, grad_table, energy_basis, quad_weight = tables
    jacobian = nodal_gradient(grad_table, coords)
    cofactor = cofactors(jacobian)
    volume = (
        jacobian[0][0] * cofactor[0][0]
        + jacobian[0][1] * cofactor[0][1]
        + jacobian[0][2] * cofactor[0][2]
    )
    norm_sq = jacobian[0][0] * jacobian[0][0]
    for component in range(3):
        for direction in range(3):
            if component + direction > 0:
                norm_sq = norm_sq + jacobian[component][direction] * jacobian[component][direction]
    ratio_term = norm_sq / volume
    weight = quad_weight[:, None] * live_values[None, :] * volume ** (-2.0 / 3.0)
    fields = [
        [
            weight
            * (
                2.0 / 3.0 * jacobian[component][direction]
                - 2.0 / 9.0 * ratio_term * cofactor[component][direction]
            )
            for direction in range(3)
        ]
        for component in range(3)
    ]
    return project(grad_table, fields)


def correlation_take(grid, axis_place):
    rotated = jnp.moveaxis(grid, axis_place, -1)
    block_count = (rotated.shape[-1] - 1) // 3
    main_part = rotated[..., : 3 * block_count].reshape(rotated.shape[:-1] + (block_count, 3))
    edge_part = rotated[..., 3::3][..., None]
    return jnp.concatenate([main_part, edge_part], axis=-1)


def correlation_add(pieces):
    block_count = pieces.shape[-2]
    block_width = pieces.shape[-1] - 1
    leading = pieces.shape[:-2]
    main_part = pieces[..., :block_width].reshape(leading + (block_count * block_width,))
    main_part = jnp.pad(main_part, [(0, 0)] * len(leading) + [(0, 1)])
    edge_part = jnp.pad(
        pieces[..., block_width:], [(0, 0)] * (len(leading) + 1) + [(0, block_width - 1)]
    )
    edge_part = edge_part.reshape(leading + (block_count * block_width,))
    edge_part = jnp.pad(edge_part, [(0, 0)] * len(leading) + [(block_width, 0)])[
        ..., : block_count * block_width + 1
    ]
    return main_part + edge_part


def to_elements(grid):
    pieces = correlation_take(grid, 1)
    pieces = correlation_take(pieces, 1)
    pieces = correlation_take(pieces, 1)
    pieces = pieces.transpose(2, 4, 6, 0, 1, 3, 5)
    return pieces.reshape(64, 3 * EX * EY * EZ)


def to_grid(nodal_values):
    pieces = nodal_values.reshape(4, 4, 4, 3, EX, EY, EZ).transpose(3, 4, 0, 5, 1, 6, 2)
    pieces = correlation_add(pieces)
    pieces = correlation_add(jnp.moveaxis(pieces, (3, 4), (4, 5)))
    pieces = correlation_add(jnp.moveaxis(pieces, (1, 2), (3, 4)))
    return pieces.transpose(0, 3, 2, 1)


def lattice_axis(start_at, extent, lobatto):
    number = start_at + lax.iota(jnp.int32, extent)
    remainder = number % 3
    offset = jnp.where(remainder == 1, lobatto[1], jnp.where(remainder == 2, lobatto[2], 0.0))
    return (number // 3).astype(jnp.float32) + offset


def lattice_grid(start_x, start_z, extent_x, extent_y, extent_z, lobatto):
    along_x = lattice_axis(start_x, extent_x, lobatto)
    along_y = lattice_axis(0, extent_y, lobatto)
    along_z = lattice_axis(start_z, extent_z, lobatto)
    grid_shape = (extent_x, extent_y, extent_z)
    return jnp.stack(
        [
            jnp.broadcast_to(along_x[:, None, None], grid_shape),
            jnp.broadcast_to(along_y[None, :, None], grid_shape),
            jnp.broadcast_to(along_z[None, None, :], grid_shape),
        ]
    )


def body(displacement, velocity, energy, mass_density, live_mask, time_step):
    tables, lobatto = basis_tables()
    vel_basis, grad_table, energy_basis, quad_weight = tables
    planes_x = 3 * EX
    planes_y = 3 * EY + 1
    planes_z = 3 * EZ
    element_count = live_mask.shape[0]
    dom_place = lax.axis_index(DOM)
    sub_place = lax.axis_index("sub")
    owned_disp = displacement.reshape(3, planes_x, planes_y, planes_z)
    owned_vel = velocity.reshape(3, planes_x, planes_y, planes_z)
    lattice = lattice_grid(
        planes_x * dom_place, planes_z * sub_place, planes_x + 1, planes_y, planes_z + 1, lobatto
    )
    live_values = live_mask.astype(jnp.float32)

    def select_nodal(nodal_values):
        return nodal_values.reshape(64, 3, element_count).reshape(64, -1)

    def restore_nodal(nodal_values):
        return nodal_values.reshape(64, 3, -1).reshape(64, 3 * element_count)

    def spread(owned_grid):
        top_z = from_behind(owned_grid[..., -1:], "sub", 1)
        widened = jnp.concatenate([top_z, owned_grid], axis=3)
        top_x = from_behind(widened[:, -1:], DOM, 1)
        return jnp.concatenate([top_x, widened], axis=1)

    def collect(local_grid):
        low_x = from_behind(local_grid[:, :1], DOM, -1)
        summed = local_grid.at[:, -1:].add(low_x)[:, 1:]
        low_z = from_behind(summed[..., :1], "sub", -1)
        return summed.at[..., -1:].add(low_z)[..., 1:]

    def as_local(vector):
        return spread(vector)

    initial_fields = spread(jnp.concatenate([owned_disp, owned_vel], axis=0))
    coords = to_elements(lattice + initial_fields[:3])
    speeds = to_elements(initial_fields[3:])
    force_packed, rate_packed = lagrange_rates(
        select_nodal(coords), select_nodal(speeds), energy, mass_density, live_values, tables
    )
    node_force = collect(to_grid(restore_nodal(force_packed)))
    mass_weight = quad_weight[:, None] * mass_density * live_values[None, :]

    def mass_operator(vector):
        nodal_values = select_nodal(to_elements(as_local(vector)))
        return collect(to_grid(restore_nodal(mass_apply(nodal_values, mass_weight, vel_basis))))

    def inner_sum(left, right):
        return jnp.sum(left * right)

    def paired_sums(residual, mass_image):
        return (
            over_axes(inner_sum(residual, residual), DOM_SUB),
            over_axes(inner_sum(residual, mass_image), DOM_SUB),
        )

    solution = jnp.zeros_like(node_force)
    residual = node_force
    mass_image = mass_operator(residual)
    norm_now, product = paired_sums(residual, mass_image)
    step_length = norm_now / product
    direction = residual
    mass_direction = mass_image
    for iteration in range(CG_ITERS):
        solution = solution + step_length * direction
        residual = residual - step_length * mass_direction
        if iteration + 1 < CG_ITERS:
            mass_image = mass_operator(residual)
            norm_next, product = paired_sums(residual, mass_image)
            conjugacy = norm_next / norm_now
            step_length = norm_next / (product - conjugacy * norm_next / step_length)
            direction = residual + conjugacy * direction
            mass_direction = mass_image + conjugacy * mass_direction
            norm_now = norm_next
    new_velocity = owned_vel + time_step * solution
    moved_disp = owned_disp + time_step * new_velocity
    gradient_sum = jnp.zeros_like(moved_disp)
    for relax_pass in range(RELAX_PASSES):
        shape_coords = select_nodal(to_elements(lattice + as_local(moved_disp)))
        gradient = collect(
            to_grid(restore_nodal(shape_gradient(shape_coords, live_values, tables)))
        )
        gradient_sum = gradient_sum + gradient
        if relax_pass + 1 < RELAX_PASSES:
            moved_disp = moved_disp - mesh_step * gradient
    mesh_velocity = new_velocity - mesh_step / time_step * gradient_sum
    return (new_velocity.reshape(3, -1), rate_packed, mesh_velocity.reshape(3, -1))


def solution(mesh):
    finer = Mesh(
        mesh.devices.reshape(4, 8, 2, mesh.shape["sub"]), ("dom_0", "dom_1", "dom_2", "sub")
    )
    return jax.shard_map(
        body,
        mesh=finer,
        in_specs=(
            P(None, DOM_SUB),
            P(None, DOM_SUB),
            P(None, DOM_SUB),
            P(None, DOM_SUB),
            P(DOM_SUB),
            P(),
        ),
        out_specs=(P(None, DOM_SUB), P(None, DOM_SUB), P(None, DOM_SUB)),
        check_vma=False,
    )
```

profile of v0, /device:TPU:57, one launch (start us, length us, event | category | flops | bytes accessed | tf_op | source)
XLA Modules:
  0.0 318.0 jit_solution(12667763642854396733)
XLA Ops:
  1.9 4.0 %collective-permute-start = (f32[6,3,25,1]{3,2,1,0:T(8,128)S(1)}, f32[6,3,25,1]{3,2,1,0:T(8,128)S(1)}, u32[]{:S(2)}, u32[]{:S(2)}) collective-permute-start(f32[6,3,25,1]{3,2,1,0:T(8,128)S(1)} %slice.910), channel_id=1, source_target_pairs={{0,1},{1,2},{2,3},{3,4},{4,5},{5,6},{6,7},{7,8},{8,9},{9,10},{10,1... | collective-permute-start | bytes 5408 | tf_op jit(solution)/shard_map/ppermute | solution.py:29
  6.0 5.6 %collective-permute-done = f32[6,3,25,1]{3,2,1,0:T(8,128)S(1)} collective-permute-done((f32[6,3,25,1]{3,2,1,0:T(8,128)S(1)}, f32[6,3,25,1]{3,2,1,0:T(8,128)S(1)}, u32[]{:S(2)}, u32[]{:S(2)}) %collective-permute-start) | collective-permute-done | bytes 1832 | tf_op jit(solution)/shard_map/ppermute | solution.py:29
  37.8 4.0 %collective-permute-start.2 = (f32[3,1,25,19]{3,2,1,0:T(8,128)S(1)}, f32[3,1,25,19]{3,2,1,0:T(8,128)S(1)}, u32[]{:S(2)}, u32[]{:S(2)}) collective-permute-start(f32[3,1,25,19]{3,2,1,0:T(8,128)S(1)} %slice.946), channel_id=1, source_target_pairs={{12,0},{24,12},{36,24},{48,36},{60,48},{72,60},{84,72},{96,84},{10... | collective-permute-start | bytes 17108 | tf_op jit(solution)/shard_map/ppermute | solution.py:29
  41.9 4.1 %collective-permute-done.2 = f32[3,1,25,19]{3,2,1,0:T(8,128)S(1)} collective-permute-done((f32[3,1,25,19]{3,2,1,0:T(8,128)S(1)}, f32[3,1,25,19]{3,2,1,0:T(8,128)S(1)}, u32[]{:S(2)}, u32[]{:S(2)}) %collective-permute-start.2) | collective-permute-done | bytes 5732 | tf_op jit(solution)/shard_map/ppermute | solution.py:29
  47.4 5.3 %collective-permute-done.3 = f32[3,3,25,1]{3,2,1,0:T(8,128)S(1)} collective-permute-done((f32[3,3,25,1]{3,2,1,0:T(8,128)S(1)}, f32[3,3,25,1]{3,2,1,0:T(8,128)S(1)}, u32[]{:S(2)}, u32[]{:S(2)}) %collective-permute-start.3) | collective-permute-done | bytes 932 | tf_op jit(solution)/shard_map/ppermute | solution.py:29
  52.8 4.0 %collective-permute-start.4 = (f32[3,3,25,1]{3,2,1,0:T(8,128)S(1)}, f32[3,3,25,1]{3,2,1,0:T(8,128)S(1)}, u32[]{:S(2)}, u32[]{:S(2)}) collective-permute-start(f32[3,3,25,1]{3,2,1,0:T(8,128)S(1)} %slice_add_fusion.6), channel_id=1, source_target_pairs={{0,1},{1,2},{2,3},{3,4},{4,5},{5,6},{6,7},{7,8},{8,9},{9,10},{10,1... | collective-permute-start | bytes 2708 | tf_op jit(solution)/shard_map/ppermute | solution.py:29
  75.8 6.1 %collective-permute-done.6 = f32[3,1,25,19]{3,2,1,0:T(8,128)S(1)} collective-permute-done((f32[3,1,25,19]{3,2,1,0:T(8,128)S(1)}, f32[3,1,25,19]{3,2,1,0:T(8,128)S(1)}, u32[]{:S(2)}, u32[]{:S(2)}) %collective-permute-start.6) | collective-permute-done | bytes 5732 | tf_op jit(solution)/shard_map/ppermute | solution.py:29
  83.3 6.3 %collective-permute-done.7 = f32[3,3,25,1]{3,2,1,0:T(8,128)S(1)} collective-permute-done((f32[3,3,25,1]{3,2,1,0:T(8,128)S(1)}, f32[3,3,25,1]{3,2,1,0:T(8,128)S(1)}, u32[]{:S(2)}, u32[]{:S(2)}) %collective-permute-start.7) | collective-permute-done | bytes 932 | tf_op jit(solution)/shard_map/ppermute | solution.py:29
  91.3 7.8 %all-reduce.50 = (f32[]{:T(128)}, f32[]{:T(128)}) all-reduce(f32[]{:T(128)} %get-tuple-element.126, f32[]{:T(128)} %get-tuple-element.125), channel_id=1, replica_groups=mesh['dom_0'=4,'dom_1'=8,'dom_2'=2,'sub'=12] {'dom_0'}, use_global_device_ids=true, to_apply=%region_1.2 | all-reduce | flops 2 | bytes 16 | tf_op jit(solution)/shard_map/psum | solution.py:33
  99.1 12.1 %all-reduce.48 = (f32[]{:T(128)}, f32[]{:T(128)}) all-reduce(f32[]{:T(128)} %get-tuple-element.137, f32[]{:T(128)} %get-tuple-element.138), channel_id=1, replica_groups=mesh['dom_0'=4,'dom_1'=8,'dom_2'=2,'sub'=12] {'dom_1'}, use_global_device_ids=true, to_apply=%region_2.3 | all-reduce | flops 2 | bytes 16 | tf_op jit(solution)/shard_map/psum | solution.py:33
  111.2 9.2 %all-reduce.52 = (f32[]{:T(128)}, f32[]{:T(128)}) all-reduce(f32[]{:T(128)} %get-tuple-element.133, f32[]{:T(128)} %get-tuple-element.134), channel_id=1, replica_groups=mesh['dom_0'=4,'dom_1'=8,'dom_2'=2,'sub'=12] {'dom_2'}, use_global_device_ids=true, to_apply=%region_3.4 | all-reduce | flops 2 | bytes 16 | tf_op jit(solution)/shard_map/psum | solution.py:33
  120.4 25.6 %all-reduce.46 = (f32[]{:T(128)}, f32[]{:T(128)}) all-reduce(f32[]{:T(128)} %get-tuple-element.141, f32[]{:T(128)} %get-tuple-element.142), channel_id=1, replica_groups=mesh['dom_0'=4,'dom_1'=8,'dom_2'=2,'sub'=12] {'sub'}, use_global_device_ids=true, to_apply=%region_4.5 | all-reduce | flops 2 | bytes 16 | tf_op jit(solution)/shard_map/psum | solution.py:33
  151.6 9.1 %collective-permute-start.9 = (f32[3,1,25,19]{3,2,1,0:T(8,128)S(1)}, f32[3,1,25,19]{3,2,1,0:T(8,128)S(1)}, u32[]{:S(2)}, u32[]{:S(2)}) collective-permute-start(f32[3,1,25,19]{3,2,1,0:T(8,128)S(1)} %pad_maximum_fusion.7), channel_id=1, source_target_pairs={{0,12},{12,24},{24,36},{36,48},{48,60},{60,72},{72,84},{84,96},{96... | collective-permute-start | bytes 17108 | tf_op jit(solution)/shard_map/ppermute | solution.py:29
  174.4 4.4 %collective-permute-done.10 = f32[3,1,25,19]{3,2,1,0:T(8,128)S(1)} collective-permute-done((f32[3,1,25,19]{3,2,1,0:T(8,128)S(1)}, f32[3,1,25,19]{3,2,1,0:T(8,128)S(1)}, u32[]{:S(2)}, u32[]{:S(2)}) %collective-permute-start.10) | collective-permute-done | bytes 5732 | tf_op jit(solution)/shard_map/ppermute | solution.py:29
  180.8 4.7 %collective-permute-done.11 = f32[3,3,25,1]{3,2,1,0:T(8,128)S(1)} collective-permute-done((f32[3,3,25,1]{3,2,1,0:T(8,128)S(1)}, f32[3,3,25,1]{3,2,1,0:T(8,128)S(1)}, u32[]{:S(2)}, u32[]{:S(2)}) %collective-permute-start.11) | collective-permute-done | bytes 932 | tf_op jit(solution)/shard_map/ppermute | solution.py:29
  187.0 7.6 %all-reduce.49 = (f32[]{:T(128)}, f32[]{:T(128)}) all-reduce(f32[]{:T(128)} %get-tuple-element.124, f32[]{:T(128)} %get-tuple-element.123), channel_id=1, replica_groups=mesh['dom_0'=4,'dom_1'=8,'dom_2'=2,'sub'=12] {'dom_0'}, use_global_device_ids=true, to_apply=%region_11.12 | all-reduce | flops 2 | bytes 16 | tf_op jit(solution)/shard_map/psum | solution.py:33
  194.6 11.1 %all-reduce.47 = (f32[]{:T(128)}, f32[]{:T(128)}) all-reduce(f32[]{:T(128)} %get-tuple-element.135, f32[]{:T(128)} %get-tuple-element.136), channel_id=1, replica_groups=mesh['dom_0'=4,'dom_1'=8,'dom_2'=2,'sub'=12] {'dom_1'}, use_global_device_ids=true, to_apply=%region_12.13 | all-reduce | flops 2 | bytes 16 | tf_op jit(solution)/shard_map/psum | solution.py:33
  205.8 8.5 %all-reduce.51 = (f32[]{:T(128)}, f32[]{:T(128)}) all-reduce(f32[]{:T(128)} %get-tuple-element.131, f32[]{:T(128)} %get-tuple-element.132), channel_id=1, replica_groups=mesh['dom_0'=4,'dom_1'=8,'dom_2'=2,'sub'=12] {'dom_2'}, use_global_device_ids=true, to_apply=%region_13.14 | all-reduce | flops 2 | bytes 16 | tf_op jit(solution)/shard_map/psum | solution.py:33
  214.3 19.9 %all-reduce.45 = (f32[]{:T(128)}, f32[]{:T(128)}) all-reduce(f32[]{:T(128)} %get-tuple-element.139, f32[]{:T(128)} %get-tuple-element.140), channel_id=1, replica_groups=mesh['dom_0'=4,'dom_1'=8,'dom_2'=2,'sub'=12] {'sub'}, use_global_device_ids=true, to_apply=%region_14.15 | all-reduce | flops 2 | bytes 16 | tf_op jit(solution)/shard_map/psum | solution.py:33
  243.4 10.5 %collective-permute-start.13 = (f32[3,1,25,19]{3,2,1,0:T(8,128)S(1)}, f32[3,1,25,19]{3,2,1,0:T(8,128)S(1)}, u32[]{:S(2)}, u32[]{:S(2)}) collective-permute-start(f32[3,1,25,19]{3,2,1,0:T(8,128)S(1)} %pad_maximum_fusion.6), channel_id=1, source_target_pairs={{0,12},{12,24},{24,36},{36,48},{48,60},{60,72},{72,84},{84,96},{96... | collective-permute-start | bytes 17108 | tf_op jit(solution)/shard_map/ppermute | solution.py:29
  267.0 5.9 %collective-permute-done.14 = f32[3,1,25,19]{3,2,1,0:T(8,128)S(1)} collective-permute-done((f32[3,1,25,19]{3,2,1,0:T(8,128)S(1)}, f32[3,1,25,19]{3,2,1,0:T(8,128)S(1)}, u32[]{:S(2)}, u32[]{:S(2)}) %collective-permute-start.14) | collective-permute-done | bytes 5732 | tf_op jit(solution)/shard_map/ppermute | solution.py:29
  274.2 5.3 %collective-permute-done.15 = f32[3,3,25,1]{3,2,1,0:T(8,128)S(1)} collective-permute-done((f32[3,3,25,1]{3,2,1,0:T(8,128)S(1)}, f32[3,3,25,1]{3,2,1,0:T(8,128)S(1)}, u32[]{:S(2)}, u32[]{:S(2)}) %collective-permute-start.15) | collective-permute-done | bytes 932 | tf_op jit(solution)/shard_map/ppermute | solution.py:29
  286.2 4.1 %collective-permute-start.17 = (f32[3,1,25,19]{3,2,1,0:T(8,128)S(1)}, f32[3,1,25,19]{3,2,1,0:T(8,128)S(1)}, u32[]{:S(2)}, u32[]{:S(2)}) collective-permute-start(f32[3,1,25,19]{3,2,1,0:T(8,128)S(1)} %pad_maximum_fusion.5), channel_id=1, source_target_pairs={{0,12},{12,24},{24,36},{36,48},{48,60},{60,72},{72,84},{84,96},{96... | collective-permute-start | bytes 17108 | tf_op jit(solution)/shard_map/ppermute | solution.py:29
  303.6 5.8 %collective-permute-done.18 = f32[3,1,25,19]{3,2,1,0:T(8,128)S(1)} collective-permute-done((f32[3,1,25,19]{3,2,1,0:T(8,128)S(1)}, f32[3,1,25,19]{3,2,1,0:T(8,128)S(1)}, u32[]{:S(2)}, u32[]{:S(2)}) %collective-permute-start.18) | collective-permute-done | bytes 5732 | tf_op jit(solution)/shard_map/ppermute | solution.py:29
  (345 shorter events, 117.6 us)
Async XLA Ops:
  0.6 31.5 %copy-start = (f32[27,48]{1,0:T(8,128)S(1)}, f32[27,48]{1,0:T(8,128)}, u32[]{:S(2)}) copy-start(f32[27,48]{1,0:T(8,128)} %param.32) | copy-start | bytes 15556
  1.9 9.7 %collective-permute-start = (f32[6,3,25,1]{3,2,1,0:T(8,128)S(1)}, f32[6,3,25,1]{3,2,1,0:T(8,128)S(1)}, u32[]{:S(2)}, u32[]{:S(2)}) collective-permute-start(f32[6,3,25,1]{3,2,1,0:T(8,128)S(1)} %slice.910), channel_id=1, source_target_pairs={{0,1},{1,2},{2,3},{3,4},{4,5},{5,6},{6,7},{7,8},{8,9},{9,10},{10,1... | collective-permute-start | bytes 5408 | tf_op jit(solution)/shard_map/ppermute | solution.py:29
  11.7 3.8 %copy-start.13 = (s32[48]{0:T(128)S(1)}, s32[48]{0:T(128)}, u32[]{:S(2)}) copy-start(s32[48]{0:T(128)} %param.34) | copy-start | bytes 580
  11.7 5.4 %collective-permute-start.1 = (f32[6,1,25,19]{3,2,1,0:T(8,128)S(1)}, f32[6,1,25,19]{3,2,1,0:T(8,128)S(1)}, u32[]{:S(2)}, u32[]{:S(2)}) collective-permute-start(f32[6,1,25,19]{3,2,1,0:T(8,128)S(1)} %pad_maximum_fusion.4), channel_id=1, source_target_pairs={{0,12},{12,24},{24,36},{36,48},{48,60},{60,72},{72,84},{84,96},{96... | collective-permute-start | bytes 34208 | tf_op jit(solution)/shard_map/ppermute | solution.py:29
  37.8 8.2 %collective-permute-start.2 = (f32[3,1,25,19]{3,2,1,0:T(8,128)S(1)}, f32[3,1,25,19]{3,2,1,0:T(8,128)S(1)}, u32[]{:S(2)}, u32[]{:S(2)}) collective-permute-start(f32[3,1,25,19]{3,2,1,0:T(8,128)S(1)} %slice.946), channel_id=1, source_target_pairs={{12,0},{24,12},{36,24},{48,36},{60,48},{72,60},{84,72},{96,84},{10... | collective-permute-start | bytes 17108 | tf_op jit(solution)/shard_map/ppermute | solution.py:29
  46.1 6.6 %collective-permute-start.3 = (f32[3,3,25,1]{3,2,1,0:T(8,128)S(1)}, f32[3,3,25,1]{3,2,1,0:T(8,128)S(1)}, u32[]{:S(2)}, u32[]{:S(2)}) collective-permute-start(f32[3,3,25,1]{3,2,1,0:T(8,128)S(1)} %slice.949), channel_id=1, source_target_pairs={{1,0},{2,1},{3,2},{4,3},{5,4},{6,5},{7,6},{8,7},{9,8},{10,9},{11,1... | collective-permute-start | bytes 2708 | tf_op jit(solution)/shard_map/ppermute | solution.py:29
  52.8 6.5 %collective-permute-start.4 = (f32[3,3,25,1]{3,2,1,0:T(8,128)S(1)}, f32[3,3,25,1]{3,2,1,0:T(8,128)S(1)}, u32[]{:S(2)}, u32[]{:S(2)}) collective-permute-start(f32[3,3,25,1]{3,2,1,0:T(8,128)S(1)} %slice_add_fusion.6), channel_id=1, source_target_pairs={{0,1},{1,2},{2,3},{3,4},{4,5},{5,6},{6,7},{7,8},{8,9},{9,10},{10,1... | collective-permute-start | bytes 2708 | tf_op jit(solution)/shard_map/ppermute | solution.py:29
  59.4 4.8 %collective-permute-start.5 = (f32[3,1,25,19]{3,2,1,0:T(8,128)S(1)}, f32[3,1,25,19]{3,2,1,0:T(8,128)S(1)}, u32[]{:S(2)}, u32[]{:S(2)}) collective-permute-start(f32[3,1,25,19]{3,2,1,0:T(8,128)S(1)} %pad_maximum_fusion.8), channel_id=1, source_target_pairs={{0,12},{12,24},{24,36},{36,48},{48,60},{60,72},{72,84},{84,96},{96... | collective-permute-start | bytes 17108 | tf_op jit(solution)/shard_map/ppermute | solution.py:29
  73.8 8.1 %collective-permute-start.6 = (f32[3,1,25,19]{3,2,1,0:T(8,128)S(1)}, f32[3,1,25,19]{3,2,1,0:T(8,128)S(1)}, u32[]{:S(2)}, u32[]{:S(2)}) collective-permute-start(f32[3,1,25,19]{3,2,1,0:T(8,128)S(1)} %slice.962), channel_id=1, source_target_pairs={{12,0},{24,12},{36,24},{48,36},{60,48},{72,60},{84,72},{96,84},{10... | collective-permute-start | bytes 17108 | tf_op jit(solution)/shard_map/ppermute | solution.py:29
  82.0 7.6 %collective-permute-start.7 = (f32[3,3,25,1]{3,2,1,0:T(8,128)S(1)}, f32[3,3,25,1]{3,2,1,0:T(8,128)S(1)}, u32[]{:S(2)}, u32[]{:S(2)}) collective-permute-start(f32[3,3,25,1]{3,2,1,0:T(8,128)S(1)} %slice.965), channel_id=1, source_target_pairs={{1,0},{2,1},{3,2},{4,3},{5,4},{6,5},{7,6},{8,7},{9,8},{10,9},{11,1... | collective-permute-start | bytes 2708 | tf_op jit(solution)/shard_map/ppermute | solution.py:29
  147.5 4.0 %collective-permute-start.8 = (f32[3,3,25,1]{3,2,1,0:T(8,128)S(1)}, f32[3,3,25,1]{3,2,1,0:T(8,128)S(1)}, u32[]{:S(2)}, u32[]{:S(2)}) collective-permute-start(f32[3,3,25,1]{3,2,1,0:T(8,128)S(1)} %slice.967), channel_id=1, source_target_pairs={{0,1},{1,2},{2,3},{3,4},{4,5},{5,6},{6,7},{7,8},{8,9},{9,10},{10,1... | collective-permute-start | bytes 2708 | tf_op jit(solution)/shard_map/ppermute | solution.py:29
  151.6 10.3 %collective-permute-start.9 = (f32[3,1,25,19]{3,2,1,0:T(8,128)S(1)}, f32[3,1,25,19]{3,2,1,0:T(8,128)S(1)}, u32[]{:S(2)}, u32[]{:S(2)}) collective-permute-start(f32[3,1,25,19]{3,2,1,0:T(8,128)S(1)} %pad_maximum_fusion.7), channel_id=1, source_target_pairs={{0,12},{12,24},{24,36},{36,48},{48,60},{60,72},{72,84},{84,96},{96... | collective-permute-start | bytes 17108 | tf_op jit(solution)/shard_map/ppermute | solution.py:29
  170.6 8.1 %collective-permute-start.10 = (f32[3,1,25,19]{3,2,1,0:T(8,128)S(1)}, f32[3,1,25,19]{3,2,1,0:T(8,128)S(1)}, u32[]{:S(2)}, u32[]{:S(2)}) collective-permute-start(f32[3,1,25,19]{3,2,1,0:T(8,128)S(1)} %slice.979), channel_id=1, source_target_pairs={{12,0},{24,12},{36,24},{48,36},{60,48},{72,60},{84,72},{96,84},{10... | collective-permute-start | bytes 17108 | tf_op jit(solution)/shard_map/ppermute | solution.py:29
  178.8 6.6 %collective-permute-start.11 = (f32[3,3,25,1]{3,2,1,0:T(8,128)S(1)}, f32[3,3,25,1]{3,2,1,0:T(8,128)S(1)}, u32[]{:S(2)}, u32[]{:S(2)}) collective-permute-start(f32[3,3,25,1]{3,2,1,0:T(8,128)S(1)} %slice.982), channel_id=1, source_target_pairs={{1,0},{2,1},{3,2},{4,3},{5,4},{6,5},{7,6},{8,7},{9,8},{10,9},{11,1... | collective-permute-start | bytes 2708 | tf_op jit(solution)/shard_map/ppermute | solution.py:29
  238.8 4.5 %collective-permute-start.12 = (f32[3,3,25,1]{3,2,1,0:T(8,128)S(1)}, f32[3,3,25,1]{3,2,1,0:T(8,128)S(1)}, u32[]{:S(2)}, u32[]{:S(2)}) collective-permute-start(f32[3,3,25,1]{3,2,1,0:T(8,128)S(1)} %slice.984), channel_id=1, source_target_pairs={{0,1},{1,2},{2,3},{3,4},{4,5},{5,6},{6,7},{7,8},{8,9},{9,10},{10,1... | collective-permute-start | bytes 2708 | tf_op jit(solution)/shard_map/ppermute | solution.py:29
  243.4 11.5 %collective-permute-start.13 = (f32[3,1,25,19]{3,2,1,0:T(8,128)S(1)}, f32[3,1,25,19]{3,2,1,0:T(8,128)S(1)}, u32[]{:S(2)}, u32[]{:S(2)}) collective-permute-start(f32[3,1,25,19]{3,2,1,0:T(8,128)S(1)} %pad_maximum_fusion.6), channel_id=1, source_target_pairs={{0,12},{12,24},{24,36},{36,48},{48,60},{60,72},{72,84},{84,96},{96... | collective-permute-start | bytes 17108 | tf_op jit(solution)/shard_map/ppermute | solution.py:29
  264.7 8.1 %collective-permute-start.14 = (f32[3,1,25,19]{3,2,1,0:T(8,128)S(1)}, f32[3,1,25,19]{3,2,1,0:T(8,128)S(1)}, u32[]{:S(2)}, u32[]{:S(2)}) collective-permute-start(f32[3,1,25,19]{3,2,1,0:T(8,128)S(1)} %slice.1005), channel_id=1, source_target_pairs={{12,0},{24,12},{36,24},{48,36},{60,48},{72,60},{84,72},{96,84},{10... | collective-permute-start | bytes 17108 | tf_op jit(solution)/shard_map/ppermute | solution.py:29
  272.9 6.6 %collective-permute-start.15 = (f32[3,3,25,1]{3,2,1,0:T(8,128)S(1)}, f32[3,3,25,1]{3,2,1,0:T(8,128)S(1)}, u32[]{:S(2)}, u32[]{:S(2)}) collective-permute-start(f32[3,3,25,1]{3,2,1,0:T(8,128)S(1)} %slice.1008), channel_id=1, source_target_pairs={{1,0},{2,1},{3,2},{4,3},{5,4},{6,5},{7,6},{8,7},{9,8},{10,9},{11,1... | collective-permute-start | bytes 2708 | tf_op jit(solution)/shard_map/ppermute | solution.py:29
  280.6 5.5 %collective-permute-start.16 = (f32[3,3,25,1]{3,2,1,0:T(8,128)S(1)}, f32[3,3,25,1]{3,2,1,0:T(8,128)S(1)}, u32[]{:S(2)}, u32[]{:S(2)}) collective-permute-start(f32[3,3,25,1]{3,2,1,0:T(8,128)S(1)} %slice.1010), channel_id=1, source_target_pairs={{0,1},{1,2},{2,3},{3,4},{4,5},{5,6},{6,7},{7,8},{8,9},{9,10},{10,1... | collective-permute-start | bytes 2708 | tf_op jit(solution)/shard_map/ppermute | solution.py:29
  286.2 5.3 %collective-permute-start.17 = (f32[3,1,25,19]{3,2,1,0:T(8,128)S(1)}, f32[3,1,25,19]{3,2,1,0:T(8,128)S(1)}, u32[]{:S(2)}, u32[]{:S(2)}) collective-permute-start(f32[3,1,25,19]{3,2,1,0:T(8,128)S(1)} %pad_maximum_fusion.5), channel_id=1, source_target_pairs={{0,12},{12,24},{24,36},{36,48},{48,60},{60,72},{72,84},{84,96},{96... | collective-permute-start | bytes 17108 | tf_op jit(solution)/shard_map/ppermute | solution.py:29
  301.3 2.0 copy-start.10
  301.3 2.0 copy-start.6
  301.4 8.1 %collective-permute-start.18 = (f32[3,1,25,19]{3,2,1,0:T(8,128)S(1)}, f32[3,1,25,19]{3,2,1,0:T(8,128)S(1)}, u32[]{:S(2)}, u32[]{:S(2)}) collective-permute-start(f32[3,1,25,19]{3,2,1,0:T(8,128)S(1)} %slice.1031), channel_id=1, source_target_pairs={{12,0},{24,12},{36,24},{48,36},{60,48},{72,60},{84,72},{96,84},{10... | collective-permute-start | bytes 17108 | tf_op jit(solution)/shard_map/ppermute | solution.py:29
  309.5 6.6 %collective-permute-start.19 = (f32[3,3,25,1]{3,2,1,0:T(8,128)S(1)}, f32[3,3,25,1]{3,2,1,0:T(8,128)S(1)}, u32[]{:S(2)}, u32[]{:S(2)}) collective-permute-start(f32[3,3,25,1]{3,2,1,0:T(8,128)S(1)} %slice.1034), channel_id=1, source_target_pairs={{1,0},{2,1},{3,2},{4,3},{5,4},{6,5},{7,6},{8,7},{9,8},{10,9},{11,1... | collective-permute-start | bytes 2708 | tf_op jit(solution)/shard_map/ppermute | solution.py:29
  (11 other events, 12.6 us)
where the time goes:
time: 320 us; the launch traced here: 318 us
  blocking collectives  102 us (32%)
  waiting for transfers between devices  70.8 us (22%)
  starting transfers between devices  67.4 us (21%)
  local copies, waits for them, and re-layouts  55.3 us (17%)
  between operations  9.13 us (3%)
  other arithmetic  7.66 us (2%)
  matrix products  5.81 us (2%)
    psum x8, blocking collectives, over_axes(): return functools.reduce(lax.psum, axes, shard)  102 us
    ppermute x20, waiting for transfers between devices, from_behind(): return lax.ppermute(shard, axis, pairs)  70.8 us
    ppermute x20, starting transfers between devices, from_behind(): return lax.ppermute(shard, axis, pairs)  67.4 us
    slice x12, local copies, waits for them, and re-layouts, correlation_take(): edge_part = rotated[..., 3::3][..., None]  15.2 us
    transpose x6, local copies, waits for them, and re-layouts, to_elements(): pieces = pieces.transpose(2, 4, 6, 0, 1, 3, 5)  7.16 us
    slice x15, local copies, waits for them, and re-layouts, correlation_add(): pieces[..., :block_width].reshape(leading + (block_count * block_width,))  6.71 us
  transfers between devices with their start and end apart: 20, of which 20 were waited for; matrix products, arithmetic and copies ran while one was open for 1% of the time, Pallas kernels for 0%

commit v1 on v0

v1 whole, which is shorter than its diff:
```python
import functools
import math

import jax
import jax.numpy as jnp
import numpy as np
from jax import lax
from jax.experimental import pallas as pl
from jax.experimental.pallas import tpu as pltpu
from jax.sharding import PartitionSpec as P

EY = 8
EZ = 6
VISC = 0.3
MESH_STEP = 0.01
BF = jnp.bfloat16
F32 = jnp.float32
ROWS = 40
BELOW = 3
WINDOW = 13
LANE_OWN = 9 * BELOW


def node_row(a, b, c):
    if b == 0 and c > 0:
        return 2 * a + c - 1
    if b > 0 and c == 0:
        return 8 + 2 * a + b - 1
    if b > 0:
        return 16 + 4 * a + 2 * (b - 1) + c - 1
    return 32 + a


def local_row(a, b, c):
    if b < 3 and c < 3:
        return node_row(a, b, c)
    if b == 3 and c < 3:
        return 48 + a if c == 0 else 40 + node_row(a, 0, c)
    if b < 3:
        return 64 + a if b == 0 else 56 + node_row(a, b, 0) - 8
    return 72 + a


def outer_triple(first, second, third):
    product = (
        first[:, None, None, :, None, None]
        * second[None, :, None, None, :, None]
        * third[None, None, :, None, None, :]
    )
    return product.reshape(
        first.shape[0] * second.shape[0] * third.shape[0],
        first.shape[1] * second.shape[1] * third.shape[1],
    )


def basis_tables():
    root_term = math.sqrt(10.0 / 7.0)
    outer = math.sqrt(5.0 + 2.0 * root_term) / 3.0
    inner = math.sqrt(5.0 - 2.0 * root_term) / 3.0
    gauss_roots = np.array([-outer, -inner, 0.0, inner, outer])
    outer_weight = (322.0 - 13.0 * math.sqrt(70.0)) / 900.0
    middle_weight = (322.0 + 13.0 * math.sqrt(70.0)) / 900.0
    weights = (
        np.array([outer_weight, middle_weight, 128.0 / 225.0, middle_weight, outer_weight]) / 2.0
    )
    points = (1.0 + gauss_roots) / 2.0
    lobatto = [0.0, (1.0 - 1.0 / math.sqrt(5.0)) / 2.0, (1.0 + 1.0 / math.sqrt(5.0)) / 2.0, 1.0]
    values = np.ones((5, 4))
    slopes = np.zeros((5, 4))
    for node in range(4):
        for other in range(4):
            if other != node:
                values[:, node] *= (points - lobatto[other]) / (lobatto[node] - lobatto[other])
        for other in range(4):
            if other != node:
                term = np.ones(5) / (lobatto[node] - lobatto[other])
                for third in range(4):
                    if third != node and third != other:
                        term = term * (points - lobatto[third]) / (lobatto[node] - lobatto[third])
                slopes[:, node] += term
    bernstein = np.stack([(1.0 - points) ** 2, 2.0 * points * (1.0 - points), points**2], axis=1)
    quad_weight = (
        weights[:, None, None] * weights[None, :, None] * weights[None, None, :]
    ).reshape(125)
    return (
        outer_triple(values, values, values),
        [
            outer_triple(slopes, values, values),
            outer_triple(values, slopes, values),
            outer_triple(values, values, slopes),
        ],
        outer_triple(bernstein, bernstein, bernstein),
        quad_weight,
    )


def split_table(table):
    high = table.astype(np.float32).astype(jnp.bfloat16)
    low = (table - high.astype(np.float64)).astype(np.float32).astype(jnp.bfloat16)
    return high, low


@functools.cache
def constants():
    vel_basis, grads, energy_basis, quad_weight = basis_tables()
    order = np.zeros(64, np.int64)
    for a in range(4):
        for b in range(4):
            for c in range(4):
                order[16 * a + 4 * b + c] = local_row(a, b, c)

    def spread_columns(table):
        wide = np.zeros((128, 80))
        wide[:125, order] = table
        return wide

    out = {}
    grad = np.concatenate([spread_columns(g) for g in grads], axis=0)
    high, low = split_table(grad)
    out["grad"] = np.concatenate([high, high, low], axis=1)
    high, low = split_table(grad.T)
    out["grad_t"] = np.concatenate([high, low], axis=0)
    phi = spread_columns(vel_basis)
    high, low = split_table(phi)
    out["phi"] = np.concatenate([high, high, low], axis=1)
    high, low = split_table(phi.T)
    out["phi_t"] = np.concatenate([high, low], axis=0)
    psi = np.zeros((128, 32))
    psi[:125, :27] = energy_basis
    high, low = split_table(psi)
    out["psi"] = np.concatenate([high, high, low], axis=1)
    high, low = split_table(psi.T)
    out["psi_t"] = np.concatenate([high, low], axis=0)
    weight = np.zeros((128, 128), np.float32)
    weight[:125] = quad_weight[:, None]
    out["weight"] = weight

    flat = np.arange(1350)
    px, py, pz = flat // 450, (flat // 18) % 25, flat % 18
    lane = 9 * ((pz + 1) // 3) + py // 3
    mask = np.zeros((ROWS, 1350), np.float32)
    mask0 = np.zeros((ROWS, 450), np.float32)
    own = np.zeros((ROWS, 128), np.float32)
    for k in range(1350):
        row = node_row(px[k] + 1, py[k] % 3, (pz[k] + 1) % 3)
        mask[row, k] = 1.0
        own[row, lane[k] + LANE_OWN] = 1.0
    for k in range(450):
        mask0[node_row(0, py[k] % 3, (pz[k] + 1) % 3), k] = 1.0
    out["mask"] = mask
    out["mask0"] = mask0
    out["own"] = own
    pick = np.zeros((1350, 128), np.float32)
    pick[flat, lane] = 1.0
    pick_high = np.zeros((1350, 128), np.float32)
    pick_high[flat, lane + 64] = 1.0
    out["pick"] = pick.astype(jnp.bfloat16)
    out["pick_high"] = pick_high.astype(jnp.bfloat16)
    back = np.zeros((128, 1350), np.float32)
    back[lane + LANE_OWN, flat] = 1.0
    out["back"] = back.astype(jnp.bfloat16)
    element = np.arange(EY * EZ)
    elane = 9 * (element % EZ) + element // EZ
    place = np.zeros((48, 128), np.float32)
    place[element, elane] = 1.0
    place_high = np.zeros((48, 128), np.float32)
    place_high[element, elane + 64] = 1.0
    out["place"] = place.astype(jnp.bfloat16)
    out["place_high"] = place_high.astype(jnp.bfloat16)
    take = np.zeros((128, 48), np.float32)
    take[elane + LANE_OWN, element] = 1.0
    out["take"] = take.astype(jnp.bfloat16)
    own_element = np.zeros((8, 128), np.float32)
    own_element[:, elane + LANE_OWN] = 1.0
    out["own_element"] = own_element
    return out


def dot(left, right):
    return jnp.dot(left, right, preferred_element_type=F32)


def split2(value):
    high = value.astype(BF)
    return high, (value - high.astype(F32)).astype(BF)


def split3(value):
    high = value.astype(BF)
    rest = value - high.astype(F32)
    middle = rest.astype(BF)
    return high, middle, (rest - middle.astype(F32)).astype(BF)


def exact_dot(value, selection):
    high, middle, low = split3(value)
    return dot(high, selection) + (dot(middle, selection) + dot(low, selection))


def stacked(value):
    high, low = split2(value)
    return jnp.concatenate([high, low, high], axis=0)


def rolled(value, by):
    return pltpu.roll(value, by % 128, 1)


def to_local(nodes):
    columns = []
    for comp in range(3):
        block = nodes[ROWS * comp : ROWS * comp + ROWS]
        corner = block[32:40]
        columns.append(
            jnp.concatenate(
                [
                    block,
                    rolled(block[0:8], -1),
                    rolled(corner, -1),
                    rolled(block[8:16], -9),
                    rolled(corner, -9),
                    rolled(corner, -10),
                ],
                axis=0,
            )
        )
    return jnp.concatenate(columns, axis=1)


def from_local(local):
    blocks = []
    for comp in range(3):
        part = local[:, 128 * comp : 128 * comp + 128]
        blocks += [
            part[0:8] + rolled(part[40:48], 1),
            part[8:16] + rolled(part[56:64], 9),
            part[16:32],
            part[32:40]
            + (rolled(part[48:56], 1) + rolled(part[64:72], 9) + rolled(part[72:80], 10)),
        ]
    return jnp.concatenate(blocks, axis=0)


def transposed_dot(table, value):
    high, low = split2(value)
    half = table.shape[0] // 2
    both = dot(table, high)
    return both[:half] + (both[half:] + dot(table[:half], low))


def add_planes(nodes, below, above):
    row = lax.broadcasted_iota(jnp.int32, (8, 128), 0)
    blocks = []
    for comp in range(3):
        at = ROWS * comp
        for group in (0, 8):
            low = pltpu.roll(below[at + group : at + group + 8], 2, 0)
            high = pltpu.roll(above[at + group : at + group + 8], 6, 0)
            blocks.append(
                nodes[at + group : at + group + 8]
                + jnp.where(row < 2, low, jnp.where(row >= 6, high, 0.0))
            )
        low = pltpu.roll(below[at + 24 : at + 32], 4, 0)
        high = pltpu.roll(above[at + 16 : at + 24], 4, 0)
        blocks.append(nodes[at + 16 : at + 24] + jnp.where(row < 4, low, 0.0))
        blocks.append(nodes[at + 24 : at + 32] + jnp.where(row >= 4, high, 0.0))
        low = pltpu.roll(below[at + 32 : at + 40], 5, 0)
        high = pltpu.roll(above[at + 32 : at + 40], 3, 0)
        blocks.append(
            nodes[at + 32 : at + 40] + jnp.where(row == 0, low, jnp.where(row == 3, high, 0.0))
        )
    return jnp.concatenate(blocks, axis=0)


def shared_sum(nodes, even_ref, first_ref, second_ref, wall_ref):
    even = jnp.concatenate([even_ref[...]] * 15, axis=0) > 0.5
    first, second = first_ref[...], second_ref[...]
    total = add_planes(nodes, jnp.where(even, second, first), jnp.where(even, first, second))
    wall = wall_ref[...]
    return total * jnp.concatenate([wall, wall, wall], axis=0)


def cofactors(j):
    return [
        [
            j[(r + 1) % 3][(c + 1) % 3] * j[(r + 2) % 3][(c + 2) % 3]
            - j[(r + 1) % 3][(c + 2) % 3] * j[(r + 2) % 3][(c + 1) % 3]
            for c in range(3)
        ]
        for r in range(3)
    ]


def gradients(ref, chunk, base=0):
    return [
        [
            ref[128 * m + 8 * chunk : 128 * m + 8 * chunk + 8, base + 128 * c : base + 128 * c + 128]
            for m in range(3)
        ]
        for c in range(3)
    ]


def plus_identity(g):
    return [[g[c][m] + 1.0 if c == m else g[c][m] for m in range(3)] for c in range(3)]


def pack_kernel(disp_ref, vel_ref, dens_ref, energy_ref, live_ref, mask_ref, pick_ref, pick_high_ref,
                place_ref, place_high_ref, out_ref):
    mask = mask_ref[...]
    for comp in range(3):
        low = mask * disp_ref[comp : comp + 1, :]
        high = mask * vel_ref[comp : comp + 1, :]
        out_ref[ROWS * comp : ROWS * comp + ROWS, :] = exact_dot(low, pick_ref[...]) + exact_dot(
            high, pick_high_ref[...]
        )
    density = jnp.concatenate([dens_ref[0:120], jnp.pad(dens_ref[120:125], ((0, 3), (0, 0)))], axis=0)
    row = lax.broadcasted_iota(jnp.int32, (8, 48), 0)
    tail = jnp.pad(energy_ref[24:27], ((0, 5), (0, 0)))
    tail = jnp.where(row == 3, live_ref[...].astype(F32), tail)
    energy = jnp.concatenate([energy_ref[0:24], tail], axis=0)
    place, place_high = place_ref[...], place_high_ref[...]
    out_ref[120:184, :] = exact_dot(density[0:64], place) + exact_dot(density[64:128], place_high)
    out_ref[184:200, :] = exact_dot(energy[0:16], place) + exact_dot(energy[16:32], place_high)


def halo_kernel(packed_ref, halo_ref, mask0_ref, pick_ref, pick_high_ref, out_ref):
    mask0 = mask0_ref[...]
    pick, pick_high = pick_ref[0:450, :], pick_high_ref[0:450, :]
    out_ref[120:200, :] = packed_ref[120:200, :]
    for comp in range(3):
        low = mask0 * halo_ref[comp : comp + 1, :]
        high = mask0 * halo_ref[comp + 3 : comp + 4, :]
        at = slice(ROWS * comp, ROWS * comp + ROWS)
        out_ref[at, :] = packed_ref[at, :] + (exact_dot(low, pick) + exact_dot(high, pick_high))


def unpack(own, below, above):
    lane = lax.broadcasted_iota(jnp.int32, own.shape, 1)
    is_own = (lane >= 27) & (lane < 90)
    is_below = lane < 36
    is_above = lane >= 81

    def window(by):
        return (
            jnp.where(is_own, rolled(own, 27 - by), 0.0)
            + jnp.where(is_below, rolled(below, -27 - by), 0.0)
            + jnp.where(is_above, rolled(above, 81 - by), 0.0)
        )

    return window(0), window(64)


def force_kernel(own_ref, below_ref, above_ref, grad_ref, grad_t_ref, psi_ref, weight_ref,
                 force_ref, disp_ref, vel_ref, mass_ref, live_ref, power_ref, wdens_ref,
                 g_ref, flux_ref, point_ref):
    disp, vel = unpack(own_ref[0:120], below_ref[0:120], above_ref[0:120])
    disp_ref[...] = disp
    vel_ref[...] = vel
    dens_low, dens_high = unpack(own_ref[120:184], below_ref[120:184], above_ref[120:184])
    energy_low, energy_high = unpack(own_ref[184:200], below_ref[184:200], above_ref[184:200])
    energy = jnp.concatenate([energy_low, energy_high], axis=0)
    lane = lax.broadcasted_iota(jnp.int32, (1, 128), 1)
    live = jnp.where(lane < 9 * WINDOW, energy[27:28], 0.0)
    live_ref[...] = jnp.broadcast_to(live, (8, 128))
    table = grad_ref[...]
    g_ref[:, 0:384] = dot(table, stacked(to_local(disp)))
    g_ref[:, 384:768] = dot(table, stacked(to_local(vel)))
    point_ref[...] = dot(psi_ref[...], stacked(energy))
    alive = jnp.broadcast_to(live, (8, 128))
    for chunk in range(16):
        at = slice(8 * chunk, 8 * chunk + 8)
        j = plus_identity(gradients(g_ref, chunk))
        g = gradients(g_ref, chunk, 384)
        cof = cofactors(j)
        volume = j[0][0] * cof[0][0] + j[0][1] * cof[0][1] + j[0][2] * cof[0][2]
        volume = jnp.where(alive > 0.5, volume, 1.0)
        inverse = 1.0 / volume
        source = dens_low if chunk < 8 else dens_high
        mass_density = source[8 * (chunk % 8) : 8 * (chunk % 8) + 8]
        density = mass_density * inverse
        pressure = (5.0 / 3.0 - 1.0) * density * point_ref[at, :]
        spatial = [
            [
                (g[c][0] * cof[m][0] + g[c][1] * cof[m][1] + g[c][2] * cof[m][2]) * inverse
                for m in range(3)
            ]
            for c in range(3)
        ]
        drag = VISC * density
        stress = [[None] * 3 for _ in range(3)]
        for c in range(3):
            for m in range(c, 3):
                value = drag * (spatial[c][m] + spatial[m][c])
                stress[c][m] = stress[m][c] = value - pressure if c == m else value
        weight = weight_ref[at, :]
        live_weight = weight * alive
        for c in range(3):
            for m in range(3):
                flux_ref[128 * m + 8 * chunk : 128 * m + 8 * chunk + 8, 128 * c : 128 * c + 128] = (
                    -live_weight
                ) * (stress[c][0] * cof[0][m] + stress[c][1] * cof[1][m] + stress[c][2] * cof[2][m])
        power = stress[0][0] * spatial[0][0]
        for c in range(3):
            for m in range(3):
                if c + m > 0:
                    power = power + stress[c][m] * spatial[c][m]
        power_ref[at, :] = live_weight * volume * power
        wdens = weight * mass_density
        wdens_ref[at, :] = wdens
        mass_ref[at, :] = wdens * alive
    force_ref[...] = from_local(transposed_dot(grad_t_ref[...], flux_ref[...]))


def energy_kernel(power_ref, wdens_ref, psi_t_ref, take_ref, out_ref):
    table = psi_t_ref[...]
    lumped = transposed_dot(table, wdens_ref[...])
    lumped = jnp.where(lumped > 0.0, lumped, 1.0)
    rate = transposed_dot(table, power_ref[...]) / lumped
    out_ref[...] = exact_dot(rate, take_ref[...])[0:27]


def total_of(value):
    return jnp.sum(jnp.sum(value, axis=0, keepdims=True), axis=1, keepdims=True)


def mass_points(nodes, phi_ref, mass_ref):
    return dot(phi_ref[...], stacked(to_local(nodes)))


def point_energy(points, mass, own_element):
    square = (
        points[:, 0:128] * points[:, 0:128]
        + points[:, 128:256] * points[:, 128:256]
        + points[:, 256:384] * points[:, 256:384]
    )
    return total_of(jnp.sum(square * mass, axis=0, keepdims=True) * own_element)


def norm_of(nodes, own):
    return total_of(nodes * nodes * jnp.concatenate([own, own, own], axis=0))


def mass_kernel(part_ref, first_ref, second_ref, even_ref, wall_ref, mass_ref, phi_ref, phi_t_ref,
                own_ref, own_element_ref, resid_ref, image_ref, sums_ref):
    resid = shared_sum(part_ref[...], even_ref, first_ref, second_ref, wall_ref)
    resid_ref[...] = resid
    points = mass_points(resid, phi_ref, mass_ref)
    mass = mass_ref[...]
    image_ref[...] = from_local(
        transposed_dot(phi_t_ref[...], points * jnp.concatenate([mass, mass, mass], axis=1))
    )
    norm = norm_of(resid, own_ref[...])
    energy = point_energy(points, mass, own_element_ref[0:1])
    lane = lax.broadcasted_iota(jnp.int32, (8, 128), 1)
    sums_ref[...] = jnp.where(lane == 0, norm, jnp.where(lane == 1, energy, 0.0))


def moment_kernel(part_ref, first_ref, second_ref, even_ref, wall_ref, mass_ref, phi_ref, own_ref,
                  own_element_ref, sums_ref, image_ref, out_ref):
    image = shared_sum(part_ref[...], even_ref, first_ref, second_ref, wall_ref)
    image_ref[...] = image
    points = mass_points(image, phi_ref, mass_ref)
    norm = norm_of(image, own_ref[...])
    energy = point_energy(points, mass_ref[...], own_element_ref[0:1])
    lane = lax.broadcasted_iota(jnp.int32, (1, 128), 1)
    row = sums_ref[0:1] + jnp.where(lane == 2, norm, jnp.where(lane == 3, energy, 0.0))
    out_ref[...] = jnp.broadcast_to(row, out_ref.shape)


def shape_forces(u, live, grad_ref, grad_t_ref, weight_ref, g_ref, flux_ref):
    g_ref[...] = dot(grad_ref[...], stacked(to_local(u)))
    for chunk in range(16):
        at = slice(8 * chunk, 8 * chunk + 8)
        j = plus_identity(gradients(g_ref, chunk))
        cof = cofactors(j)
        volume = j[0][0] * cof[0][0] + j[0][1] * cof[0][1] + j[0][2] * cof[0][2]
        volume = jnp.where(live > 0.5, volume, 1.0)
        norm = j[0][0] * j[0][0]
        for c in range(3):
            for m in range(3):
                if c + m > 0:
                    norm = norm + j[c][m] * j[c][m]
        weight = weight_ref[at, :] * live * jnp.exp(jnp.log(volume) * (-2.0 / 3.0))
        first = weight * (2.0 / 3.0)
        second = weight * (-2.0 / 9.0) * (norm / volume)
        for c in range(3):
            for m in range(3):
                flux_ref[128 * m + 8 * chunk : 128 * m + 8 * chunk + 8, 128 * c : 128 * c + 128] = (
                    first * j[c][m] + second * cof[c][m]
                )
    return from_local(transposed_dot(grad_t_ref[...], flux_ref[...]))


def first_shape_kernel(moments_ref, disp_ref, vel_ref, resid_ref, image_ref, live_ref, step_ref,
                       grad_ref, grad_t_ref, weight_ref, newvel_ref, moved_ref, part_ref,
                       g_ref, flux_ref):
    moments = jnp.sum(moments_ref[...], axis=0, keepdims=True)
    mu0, mu1, mu2, mu3 = (moments[:, i : i + 1] for i in range(4))
    alpha = mu0 / mu1
    rest = alpha * alpha * mu2 - mu0
    beta = rest / mu0
    gain = 1.0 + beta
    second = rest / (gain * gain * mu1 - 2.0 * gain * alpha * mu2 + alpha * alpha * mu3)
    step = step_ref[0:1, 0:1]
    newvel = vel_ref[...] + step * (
        (alpha + second * gain) * resid_ref[...] - (alpha * second) * image_ref[...]
    )
    newvel_ref[...] = newvel
    moved = disp_ref[...] + step * newvel
    moved_ref[...] = moved
    part_ref[...] = shape_forces(
        moved, live_ref[...], grad_ref, grad_t_ref, weight_ref, g_ref, flux_ref
    )


def second_shape_kernel(part_ref, first_ref, second_ref, even_ref, wall_ref, newvel_ref, moved_ref,
                        live_ref, step_ref, grad_ref, grad_t_ref, weight_ref, base_ref, next_ref,
                        g_ref, flux_ref):
    gradient = shared_sum(part_ref[...], even_ref, first_ref, second_ref, wall_ref)
    u = moved_ref[...] - MESH_STEP * gradient
    part = shape_forces(u, live_ref[...], grad_ref, grad_t_ref, weight_ref, g_ref, flux_ref)
    next_ref[...] = part
    base_ref[...] = newvel_ref[...] - (MESH_STEP / step_ref[0:1, 0:1]) * (gradient + part)


def write_nodes(nodes, mask_ref, back_ref, out_ref):
    mask = mask_ref[...]
    back = back_ref[...]
    for comp in range(3):
        wide = exact_dot(nodes[ROWS * comp : ROWS * comp + ROWS], back)
        out_ref[comp : comp + 1, :] = jnp.sum(wide * mask, axis=0, keepdims=True)


def velocity_kernel(nodes_ref, mask_ref, back_ref, out_ref):
    write_nodes(nodes_ref[...], mask_ref, back_ref, out_ref)


def mesh_kernel(base_ref, above_ref, step_ref, mask_ref, back_ref, out_ref):
    zero = jnp.zeros((120, 128), F32)
    extra = add_planes(zero, zero, above_ref[...])
    nodes = base_ref[...] - (MESH_STEP / step_ref[0:1, 0:1]) * extra
    write_nodes(nodes, mask_ref, back_ref, out_ref)


def call(kernel, name, outs, scratch=(), flops=1_000_000):
    spec = pl.BlockSpec(memory_space=pltpu.VMEM)

    def run(*args):
        return pl.pallas_call(
            kernel,
            out_shape=[jax.ShapeDtypeStruct(shape, F32) for shape in outs],
            in_specs=[spec] * len(args),
            out_specs=[spec] * len(outs),
            scratch_shapes=[pltpu.VMEM(shape, F32) for shape in scratch],
            name=name,
            cost_estimate=pl.CostEstimate(flops=flops, bytes_accessed=400_000, transcendentals=0),
        )(*args)

    return run


NODES = (120, 128)
POINTS = (128, 128)


def body(displacement, velocity, energy, mass_density, live_mask, time_step):
    table = {name: jnp.asarray(value) for name, value in constants().items()}
    n_dom, n_sub = lax.axis_size("dom"), lax.axis_size("sub")
    dom, sub = lax.axis_index("dom"), lax.axis_index("sub")
    up = [(i, i + 1) for i in range(n_dom - 1)]
    down = [(i + 1, i) for i in range(n_dom - 1)]
    pairs_first = [p for i in range(0, n_dom - 1, 2) for p in ((i, i + 1), (i + 1, i))]
    pairs_second = [p for i in range(1, n_dom - 1, 2) for p in ((i, i + 1), (i + 1, i))]
    z_up = [(i, i + 1) for i in range(n_sub - 1)]
    z_down = [(i + 1, i) for i in range(n_sub - 1)]

    step = jnp.broadcast_to(time_step.reshape(1, 1), (8, 128))
    even = jnp.broadcast_to((1 - dom % 2).astype(F32).reshape(1, 1), (8, 128))
    rows = np.arange(ROWS)
    row_a = np.select([rows < 8, rows < 16, rows < 32, rows < 36],
                      [rows // 2, (rows - 8) // 2, (rows - 16) // 4, rows - 32], 9)
    row_c = np.select([rows < 8, rows < 16, rows < 32], [rows % 2 + 1, 0 * rows, rows % 2 + 1], 0)
    node_z = 3 * (np.arange(128) // 9 - BELOW)[None, :] + row_c[:, None]
    on_x = jnp.asarray(np.broadcast_to((row_a == 0)[:, None], (ROWS, 128)))
    on_z = jnp.asarray(node_z <= 0)
    wall = jnp.where((on_x & (dom == 0)) | (on_z & (sub == 0)), 0.0, 1.0).astype(F32)

    last = jnp.concatenate([displacement[:, 900:], velocity[:, 900:]], axis=0)
    halo = lax.ppermute(last, "dom", up)
    (packed,) = call(pack_kernel, "pack", [(200, 128)])(
        displacement, velocity, mass_density, energy, live_mask.reshape(1, 48), table["mask"],
        table["pick"], table["pick_high"], table["place"], table["place_high"],
    )
    (own,) = call(halo_kernel, "halo", [(200, 128)])(
        packed, halo, table["mask0"], table["pick"], table["pick_high"]
    )
    below = lax.ppermute(own, "sub", z_up)
    above = lax.ppermute(own, "sub", z_down)
    force, disp, vel, mass, live, power, wdens = call(
        force_kernel, "force",
        [NODES, NODES, NODES, POINTS, (8, 128), POINTS, POINTS],
        [(384, 768), (384, 384), POINTS],
    )(own, below, above, table["grad"], table["grad_t"], table["psi"], table["weight"])

    def swap(part):
        return lax.ppermute(part, "dom", pairs_first), lax.ppermute(part, "dom", pairs_second)

    first, second = swap(force)
    (energy_rate,) = call(energy_kernel, "energy", [(27, 48)])(
        power, wdens, table["psi_t"], table["take"]
    )
    resid, image_part, sums = call(mass_kernel, "mass", [NODES, NODES, (8, 128)])(
        force, first, second, even, wall, mass, table["phi"], table["phi_t"], table["own"],
        table["own_element"],
    )
    first, second = swap(image_part)
    image, local = call(moment_kernel, "moment", [NODES, (n_dom, 128)])(
        image_part, first, second, even, wall, mass, table["phi"], table["own"],
        table["own_element"], sums,
    )
    slab = jnp.sum(lax.all_to_all(local, "dom", 0, 0, tiled=True), axis=0, keepdims=True)
    moments = lax.all_to_all(jnp.broadcast_to(slab, (n_sub, 128)), "sub", 0, 0, tiled=True)
    newvel, moved, part = call(
        first_shape_kernel, "shape1", [NODES, NODES, NODES], [(384, 384), (384, 384)]
    )(moments, disp, vel, resid, image, live, step, table["grad"], table["grad_t"], table["weight"])
    first, second = swap(part)
    (new_velocity,) = call(velocity_kernel, "newvel", [(3, 1350)])(
        newvel, table["mask"], table["back"]
    )
    base, part = call(
        second_shape_kernel, "shape2", [NODES, NODES], [(384, 384), (384, 384)]
    )(part, first, second, even, wall, newvel, moved, live, step, table["grad"], table["grad_t"],
      table["weight"])
    from_above = lax.ppermute(part, "dom", down)
    (mesh_velocity,) = call(mesh_kernel, "mesh", [(3, 1350)])(
        base, from_above, step, table["mask"], table["back"]
    )
    return new_velocity, energy_rate, mesh_velocity


def solution(mesh):
    both = ("dom", "sub")
    return jax.shard_map(
        body,
        mesh=mesh,
        in_specs=(P(None, both), P(None, both), P(None, both), P(None, both), P(both), P()),
        out_specs=(P(None, both), P(None, both), P(None, both)),
        check_vma=False,
    )
```

time: 320 us -> 123 us (0.38)
  blocking collectives: 102 us -> 14.8 us
  local copies, waits for them, and re-layouts: 55.3 us -> 7.8 us
  waiting for transfers between devices: 70.8 us -> 28.5 us
  Pallas kernels: 0 us -> 24.5 us
  starting transfers between devices: 67.4 us -> 43.4 us
  between operations: 9.13 us -> 1.48 us
  other arithmetic: 7.66 us -> 0.79 us
  matrix products: 5.81 us -> 0 us
    psum x8 -> x0, blocking collectives: 102 us -> none  [over_axes(): return functools.reduce(lax.psum, axes, shard)]
    ppermute x20 -> x10, waiting for transfers between devices: 70.8 us -> 20.3 us  [the longest x3 12.4 us: swap(): lax.ppermute(part, 'dom', pairs_second)]
    ppermute x20 -> x10, starting transfers between devices: 67.4 us -> 28.9 us  [the longest x3 10.4 us: swap(): lax.ppermute(part, 'dom', pairs_second)]
    slice x85 -> x2, local copies, waits for them, and re-layouts: 27.5 us -> 1.55 us  [body(): last = jnp.concatenate([displacement[:, 900:], velocity[:, 900:]], axis=0)]
    pallas_call x0 -> x10, Pallas kernels: none -> 24.5 us  [run(): pl.pallas_call(kernel, out_shape=[jax.ShapeDtypeStruct(shape, F32) for sh...]
    all_to_all x0 -> x1, blocking collectives: none -> 14.8 us  [body(): lax.all_to_all(local, 'dom', 0, 0, tiled=True)]
    all_to_all x0 -> x1, starting transfers between devices: none -> 14.5 us  [body(): lax.all_to_all(jnp.broadcast_to(slab, (n_sub, 128)), 'sub', 0, 0, tiled=T...]
    all_to_all x0 -> x1, waiting for transfers between devices: none -> 8.22 us  [body(): lax.all_to_all(jnp.broadcast_to(slab, (n_sub, 128)), 'sub', 0, 0, tiled=T...]
  transfers between devices with their start and end apart: 20 -> 11, of which waited for: 20 -> 7; matrix products, arithmetic and copies ran while one was open for 1% -> 1% of each run, Pallas kernels for 0% -> 6%
where the time goes in v1:
time: 123 us; the launch traced here: 121 us
  starting transfers between devices  43.4 us (35%)
  waiting for transfers between devices  28.5 us (23%)
  Pallas kernels  24.5 us (20%)
  blocking collectives  14.8 us (12%)
  local copies, waits for them, and re-layouts  7.8 us (6%)
  between operations  1.48 us (1%)
    pallas_call x10, Pallas kernels, run(): pl.pallas_call(kernel, out_shape=[jax.ShapeDtypeStruct(shape, F32) for sh...  24.5 us
    all_to_all x1, blocking collectives, body(): lax.all_to_all(local, 'dom', 0, 0, tiled=True)  14.8 us
    all_to_all x1, starting transfers between devices, body(): lax.all_to_all(jnp.broadcast_to(slab, (n_sub, 128)), 'sub', 0, 0, tiled=T...  14.5 us
    ppermute x3, waiting for transfers between devices, swap(): lax.ppermute(part, 'dom', pairs_second)  12.4 us
    ppermute x3, starting transfers between devices, swap(): lax.ppermute(part, 'dom', pairs_second)  10.4 us
    ppermute x3, starting transfers between devices, swap(): lax.ppermute(part, 'dom', pairs_first)  8.36 us
    all_to_all x1, waiting for transfers between devices, body(): lax.all_to_all(jnp.broadcast_to(slab, (n_sub, 128)), 'sub', 0, 0, tiled=T...  8.22 us
    ppermute x1, waiting for transfers between devices, body(): above = lax.ppermute(own, 'sub', z_down)  4.65 us
  transfers between devices with their start and end apart: 11, of which 7 were waited for; matrix products, arithmetic and copies ran while one was open for 1% of the time, Pallas kernels for 6%

profile of v1, /device:TPU:57, one launch (start us, length us, event | category | flops | bytes accessed | tf_op | source)
XLA Modules:
  0.0 121.3 jit_solution(8817253253425100455)
XLA Ops:
  2.2 2.9 %collective-permute-start = (f32[6,450]{1,0:T(8,128)S(1)}, f32[6,450]{1,0:T(8,128)S(1)}, u32[]{:S(2)}, u32[]{:S(2)}) collective-permute-start(f32[6,450]{1,0:T(8,128)S(1)} %pad_maximum_fusion), channel_id=1, source_target_pairs={{0,12},{12,24},{24,36},{36,48},{48,60},{60,72},{72,84},{84,96},{96... | collective-permute-start | bytes 32408 | tf_op jit(solution)/shard_map/ppermute | solution.py:590
  5.8 3.0 %pack.1.packed_ref = f32[200,128]{1,0:T(8,128)} custom-call(f32[3,1350]{1,0:T(4,128)} %disp_ref.1, f32[3,1350]{1,0:T(4,128)} %vel_ref.1, f32[125,48]{1,0:T(8,128)} %copy.29.dens_ref, f32[27,48]{1,0:T(8,128)} %energy_ref.1, s32[1,48]{1,0:T(1,128)} %bitcast.9, f32[40,1350]{1,0:T(8,128)} %constant.70.clone.mask_ref, bf16[1350,128]{1,0:T(8,128)(2,1)} %constant.73.clone.pick_ref, ...), custom_call_target="tpu_custom_call" | custom-call | flops 1000000 | bytes 400000 | tf_op jit(solution)/shard_map/pack/pallas_call | solution.py:550
  9.5 2.4 %halo.1.own_ref = f32[200,128]{1,0:T(8,128)} custom-call(f32[200,128]{1,0:T(8,128)} %pack.1.packed_ref, f32[6,450]{1,0:T(8,128)} %copy-done.10, f32[40,450]{1,0:T(8,128)} %constant.71.clone.mask0_ref, bf16[1350,128]{1,0:T(8,128)(2,1)} %constant.73.clone.pick_ref, bf16[1350,128]{1,0:T(8,128)(2,1)} %constant.74.clone.pick_high_ref), custom_call_target="tpu_custom_call" | custom-call | flops 1000000 | bytes 400000 | tf_op jit(solution)/shard_map/halo/pallas_call | solution.py:550
  11.8 4.0 %collective-permute-start.1 = (f32[200,128]{1,0:T(8,128)}, f32[200,128]{1,0:T(8,128)S(1)}, u32[]{:S(2)}, u32[]{:S(2)}) collective-permute-start(f32[200,128]{1,0:T(8,128)} %halo.1.own_ref), channel_id=1, source_target_pairs={{0,1},{1,2},{2,3},{3,4},{4,5},{5,6},{6,7},{7,8},{8,9},{9,10},{10,1... | collective-permute-start | bytes 307208 | tf_op jit(solution)/shard_map/ppermute | solution.py:598
  18.7 4.6 %collective-permute-done.2.above_ref = f32[200,128]{1,0:T(8,128)S(1)} collective-permute-done((f32[200,128]{1,0:T(8,128)}, f32[200,128]{1,0:T(8,128)S(1)}, u32[]{:S(2)}, u32[]{:S(2)}) %collective-permute-start.2) | collective-permute-done | bytes 102432 | tf_op jit(solution)/shard_map/ppermute | solution.py:599
  23.9 2.9 %force.1 = (f32[120,128]{1,0:T(8,128)}, f32[120,128]{1,0:T(8,128)}, f32[120,128]{1,0:T(8,128)}, f32[128,128]{1,0:T(8,128)}, f32[8,128]{1,0:T(8,128)}, /*index=5*/f32[128,128]{1,0:T(8,128)}, f32[128,128]{1,0:T(8,128)}) custom-call(f32[200,128]{1,0:T(8,128)} %halo.1.own_ref, f32[200,128]{1,0:T(8,128)} %copy-done, f32[200,128]{1,0:T(8,128)} %copy-done.1, ...), custom_call_target="tpu_custom_call" | custom-call | flops 1000000 | bytes 400000 | tf_op jit(solution)/shard_map/force/pallas_call | solution.py:550
  26.9 2.5 %collective-permute-start.3 = (f32[120,128]{1,0:T(8,128)}, f32[120,128]{1,0:T(8,128)S(1)}, u32[]{:S(2)}, u32[]{:S(2)}) collective-permute-start(f32[120,128]{1,0:T(8,128)} %get-tuple-element.20.part_ref), channel_id=1, source_target_pairs={{0,12},{12,0},{24,36},{36,24},{48,60},{60,48},{72,84},{84,72},{96,... | collective-permute-start | bytes 184328 | tf_op jit(solution)/shard_map/ppermute | solution.py:607
  29.3 3.1 %collective-permute-start.4 = (f32[120,128]{1,0:T(8,128)}, f32[120,128]{1,0:T(8,128)S(1)}, u32[]{:S(2)}, u32[]{:S(2)}) collective-permute-start(f32[120,128]{1,0:T(8,128)} %get-tuple-element.20.part_ref), channel_id=1, source_target_pairs={{12,24},{24,12},{36,48},{48,36},{60,72},{72,60},{84,96},{96,84},{1... | collective-permute-start | bytes 184328 | tf_op jit(solution)/shard_map/ppermute | solution.py:607
  33.2 4.1 %collective-permute-done.4.second_ref = f32[120,128]{1,0:T(8,128)S(1)} collective-permute-done((f32[120,128]{1,0:T(8,128)}, f32[120,128]{1,0:T(8,128)S(1)}, u32[]{:S(2)}, u32[]{:S(2)}) %collective-permute-start.4) | collective-permute-done | bytes 61472 | tf_op jit(solution)/shard_map/ppermute | solution.py:607
  37.8 2.1 %mass.1 = (f32[120,128]{1,0:T(8,128)}, f32[120,128]{1,0:T(8,128)}, f32[8,128]{1,0:T(8,128)}) custom-call(f32[120,128]{1,0:T(8,128)} %get-tuple-element.20.part_ref, f32[120,128]{1,0:T(8,128)} %copy-done.2, f32[120,128]{1,0:T(8,128)} %copy-done.3, f32[8,128]{1,0:T(8,128)} %broadcast_in_dim.24.even_ref, f32[40,128]{1,0:T(8,128)} %or_select_fusion.wall_ref, ...), custom_call_target="tpu_custom_call" | custom-call | flops 1000000 | bytes 400000 | tf_op jit(solution)/shard_map/mass/pallas_call | solution.py:550
  41.9 3.1 %collective-permute-start.6 = (f32[120,128]{1,0:T(8,128)}, f32[120,128]{1,0:T(8,128)S(1)}, u32[]{:S(2)}, u32[]{:S(2)}) collective-permute-start(f32[120,128]{1,0:T(8,128)} %get-tuple-element.22.part_ref), channel_id=1, source_target_pairs={{12,24},{24,12},{36,48},{48,36},{60,72},{72,60},{84,96},{96,84},{1... | collective-permute-start | bytes 184328 | tf_op jit(solution)/shard_map/ppermute | solution.py:607
  45.0 4.7 %collective-permute-done.6.second_ref = f32[120,128]{1,0:T(8,128)S(1)} collective-permute-done((f32[120,128]{1,0:T(8,128)}, f32[120,128]{1,0:T(8,128)S(1)}, u32[]{:S(2)}, u32[]{:S(2)}) %collective-permute-start.6) | collective-permute-done | bytes 61472 | tf_op jit(solution)/shard_map/ppermute | solution.py:607
  50.4 2.0 %moment.1 = (f32[120,128]{1,0:T(8,128)}, f32[64,128]{1,0:T(8,128)}) custom-call(f32[120,128]{1,0:T(8,128)} %get-tuple-element.22.part_ref, f32[120,128]{1,0:T(8,128)} %copy-done.5, f32[120,128]{1,0:T(8,128)} %copy-done.8, f32[8,128]{1,0:T(8,128)} %broadcast_in_dim.24.even_ref, f32[40,128]{1,0:T(8,128)} %or_select_fusion.wall_ref, ...), custom_call_target="tpu_custom_call" | custom-call | flops 1000000 | bytes 400000 | tf_op jit(solution)/shard_map/moment/pallas_call | solution.py:550
  52.4 14.8 %all_to_all.17 = f32[64,1,128]{2,1,0:T(1,128)S(1)} all-to-all(f32[64,1,128]{2,1,0:T(1,128)} %bitcast.8), channel_id=1, replica_groups=mesh['dom'=64,'sub'=12] {'dom'}, dimensions={0} | all-to-all | bytes 65536 | tf_op jit(solution)/shard_map/all_to_all | solution.py:622
  67.8 14.5 %all-to-all-start.1 = ((f32[12,1,128]{2,1,0:T(1,128)}), f32[12,1,128]{2,1,0:T(1,128)S(1)}, u32[]{:S(2)}, u32[]{:S(2)}) async-start(f32[12,1,128]{2,1,0:T(1,128)} %broadcast_in_dim.27), calls=%async_computation.1 | async-start | bytes 12288 | tf_op jit(solution)/shard_map/all_to_all | solution.py:623
  83.0 8.2 %all-to-all-done.1 = f32[12,1,128]{2,1,0:T(1,128)S(1)} async-done(((f32[12,1,128]{2,1,0:T(1,128)}), f32[12,1,128]{2,1,0:T(1,128)S(1)}, u32[]{:S(2)}, u32[]{:S(2)}) %all-to-all-start.1) | async-done | bytes 6176 | tf_op jit(solution)/shard_map/all_to_all | solution.py:623
  92.4 2.8 %shape1.1 = (f32[120,128]{1,0:T(8,128)}, f32[120,128]{1,0:T(8,128)}, f32[120,128]{1,0:T(8,128)}) custom-call(f32[12,128]{1,0:T(8,128)} %bitcast.7, f32[120,128]{1,0:T(8,128)} %get-tuple-element.25.disp_ref, f32[120,128]{1,0:T(8,128)} %get-tuple-element.26.vel_ref, f32[120,128]{1,0:T(8,128)} %get-tuple-element.27.resid_ref, ...), custom_call_target="tpu_custom_call" | custom-call | flops 1000000 | bytes 400000 | tf_op jit(solution)/shard_map/shape1/pallas_call | solution.py:550
  95.2 4.0 %collective-permute-start.7 = (f32[120,128]{1,0:T(8,128)}, f32[120,128]{1,0:T(8,128)S(1)}, u32[]{:S(2)}, u32[]{:S(2)}) collective-permute-start(f32[120,128]{1,0:T(8,128)} %get-tuple-element.33.part_ref), channel_id=1, source_target_pairs={{0,12},{12,0},{24,36},{36,24},{48,60},{60,48},{72,84},{84,72},{96,... | collective-permute-start | bytes 184328 | tf_op jit(solution)/shard_map/ppermute | solution.py:607
  99.2 4.2 %collective-permute-start.8 = (f32[120,128]{1,0:T(8,128)}, f32[120,128]{1,0:T(8,128)S(1)}, u32[]{:S(2)}, u32[]{:S(2)}) collective-permute-start(f32[120,128]{1,0:T(8,128)} %get-tuple-element.33.part_ref), channel_id=1, source_target_pairs={{12,24},{24,12},{36,48},{48,36},{60,72},{72,60},{84,96},{96,84},{1... | collective-permute-start | bytes 184328 | tf_op jit(solution)/shard_map/ppermute | solution.py:607
  103.5 3.6 %collective-permute-done.8.second_ref = f32[120,128]{1,0:T(8,128)S(1)} collective-permute-done((f32[120,128]{1,0:T(8,128)}, f32[120,128]{1,0:T(8,128)S(1)}, u32[]{:S(2)}, u32[]{:S(2)}) %collective-permute-start.8) | collective-permute-done | bytes 61472 | tf_op jit(solution)/shard_map/ppermute | solution.py:607
  107.7 2.7 %shape2.1 = (f32[120,128]{1,0:T(8,128)}, f32[120,128]{1,0:T(8,128)}) custom-call(f32[120,128]{1,0:T(8,128)} %get-tuple-element.33.part_ref, f32[120,128]{1,0:T(8,128)} %copy-done.4, f32[120,128]{1,0:T(8,128)} %copy-done.6, f32[8,128]{1,0:T(8,128)} %broadcast_in_dim.24.even_ref, f32[40,128]{1,0:T(8,128)} %or_select_fusion.wall_ref, ...), custom_call_target="tpu_custom_call" | custom-call | flops 1000000 | bytes 400000 | tf_op jit(solution)/shard_map/shape2/pallas_call | solution.py:550
  110.4 1.9 %collective-permute-start.9 = (f32[120,128]{1,0:T(8,128)}, f32[120,128]{1,0:T(8,128)S(1)}, u32[]{:S(2)}, u32[]{:S(2)}) collective-permute-start(f32[120,128]{1,0:T(8,128)} %get-tuple-element.36), channel_id=1, source_target_pairs={{12,0},{24,12},{36,24},{48,36},{60,48},{72,60},{84,72},{96,84},{10... | collective-permute-start | bytes 184328 | tf_op jit(solution)/shard_map/ppermute | solution.py:635
  114.2 2.4 %newvel.1 = f32[3,1350]{1,0:T(4,128)} custom-call(f32[120,128]{1,0:T(8,128)} %get-tuple-element.30.nodes_ref.newvel_ref, f32[40,1350]{1,0:T(8,128)} %constant.70.clone.mask_ref, bf16[128,1350]{1,0:T(8,128)(2,1)} %constant.75.clone.back_ref), custom_call_target="tpu_custom_call" | custom-call | flops 1000000 | bytes 400000 | tf_op jit(solution)/shard_map/newvel/pallas_call | solution.py:550
  118.9 2.4 %mesh.1 = f32[3,1350]{1,0:T(4,128)} custom-call(f32[120,128]{1,0:T(8,128)} %get-tuple-element.35.base_ref, f32[120,128]{1,0:T(8,128)} %copy-done.7, f32[8,128]{1,0:T(8,128)} %broadcast_in_dim.28.step_ref, f32[40,1350]{1,0:T(8,128)} %constant.70.clone.mask_ref, bf16[128,1350]{1,0:T(8,128)(2,1)} %constant.75.clone.back_ref), custom_call_target="tpu_custom_call" | custom-call | flops 1000000 | bytes 400000 | tf_op jit(solution)/shard_map/mesh/pallas_call | solution.py:550
  (46 shorter events, 16.9 us)
Async XLA Ops:
  1.4 3.7 %copy-start.9 = (f32[125,48]{0,1:T(8,128)S(1)}, f32[125,48]{0,1:T(8,128)}, u32[]{:S(2)}) copy-start(f32[125,48]{0,1:T(8,128)} %param.28) | copy-start | bytes 72004
  2.2 6.7 %collective-permute-start = (f32[6,450]{1,0:T(8,128)S(1)}, f32[6,450]{1,0:T(8,128)S(1)}, u32[]{:S(2)}, u32[]{:S(2)}) collective-permute-start(f32[6,450]{1,0:T(8,128)S(1)} %pad_maximum_fusion), channel_id=1, source_target_pairs={{0,12},{12,24},{24,36},{36,48},{48,60},{60,72},{72,84},{84,96},{96... | collective-permute-start | bytes 32408 | tf_op jit(solution)/shard_map/ppermute | solution.py:590
  8.8 8.3 %copy-start.12 = (pred[40]{0:T(512)(128)(4,1)S(1)}, pred[40]{0:T(512)(128)(4,1)}, u32[]{:S(2)}) copy-start(pred[40]{0:T(512)(128)(4,1)} %constant.80.clone) | copy-start | bytes 124
  8.8 0.6 copy-start.10
  11.8 6.8 %collective-permute-start.1 = (f32[200,128]{1,0:T(8,128)}, f32[200,128]{1,0:T(8,128)S(1)}, u32[]{:S(2)}, u32[]{:S(2)}) collective-permute-start(f32[200,128]{1,0:T(8,128)} %halo.1.own_ref), channel_id=1, source_target_pairs={{0,1},{1,2},{2,3},{3,4},{4,5},{5,6},{6,7},{7,8},{8,9},{9,10},{10,1... | collective-permute-start | bytes 307208 | tf_op jit(solution)/shard_map/ppermute | solution.py:598
  15.8 7.5 %collective-permute-start.2 = (f32[200,128]{1,0:T(8,128)}, f32[200,128]{1,0:T(8,128)S(1)}, u32[]{:S(2)}, u32[]{:S(2)}) collective-permute-start(f32[200,128]{1,0:T(8,128)} %halo.1.own_ref), channel_id=1, source_target_pairs={{1,0},{2,1},{3,2},{4,3},{5,4},{6,5},{7,6},{8,7},{9,8},{10,9},{11,1... | collective-permute-start | bytes 307208 | tf_op jit(solution)/shard_map/ppermute | solution.py:599
  18.7 4.7 %copy-start = (f32[200,128]{1,0:T(8,128)}, f32[200,128]{1,0:T(8,128)S(1)}, u32[]{:S(2)}) copy-start(f32[200,128]{1,0:T(8,128)S(1)} %collective-permute-done.1.below_ref) | copy-start | bytes 307204
  23.3 0.6 copy-start.1
  23.9 8.5 %copy-start.11 = (pred[40,128]{1,0:T(8,128)(4,1)S(1)}, pred[40,128]{1,0:T(8,128)(4,1)}, u32[]{:S(2)}) copy-start(pred[40,128]{1,0:T(8,128)(4,1)} %constant.81.clone) | copy-start | bytes 15364
  26.9 6.3 %collective-permute-start.3 = (f32[120,128]{1,0:T(8,128)}, f32[120,128]{1,0:T(8,128)S(1)}, u32[]{:S(2)}, u32[]{:S(2)}) collective-permute-start(f32[120,128]{1,0:T(8,128)} %get-tuple-element.20.part_ref), channel_id=1, source_target_pairs={{0,12},{12,0},{24,36},{36,24},{48,60},{60,48},{72,84},{84,72},{96,... | collective-permute-start | bytes 184328 | tf_op jit(solution)/shard_map/ppermute | solution.py:607
  29.3 7.9 %collective-permute-start.4 = (f32[120,128]{1,0:T(8,128)}, f32[120,128]{1,0:T(8,128)S(1)}, u32[]{:S(2)}, u32[]{:S(2)}) collective-permute-start(f32[120,128]{1,0:T(8,128)} %get-tuple-element.20.part_ref), channel_id=1, source_target_pairs={{12,24},{24,12},{36,48},{48,36},{60,72},{72,60},{84,96},{96,84},{1... | collective-permute-start | bytes 184328 | tf_op jit(solution)/shard_map/ppermute | solution.py:607
  33.1 4.7 %copy-start.2 = (f32[120,128]{1,0:T(8,128)}, f32[120,128]{1,0:T(8,128)S(1)}, u32[]{:S(2)}) copy-start(f32[120,128]{1,0:T(8,128)S(1)} %collective-permute-done.3.first_ref) | copy-start | bytes 184324
  37.2 0.6 copy-start.3
  40.0 5.0 %collective-permute-start.5 = (f32[120,128]{1,0:T(8,128)}, f32[120,128]{1,0:T(8,128)S(1)}, u32[]{:S(2)}, u32[]{:S(2)}) collective-permute-start(f32[120,128]{1,0:T(8,128)} %get-tuple-element.22.part_ref), channel_id=1, source_target_pairs={{0,12},{12,0},{24,36},{36,24},{48,60},{60,48},{72,84},{84,72},{96,... | collective-permute-start | bytes 184328 | tf_op jit(solution)/shard_map/ppermute | solution.py:607
  41.9 7.9 %collective-permute-start.6 = (f32[120,128]{1,0:T(8,128)}, f32[120,128]{1,0:T(8,128)S(1)}, u32[]{:S(2)}, u32[]{:S(2)}) collective-permute-start(f32[120,128]{1,0:T(8,128)} %get-tuple-element.22.part_ref), channel_id=1, source_target_pairs={{12,24},{24,12},{36,48},{48,36},{60,72},{72,60},{84,96},{96,84},{1... | collective-permute-start | bytes 184328 | tf_op jit(solution)/shard_map/ppermute | solution.py:607
  45.0 4.7 %copy-start.5 = (f32[120,128]{1,0:T(8,128)}, f32[120,128]{1,0:T(8,128)S(1)}, u32[]{:S(2)}) copy-start(f32[120,128]{1,0:T(8,128)S(1)} %collective-permute-done.5.first_ref) | copy-start | bytes 184324
  49.8 0.6 copy-start.8
  67.8 23.4 %all-to-all-start.1 = ((f32[12,1,128]{2,1,0:T(1,128)}), f32[12,1,128]{2,1,0:T(1,128)S(1)}, u32[]{:S(2)}, u32[]{:S(2)}) async-start(f32[12,1,128]{2,1,0:T(1,128)} %broadcast_in_dim.27), calls=%async_computation.1 | async-start | bytes 12288 | tf_op jit(solution)/shard_map/all_to_all | solution.py:623
  95.2 8.2 %collective-permute-start.7 = (f32[120,128]{1,0:T(8,128)}, f32[120,128]{1,0:T(8,128)S(1)}, u32[]{:S(2)}, u32[]{:S(2)}) collective-permute-start(f32[120,128]{1,0:T(8,128)} %get-tuple-element.33.part_ref), channel_id=1, source_target_pairs={{0,12},{12,0},{24,36},{36,24},{48,60},{60,48},{72,84},{84,72},{96,... | collective-permute-start | bytes 184328 | tf_op jit(solution)/shard_map/ppermute | solution.py:607
  99.2 7.9 %collective-permute-start.8 = (f32[120,128]{1,0:T(8,128)}, f32[120,128]{1,0:T(8,128)S(1)}, u32[]{:S(2)}, u32[]{:S(2)}) collective-permute-start(f32[120,128]{1,0:T(8,128)} %get-tuple-element.33.part_ref), channel_id=1, source_target_pairs={{12,24},{24,12},{36,48},{48,36},{60,72},{72,60},{84,96},{96,84},{1... | collective-permute-start | bytes 184328 | tf_op jit(solution)/shard_map/ppermute | solution.py:607
  103.5 3.6 %copy-start.4 = (f32[120,128]{1,0:T(8,128)}, f32[120,128]{1,0:T(8,128)S(1)}, u32[]{:S(2)}) copy-start(f32[120,128]{1,0:T(8,128)S(1)} %collective-permute-done.7.first_ref) | copy-start | bytes 184324
  107.1 0.6 copy-start.6
  110.4 7.8 %collective-permute-start.9 = (f32[120,128]{1,0:T(8,128)}, f32[120,128]{1,0:T(8,128)S(1)}, u32[]{:S(2)}, u32[]{:S(2)}) collective-permute-start(f32[120,128]{1,0:T(8,128)} %get-tuple-element.36), channel_id=1, source_target_pairs={{12,0},{24,12},{36,24},{48,36},{60,48},{72,60},{84,72},{96,84},{10... | collective-permute-start | bytes 184328 | tf_op jit(solution)/shard_map/ppermute | solution.py:635
  118.3 0.6 copy-start.7

commit v2 on v1

--- a/solution.py
+++ b/solution.py
@@ -29,6 +29,16 @@
     if b > 0:
         return 16 + 4 * a + 2 * (b - 1) + c - 1
     return 32 + a
+
+
+def face_row(b, c):
+    if b == 0 and c > 0:
+        return c - 1
+    if b > 0 and c == 0:
+        return 2 + b - 1
+    if b > 0:
+        return 4 + 2 * (b - 1) + c - 1
+    return 8
 
 
 def local_row(a, b, c):
@@ -135,38 +145,48 @@
     weight[:125] = quad_weight[:, None]
     out["weight"] = weight
 
-    flat = np.arange(1350)
-    px, py, pz = flat // 450, (flat // 18) % 25, flat % 18
+    flat = np.arange(450)
+    py, pz = flat // 18, flat % 18
     lane = 9 * ((pz + 1) // 3) + py // 3
-    mask = np.zeros((ROWS, 1350), np.float32)
-    mask0 = np.zeros((ROWS, 450), np.float32)
+    mask = np.zeros((4, ROWS, 450), np.float32)
     own = np.zeros((ROWS, 128), np.float32)
-    for k in range(1350):
-        row = node_row(px[k] + 1, py[k] % 3, (pz[k] + 1) % 3)
-        mask[row, k] = 1.0
-        own[row, lane[k] + LANE_OWN] = 1.0
-    for k in range(450):
-        mask0[node_row(0, py[k] % 3, (pz[k] + 1) % 3), k] = 1.0
-    out["mask"] = mask
-    out["mask0"] = mask0
+    face_mask = np.zeros((16, 454), np.float32)
+    for a in range(4):
+        for k in range(450):
+            b, c = py[k] % 3, (pz[k] + 1) % 3
+            row = node_row(a, b, c)
+            mask[a, row, k] = 1.0
+            if a > 0:
+                own[row, lane[k] + LANE_OWN] = 1.0
+            else:
+                face_mask[face_row(b, c), k + 4] = 1.0
+    out["mask"] = mask.reshape(4 * ROWS, 450)
     out["own"] = own
-    pick = np.zeros((1350, 128), np.float32)
+    out["face_mask"] = face_mask
+    pick = np.zeros((450, 128), np.float32)
     pick[flat, lane] = 1.0
-    pick_high = np.zeros((1350, 128), np.float32)
-    pick_high[flat, lane + 64] = 1.0
     out["pick"] = pick.astype(jnp.bfloat16)
-    out["pick_high"] = pick_high.astype(jnp.bfloat16)
-    back = np.zeros((128, 1350), np.float32)
+    back = np.zeros((128, 450), np.float32)
     back[lane + LANE_OWN, flat] = 1.0
     out["back"] = back.astype(jnp.bfloat16)
+    face_back = np.zeros((128, 454), np.float32)
+    face_back[lane + LANE_OWN, flat + 4] = 1.0
+    out["face_back"] = face_back.astype(jnp.bfloat16)
+    off_x = np.ones((ROWS, 128), np.float32)
+    off_z = np.ones((ROWS, 128), np.float32)
+    for b in range(3):
+        for c in range(3):
+            for a in range(4):
+                if a == 0:
+                    off_x[node_row(a, b, c)] = 0.0
+                off_z[node_row(a, b, c), 3 * (np.arange(128) // 9 - BELOW) + c <= 0] = 0.0
+    out["off_x"] = off_x
+    out["off_z"] = off_z
     element = np.arange(EY * EZ)
     elane = 9 * (element % EZ) + element // EZ
     place = np.zeros((48, 128), np.float32)
     place[element, elane] = 1.0
-    place_high = np.zeros((48, 128), np.float32)
-    place_high[element, elane + 64] = 1.0
     out["place"] = place.astype(jnp.bfloat16)
-    out["place_high"] = place_high.astype(jnp.bfloat16)
     take = np.zeros((128, 48), np.float32)
     take[elane + LANE_OWN, element] = 1.0
     out["take"] = take.astype(jnp.bfloat16)
@@ -193,8 +213,10 @@
 
 
 def exact_dot(value, selection):
-    high, middle, low = split3(value)
-    return dot(high, selection) + (dot(middle, selection) + dot(low, selection))
+    high, middle, low = (part.astype(F32) for part in split3(value))
+    rows = value.shape[0]
+    wide = dot(jnp.concatenate([high, middle, low], axis=0).astype(BF), selection)
+    return wide[:rows] + (wide[rows : 2 * rows] + wide[2 * rows :])
 
 
 def stacked(value):
@@ -248,35 +270,74 @@
     return both[:half] + (both[half:] + dot(table[:half], low))
 
 
-def add_planes(nodes, below, above):
-    row = lax.broadcasted_iota(jnp.int32, (8, 128), 0)
+def turned(value, by):
+    return value if by % 8 == 0 else pltpu.roll(value, by % 8, 0)
+
+
+def row_index():
+    return lax.broadcasted_iota(jnp.int32, (8, 128), 0)
+
+
+def face_of(nodes, plane):
+    row = row_index()
+    by = (0, 2, 4) if plane == 0 else (2, 4, 0)
+    inner = 16 if plane == 0 else 24
+    blocks = []
+    corners = jnp.zeros((8, 128), F32)
+    for comp in range(3):
+        at = ROWS * comp
+        first = turned(nodes[at : at + 8], by[0])
+        second = turned(nodes[at + 8 : at + 16], by[1])
+        third = turned(nodes[at + inner : at + inner + 8], by[2])
+        blocks.append(jnp.where(row < 2, first, jnp.where(row < 4, second, third)))
+        corners = jnp.where(row == comp, turned(nodes[at + 32 : at + 40], comp - plane), corners)
+    return jnp.concatenate(blocks + [corners], axis=0)
+
+
+def add_faces(nodes, below, above):
+    row = row_index()
     blocks = []
     for comp in range(3):
         at = ROWS * comp
-        for group in (0, 8):
-            low = pltpu.roll(below[at + group : at + group + 8], 2, 0)
-            high = pltpu.roll(above[at + group : at + group + 8], 6, 0)
-            blocks.append(
-                nodes[at + group : at + group + 8]
-                + jnp.where(row < 2, low, jnp.where(row >= 6, high, 0.0))
-            )
-        low = pltpu.roll(below[at + 24 : at + 32], 4, 0)
-        high = pltpu.roll(above[at + 16 : at + 24], 4, 0)
-        blocks.append(nodes[at + 16 : at + 24] + jnp.where(row < 4, low, 0.0))
+        low, high = below[8 * comp : 8 * comp + 8], above[8 * comp : 8 * comp + 8]
+        blocks.append(
+            nodes[at : at + 8] + jnp.where(row < 2, low, jnp.where(row >= 6, turned(high, 6), 0.0))
+        )
+        blocks.append(
+            nodes[at + 8 : at + 16]
+            + jnp.where(row < 2, turned(low, 6), jnp.where(row >= 6, turned(high, 4), 0.0))
+        )
+        blocks.append(nodes[at + 16 : at + 24] + jnp.where(row < 4, turned(low, 4), 0.0))
         blocks.append(nodes[at + 24 : at + 32] + jnp.where(row >= 4, high, 0.0))
-        low = pltpu.roll(below[at + 32 : at + 40], 5, 0)
-        high = pltpu.roll(above[at + 32 : at + 40], 3, 0)
+        low, high = turned(below[24:32], -comp), turned(above[24:32], 3 - comp)
         blocks.append(
             nodes[at + 32 : at + 40] + jnp.where(row == 0, low, jnp.where(row == 3, high, 0.0))
         )
     return jnp.concatenate(blocks, axis=0)
 
 
-def shared_sum(nodes, even_ref, first_ref, second_ref, wall_ref):
-    even = jnp.concatenate([even_ref[...]] * 15, axis=0) > 0.5
+def flag(flags_ref, row):
+    return flags_ref[row : row + 1, 0:1]
+
+
+def is_even(flags_ref):
+    return jnp.broadcast_to(flag(flags_ref, 0), (32, 128)) > 0.5
+
+
+def send_faces(nodes, flags_ref, first_ref, second_ref):
+    even = is_even(flags_ref)
+    low, high = face_of(nodes, 0), face_of(nodes, 3)
+    first_ref[...] = jnp.where(even, high, low)
+    second_ref[...] = jnp.where(even, low, high)
+
+
+def shared_sum(nodes, flags_ref, first_ref, second_ref, off_x_ref, off_z_ref):
+    even = is_even(flags_ref)
     first, second = first_ref[...], second_ref[...]
-    total = add_planes(nodes, jnp.where(even, second, first), jnp.where(even, first, second))
-    wall = wall_ref[...]
+    total = add_faces(nodes, jnp.where(even, second, first), jnp.where(even, first, second))
+    wall = jnp.maximum(off_x_ref[...], flag(flags_ref, 1)) * jnp.maximum(
+        off_z_ref[...], flag(flags_ref, 2)
+    )
     return total * jnp.concatenate([wall, wall, wall], axis=0)
 
 
@@ -305,34 +366,44 @@
     return [[g[c][m] + 1.0 if c == m else g[c][m] for m in range(3)] for c in range(3)]
 
 
-def pack_kernel(disp_ref, vel_ref, dens_ref, energy_ref, live_ref, mask_ref, pick_ref, pick_high_ref,
-                place_ref, place_high_ref, out_ref):
-    mask = mask_ref[...]
-    for comp in range(3):
-        low = mask * disp_ref[comp : comp + 1, :]
-        high = mask * vel_ref[comp : comp + 1, :]
-        out_ref[ROWS * comp : ROWS * comp + ROWS, :] = exact_dot(low, pick_ref[...]) + exact_dot(
-            high, pick_high_ref[...]
-        )
-    density = jnp.concatenate([dens_ref[0:120], jnp.pad(dens_ref[120:125], ((0, 3), (0, 0)))], axis=0)
+def last_kernel(disp_ref, vel_ref, out_ref):
+    out_ref[0:3, :] = disp_ref[:, 900:1350]
+    out_ref[3:6, :] = vel_ref[:, 900:1350]
+
+
+def add_packed(value, out_ref, at):
+    half = value.shape[0] // 2
+    out_ref[at : at + half, :] = value[:half] + rolled(value[half:], 64)
+
+
+def pack_kernel(disp_ref, vel_ref, dens_ref, energy_ref, live_ref, mask_ref, pick_ref, place_ref,
+                out_ref):
+    masks = [mask_ref[ROWS * a : ROWS * a + ROWS] for a in range(1, 4)]
+    blocks = []
+    for ref in (disp_ref, vel_ref):
+        planes = [ref[:, 450 * x : 450 * x + 450] for x in range(3)]
+        for comp in range(3):
+            blocks.append(
+                sum(masks[x] * planes[x][comp : comp + 1, :] for x in range(3))
+            )
+    add_packed(exact_dot(jnp.concatenate(blocks, axis=0), pick_ref[...]), out_ref, 0)
     row = lax.broadcasted_iota(jnp.int32, (8, 48), 0)
     tail = jnp.pad(energy_ref[24:27], ((0, 5), (0, 0)))
     tail = jnp.where(row == 3, live_ref[...].astype(F32), tail)
-    energy = jnp.concatenate([energy_ref[0:24], tail], axis=0)
-    place, place_high = place_ref[...], place_high_ref[...]
-    out_ref[120:184, :] = exact_dot(density[0:64], place) + exact_dot(density[64:128], place_high)
-    out_ref[184:200, :] = exact_dot(energy[0:16], place) + exact_dot(energy[16:32], place_high)
-
-
-def halo_kernel(packed_ref, halo_ref, mask0_ref, pick_ref, pick_high_ref, out_ref):
-    mask0 = mask0_ref[...]
-    pick, pick_high = pick_ref[0:450, :], pick_high_ref[0:450, :]
+    values = jnp.concatenate(
+        [dens_ref[0:120], jnp.pad(dens_ref[120:125], ((0, 3), (0, 0))), energy_ref[0:24], tail], axis=0
+    )
+    placed = exact_dot(values, place_ref[...])
+    add_packed(placed[0:128], out_ref, 120)
+    add_packed(placed[128:160], out_ref, 184)
+
+
+def halo_kernel(packed_ref, halo_ref, mask_ref, pick_ref, out_ref):
+    mask = mask_ref[0:ROWS]
+    blocks = [mask * halo_ref[comp : comp + 1, :] for comp in range(6)]
+    nodes = exact_dot(jnp.concatenate(blocks, axis=0), pick_ref[...])
+    out_ref[0:120, :] = packed_ref[0:120, :] + (nodes[:120] + rolled(nodes[120:], 64))
     out_ref[120:200, :] = packed_ref[120:200, :]
-    for comp in range(3):
-        low = mask0 * halo_ref[comp : comp + 1, :]
-        high = mask0 * halo_ref[comp + 3 : comp + 4, :]
-        at = slice(ROWS * comp, ROWS * comp + ROWS)
-        out_ref[at, :] = packed_ref[at, :] + (exact_dot(low, pick) + exact_dot(high, pick_high))
 
 
 def unpack(own, below, above):
@@ -352,8 +423,8 @@
 
 
 def force_kernel(own_ref, below_ref, above_ref, grad_ref, grad_t_ref, psi_ref, weight_ref,
-                 force_ref, disp_ref, vel_ref, mass_ref, live_ref, power_ref, wdens_ref,
-                 g_ref, flux_ref, point_ref):
+                 flags_ref, force_ref, face1_ref, face2_ref, disp_ref, vel_ref, mass_ref, live_ref,
+                 power_ref, wdens_ref, g_ref, flux_ref, point_ref):
     disp, vel = unpack(own_ref[0:120], below_ref[0:120], above_ref[0:120])
     disp_ref[...] = disp
     vel_ref[...] = vel
@@ -409,7 +480,9 @@
         wdens = weight * mass_density
         wdens_ref[at, :] = wdens
         mass_ref[at, :] = wdens * alive
-    force_ref[...] = from_local(transposed_dot(grad_t_ref[...], flux_ref[...]))
+    force = from_local(transposed_dot(grad_t_ref[...], flux_ref[...]))
+    force_ref[...] = force
+    send_faces(force, flags_ref, face1_ref, face2_ref)
 
 
 def energy_kernel(power_ref, wdens_ref, psi_t_ref, take_ref, out_ref):
@@ -424,7 +497,7 @@
     return jnp.sum(jnp.sum(value, axis=0, keepdims=True), axis=1, keepdims=True)
 
 
-def mass_points(nodes, phi_ref, mass_ref):
+def mass_points(nodes, phi_ref):
     return dot(phi_ref[...], stacked(to_local(nodes)))
 
 
@@ -441,26 +514,29 @@
     return total_of(nodes * nodes * jnp.concatenate([own, own, own], axis=0))
 
 
-def mass_kernel(part_ref, first_ref, second_ref, even_ref, wall_ref, mass_ref, phi_ref, phi_t_ref,
-                own_ref, own_element_ref, resid_ref, image_ref, sums_ref):
-    resid = shared_sum(part_ref[...], even_ref, first_ref, second_ref, wall_ref)
+def mass_kernel(part_ref, first_ref, second_ref, flags_ref, off_x_ref, off_z_ref, mass_ref, phi_ref,
+                phi_t_ref, own_ref, own_element_ref, resid_ref, image_ref, face1_ref, face2_ref,
+                sums_ref):
+    resid = shared_sum(part_ref[...], flags_ref, first_ref, second_ref, off_x_ref, off_z_ref)
     resid_ref[...] = resid
-    points = mass_points(resid, phi_ref, mass_ref)
+    points = mass_points(resid, phi_ref)
     mass = mass_ref[...]
-    image_ref[...] = from_local(
+    image = from_local(
         transposed_dot(phi_t_ref[...], points * jnp.concatenate([mass, mass, mass], axis=1))
     )
+    image_ref[...] = image
+    send_faces(image, flags_ref, face1_ref, face2_ref)
     norm = norm_of(resid, own_ref[...])
     energy = point_energy(points, mass, own_element_ref[0:1])
     lane = lax.broadcasted_iota(jnp.int32, (8, 128), 1)
     sums_ref[...] = jnp.where(lane == 0, norm, jnp.where(lane == 1, energy, 0.0))
 
 
-def moment_kernel(part_ref, first_ref, second_ref, even_ref, wall_ref, mass_ref, phi_ref, own_ref,
-                  own_element_ref, sums_ref, image_ref, out_ref):
-    image = shared_sum(part_ref[...], even_ref, first_ref, second_ref, wall_ref)
+def moment_kernel(part_ref, first_ref, second_ref, flags_ref, off_x_ref, off_z_ref, mass_ref, phi_ref,
+                  own_ref, own_element_ref, sums_ref, image_ref, out_ref):
+    image = shared_sum(part_ref[...], flags_ref, first_ref, second_ref, off_x_ref, off_z_ref)
     image_ref[...] = image
-    points = mass_points(image, phi_ref, mass_ref)
+    points = mass_points(image, phi_ref)
     norm = norm_of(image, own_ref[...])
     energy = point_energy(points, mass_ref[...], own_element_ref[0:1])
     lane = lax.broadcasted_iota(jnp.int32, (1, 128), 1)
@@ -492,9 +568,9 @@
     return from_local(transposed_dot(grad_t_ref[...], flux_ref[...]))
 
 
-def first_shape_kernel(moments_ref, disp_ref, vel_ref, resid_ref, image_ref, live_ref, step_ref,
-                       grad_ref, grad_t_ref, weight_ref, newvel_ref, moved_ref, part_ref,
-                       g_ref, flux_ref):
+def first_shape_kernel(moments_ref, disp_ref, vel_ref, resid_ref, image_ref, live_ref, flags_ref,
+                       grad_ref, grad_t_ref, weight_ref, newvel_ref, moved_ref, part_ref, face1_ref,
+                       face2_ref, g_ref, flux_ref):
     moments = jnp.sum(moments_ref[...], axis=0, keepdims=True)
     mu0, mu1, mu2, mu3 = (moments[:, i : i + 1] for i in range(4))
     alpha = mu0 / mu1
@@ -502,45 +578,49 @@
     beta = rest / mu0
     gain = 1.0 + beta
     second = rest / (gain * gain * mu1 - 2.0 * gain * alpha * mu2 + alpha * alpha * mu3)
-    step = step_ref[0:1, 0:1]
+    step = flag(flags_ref, 3)
     newvel = vel_ref[...] + step * (
         (alpha + second * gain) * resid_ref[...] - (alpha * second) * image_ref[...]
     )
     newvel_ref[...] = newvel
     moved = disp_ref[...] + step * newvel
     moved_ref[...] = moved
-    part_ref[...] = shape_forces(
-        moved, live_ref[...], grad_ref, grad_t_ref, weight_ref, g_ref, flux_ref
-    )
-
-
-def second_shape_kernel(part_ref, first_ref, second_ref, even_ref, wall_ref, newvel_ref, moved_ref,
-                        live_ref, step_ref, grad_ref, grad_t_ref, weight_ref, base_ref, next_ref,
+    part = shape_forces(moved, live_ref[...], grad_ref, grad_t_ref, weight_ref, g_ref, flux_ref)
+    part_ref[...] = part
+    send_faces(part, flags_ref, face1_ref, face2_ref)
+
+
+def second_shape_kernel(part_ref, first_ref, second_ref, flags_ref, off_x_ref, off_z_ref, newvel_ref,
+                        moved_ref, live_ref, grad_ref, grad_t_ref, weight_ref, base_ref, face_ref,
                         g_ref, flux_ref):
-    gradient = shared_sum(part_ref[...], even_ref, first_ref, second_ref, wall_ref)
+    gradient = shared_sum(part_ref[...], flags_ref, first_ref, second_ref, off_x_ref, off_z_ref)
     u = moved_ref[...] - MESH_STEP * gradient
     part = shape_forces(u, live_ref[...], grad_ref, grad_t_ref, weight_ref, g_ref, flux_ref)
-    next_ref[...] = part
-    base_ref[...] = newvel_ref[...] - (MESH_STEP / step_ref[0:1, 0:1]) * (gradient + part)
-
-
-def write_nodes(nodes, mask_ref, back_ref, out_ref):
-    mask = mask_ref[...]
-    back = back_ref[...]
+    face_ref[...] = face_of(part, 0)
+    base_ref[...] = newvel_ref[...] - (MESH_STEP / flag(flags_ref, 3)) * (gradient + part)
+
+
+def write_kernel(nodes_ref, mask_ref, back_ref, out_ref):
+    wide = exact_dot(nodes_ref[...], back_ref[...])
     for comp in range(3):
-        wide = exact_dot(nodes[ROWS * comp : ROWS * comp + ROWS], back)
-        out_ref[comp : comp + 1, :] = jnp.sum(wide * mask, axis=0, keepdims=True)
-
-
-def velocity_kernel(nodes_ref, mask_ref, back_ref, out_ref):
-    write_nodes(nodes_ref[...], mask_ref, back_ref, out_ref)
-
-
-def mesh_kernel(base_ref, above_ref, step_ref, mask_ref, back_ref, out_ref):
-    zero = jnp.zeros((120, 128), F32)
-    extra = add_planes(zero, zero, above_ref[...])
-    nodes = base_ref[...] - (MESH_STEP / step_ref[0:1, 0:1]) * extra
-    write_nodes(nodes, mask_ref, back_ref, out_ref)
+        part = wide[ROWS * comp : ROWS * comp + ROWS]
+        planes = [
+            jnp.sum(part * mask_ref[ROWS * a : ROWS * a + ROWS], axis=0, keepdims=True)
+            for a in range(1, 4)
+        ]
+        out_ref[comp : comp + 1, :] = jnp.concatenate(planes, axis=1)
+
+
+def mesh_kernel(base_ref, face_ref, flags_ref, face_mask_ref, face_back_ref, out_ref):
+    scale = -MESH_STEP / flag(flags_ref, 3)
+    wide = exact_dot(face_ref[...], face_back_ref[...])
+    mask = face_mask_ref[0:8]
+    corner = face_mask_ref[8:9]
+    out_ref[:, 0:896] = base_ref[:, 0:896]
+    for comp in range(3):
+        extra = jnp.sum(wide[8 * comp : 8 * comp + 8] * mask, axis=0, keepdims=True)
+        extra = extra + wide[24 + comp : 25 + comp] * corner
+        out_ref[comp : comp + 1, 896:1350] = base_ref[comp : comp + 1, 896:1350] + scale * extra
 
 
 def call(kernel, name, outs, scratch=(), flops=1_000_000):
@@ -554,6 +634,7 @@
             out_specs=[spec] * len(outs),
             scratch_shapes=[pltpu.VMEM(shape, F32) for shape in scratch],
             name=name,
+            compiler_params=pltpu.CompilerParams(vmem_limit_bytes=16 * 1024 * 1024),
             cost_estimate=pl.CostEstimate(flops=flops, bytes_accessed=400_000, transcendentals=0),
         )(*args)
 
@@ -562,6 +643,7 @@
 
 NODES = (120, 128)
 POINTS = (128, 128)
+FACE = (32, 128)
 
 
 def body(displacement, velocity, energy, mass_density, live_mask, time_step):
@@ -575,66 +657,66 @@
     z_up = [(i, i + 1) for i in range(n_sub - 1)]
     z_down = [(i + 1, i) for i in range(n_sub - 1)]
 
-    step = jnp.broadcast_to(time_step.reshape(1, 1), (8, 128))
-    even = jnp.broadcast_to((1 - dom % 2).astype(F32).reshape(1, 1), (8, 128))
-    rows = np.arange(ROWS)
-    row_a = np.select([rows < 8, rows < 16, rows < 32, rows < 36],
-                      [rows // 2, (rows - 8) // 2, (rows - 16) // 4, rows - 32], 9)
-    row_c = np.select([rows < 8, rows < 16, rows < 32], [rows % 2 + 1, 0 * rows, rows % 2 + 1], 0)
-    node_z = 3 * (np.arange(128) // 9 - BELOW)[None, :] + row_c[:, None]
-    on_x = jnp.asarray(np.broadcast_to((row_a == 0)[:, None], (ROWS, 128)))
-    on_z = jnp.asarray(node_z <= 0)
-    wall = jnp.where((on_x & (dom == 0)) | (on_z & (sub == 0)), 0.0, 1.0).astype(F32)
-
-    last = jnp.concatenate([displacement[:, 900:], velocity[:, 900:]], axis=0)
+    row = lax.broadcasted_iota(jnp.int32, (8, 128), 0)
+    flags = jnp.where(
+        row == 0,
+        (1 - dom % 2).astype(F32),
+        jnp.where(
+            row == 1,
+            jnp.minimum(dom, 1).astype(F32),
+            jnp.where(row == 2, jnp.minimum(sub, 1).astype(F32), time_step),
+        ),
+    )
+    walls = (table["off_x"], table["off_z"])
+
+    (last,) = call(last_kernel, "last", [(6, 450)])(displacement, velocity)
     halo = lax.ppermute(last, "dom", up)
     (packed,) = call(pack_kernel, "pack", [(200, 128)])(
         displacement, velocity, mass_density, energy, live_mask.reshape(1, 48), table["mask"],
-        table["pick"], table["pick_high"], table["place"], table["place_high"],
-    )
-    (own,) = call(halo_kernel, "halo", [(200, 128)])(
-        packed, halo, table["mask0"], table["pick"], table["pick_high"]
-    )
+        table["pick"], table["place"],
+    )
+    (own,) = call(halo_kernel, "halo", [(200, 128)])(packed, halo, table["mask"], table["pick"])
     below = lax.ppermute(own, "sub", z_up)
     above = lax.ppermute(own, "sub", z_down)
-    force, disp, vel, mass, live, power, wdens = call(
+    force, face1, face2, disp, vel, mass, live, power, wdens = call(
         force_kernel, "force",
-        [NODES, NODES, NODES, POINTS, (8, 128), POINTS, POINTS],
+        [NODES, FACE, FACE, NODES, NODES, POINTS, (8, 128), POINTS, POINTS],
         [(384, 768), (384, 384), POINTS],
-    )(own, below, above, table["grad"], table["grad_t"], table["psi"], table["weight"])
-
-    def swap(part):
-        return lax.ppermute(part, "dom", pairs_first), lax.ppermute(part, "dom", pairs_second)
-
-    first, second = swap(force)
+    )(own, below, above, table["grad"], table["grad_t"], table["psi"], table["weight"], flags)
+
+    def swap(face1, face2):
+        return lax.ppermute(face1, "dom", pairs_first), lax.ppermute(face2, "dom", pairs_second)
+
+    first, second = swap(face1, face2)
     (energy_rate,) = call(energy_kernel, "energy", [(27, 48)])(
         power, wdens, table["psi_t"], table["take"]
     )
-    resid, image_part, sums = call(mass_kernel, "mass", [NODES, NODES, (8, 128)])(
-        force, first, second, even, wall, mass, table["phi"], table["phi_t"], table["own"],
-        table["own_element"],
-    )
-    first, second = swap(image_part)
+    force, energy_rate = lax.optimization_barrier((force, energy_rate))
+    resid, image_part, face1, face2, sums = call(
+        mass_kernel, "mass", [NODES, NODES, FACE, FACE, (8, 128)]
+    )(force, first, second, flags, *walls, mass, table["phi"], table["phi_t"], table["own"],
+      table["own_element"])
+    first, second = swap(face1, face2)
     image, local = call(moment_kernel, "moment", [NODES, (n_dom, 128)])(
-        image_part, first, second, even, wall, mass, table["phi"], table["own"],
+        image_part, first, second, flags, *walls, mass, table["phi"], table["own"],
         table["own_element"], sums,
     )
     slab = jnp.sum(lax.all_to_all(local, "dom", 0, 0, tiled=True), axis=0, keepdims=True)
     moments = lax.all_to_all(jnp.broadcast_to(slab, (n_sub, 128)), "sub", 0, 0, tiled=True)
-    newvel, moved, part = call(
-        first_shape_kernel, "shape1", [NODES, NODES, NODES], [(384, 384), (384, 384)]
-    )(moments, disp, vel, resid, image, live, step, table["grad"], table["grad_t"], table["weight"])
-    first, second = swap(part)
-    (new_velocity,) = call(velocity_kernel, "newvel", [(3, 1350)])(
-        newvel, table["mask"], table["back"]
-    )
-    base, part = call(
-        second_shape_kernel, "shape2", [NODES, NODES], [(384, 384), (384, 384)]
-    )(part, first, second, even, wall, newvel, moved, live, step, table["grad"], table["grad_t"],
+    newvel, moved, part, face1, face2 = call(
+        first_shape_kernel, "shape1", [NODES, NODES, NODES, FACE, FACE], [(384, 384), (384, 384)]
+    )(moments, disp, vel, resid, image, live, flags, table["grad"], table["grad_t"], table["weight"])
+    first, second = swap(face1, face2)
+    (new_velocity,) = call(write_kernel, "newvel", [(3, 1350)])(newvel, table["mask"], table["back"])
+    part, new_velocity = lax.optimization_barrier((part, new_velocity))
+    base, face = call(
+        second_shape_kernel, "shape2", [NODES, FACE], [(384, 384), (384, 384)]
+    )(part, first, second, flags, *walls, newvel, moved, live, table["grad"], table["grad_t"],
       table["weight"])
-    from_above = lax.ppermute(part, "dom", down)
+    from_above = lax.ppermute(face, "dom", down)
+    (mesh_base,) = call(write_kernel, "base", [(3, 1350)])(base, table["mask"], table["back"])
     (mesh_velocity,) = call(mesh_kernel, "mesh", [(3, 1350)])(
-        base, from_above, step, table["mask"], table["back"]
+        mesh_base, from_above, flags, table["face_mask"], table["face_back"]
     )
     return new_velocity, energy_rate, mesh_velocity
 

time: 123 us -> 101 us (0.82)
  blocking collectives: 14.8 us -> 39.8 us
  Pallas kernels: 24.5 us -> 8.11 us
  starting transfers between devices: 43.4 us -> 29.6 us
  waiting for transfers between devices: 28.5 us -> 16.3 us
  local copies, waits for them, and re-layouts: 7.8 us -> 4.46 us
    all_to_all x0 -> x1, blocking collectives: none -> 25.2 us  [body(): lax.all_to_all(jnp.broadcast_to(slab, (n_sub, 128)), 'sub', 0, 0, tiled=T...]
    pallas_call x10 -> x12, Pallas kernels: 24.5 us -> 8.11 us  [run(): pl.pallas_call(kernel, out_shape=[jax.ShapeDtypeStruct(shape, F32) for sh...]
    all_to_all x1 -> x0, starting transfers between devices: 14.5 us -> none  [body(): lax.all_to_all(jnp.broadcast_to(slab, (n_sub, 128)), 'sub', 0, 0, tiled=T...]
    all_to_all x1 -> x0, waiting for transfers between devices: 8.22 us -> none  [body(): lax.all_to_all(jnp.broadcast_to(slab, (n_sub, 128)), 'sub', 0, 0, tiled=T...]
    ppermute x1, waiting for transfers between devices: 4.65 us -> 1.2 us  [body(): above = lax.ppermute(own, 'sub', z_down)]
    slice x2 -> x0, local copies, waits for them, and re-layouts: 1.55 us -> none  [body(): last = jnp.concatenate([displacement[:, 900:], velocity[:, 900:]], axis=0)]
    unnamed x28 -> x52, local copies, waits for them, and re-layouts: 4.43 us -> 4.45 us
  transfers between devices with their start and end apart: 11 -> 10, of which waited for: 7 -> 6; matrix products, arithmetic and copies ran while one was open for 1% -> 1% of each run, Pallas kernels for 6% -> 3%
where the time goes in v2:
time: 101 us; the launch traced here: 100 us
  blocking collectives  39.8 us (39%)
  starting transfers between devices  29.6 us (29%)
  waiting for transfers between devices  16.3 us (16%)
  Pallas kernels  8.11 us (8%)
  local copies, waits for them, and re-layouts  4.46 us (4%)
  between operations  1.72 us (2%)
    all_to_all x1, blocking collectives, body(): lax.all_to_all(jnp.broadcast_to(slab, (n_sub, 128)), 'sub', 0, 0, tiled=T...  25.2 us
    all_to_all x1, blocking collectives, body(): lax.all_to_all(local, 'dom', 0, 0, tiled=True)  14.6 us
    ppermute x3, starting transfers between devices, swap(): lax.ppermute(face2, 'dom', pairs_second)  10.5 us
    ppermute x3, waiting for transfers between devices, swap(): lax.ppermute(face2, 'dom', pairs_second)  9.01 us
    ppermute x3, starting transfers between devices, swap(): lax.ppermute(face1, 'dom', pairs_first)  8.38 us
    pallas_call x12, Pallas kernels, run(): pl.pallas_call(kernel, out_shape=[jax.ShapeDtypeStruct(shape, F32) for sh...  8.11 us
    ppermute x1, waiting for transfers between devices, body(): from_above = lax.ppermute(face, 'dom', down)  4.83 us
    ppermute x1, starting transfers between devices, body(): below = lax.ppermute(own, 'sub', z_up)  4.63 us
  transfers between devices with their start and end apart: 10, of which 6 were waited for; matrix products, arithmetic and copies ran while one was open for 1% of the time, Pallas kernels for 3%

profile of v2, /device:TPU:57, one launch (start us, length us, event | category | flops | bytes accessed | tf_op | source)
XLA Modules:
  0.0 100.1 jit_solution(4574820191107248460)
XLA Ops:
  2.2 2.9 %collective-permute-start = (f32[6,450]{1,0:T(8,128)S(1)}, f32[6,450]{1,0:T(8,128)S(1)}, u32[]{:S(2)}, u32[]{:S(2)}) collective-permute-start(f32[6,450]{1,0:T(8,128)S(1)} %last.1), channel_id=1, source_target_pairs={{0,12},{12,24},{24,36},{36,48},{48,60},{60,72},{72,84},{84,96},{96... | collective-permute-start | bytes 32408 | tf_op jit(solution)/shard_map/ppermute | solution.py:673
  7.4 1.0 copy-done
  9.8 1.3 %collective-permute-start.2 = (f32[200,128]{1,0:T(8,128)S(1)}, f32[200,128]{1,0:T(8,128)S(1)}, u32[]{:S(2)}, u32[]{:S(2)}) collective-permute-start(f32[200,128]{1,0:T(8,128)S(1)} %halo.1.own_ref), channel_id=1, source_target_pairs={{1,0},{2,1},{3,2},{4,3},{5,4},{6,5},{7,6},{8,7},{9,8},{10,9},{11,1... | collective-permute-start | bytes 307208 | tf_op jit(solution)/shard_map/ppermute | solution.py:680
  11.1 4.6 %collective-permute-start.1 = (f32[200,128]{1,0:T(8,128)S(1)}, f32[200,128]{1,0:T(8,128)S(1)}, u32[]{:S(2)}, u32[]{:S(2)}) collective-permute-start(f32[200,128]{1,0:T(8,128)S(1)} %halo.1.own_ref), channel_id=1, source_target_pairs={{0,1},{1,2},{2,3},{3,4},{4,5},{5,6},{6,7},{7,8},{8,9},{9,10},{10,1... | collective-permute-start | bytes 307208 | tf_op jit(solution)/shard_map/ppermute | solution.py:679
  15.8 1.2 %collective-permute-done.2.above_ref = f32[200,128]{1,0:T(8,128)S(1)} collective-permute-done((f32[200,128]{1,0:T(8,128)S(1)}, f32[200,128]{1,0:T(8,128)S(1)}, u32[]{:S(2)}, u32[]{:S(2)}) %collective-permute-start.2) | collective-permute-done | bytes 102432 | tf_op jit(solution)/shard_map/ppermute | solution.py:680
  17.0 1.2 %collective-permute-done.1.below_ref = f32[200,128]{1,0:T(8,128)S(1)} collective-permute-done((f32[200,128]{1,0:T(8,128)S(1)}, f32[200,128]{1,0:T(8,128)S(1)}, u32[]{:S(2)}, u32[]{:S(2)}) %collective-permute-start.1) | collective-permute-done | bytes 102432 | tf_op jit(solution)/shard_map/ppermute | solution.py:679
  18.2 1.1 %force.1 = (f32[120,128]{1,0:T(8,128)S(1)}, f32[32,128]{1,0:T(8,128)S(1)}, f32[32,128]{1,0:T(8,128)S(1)}, f32[120,128]{1,0:T(8,128)S(1)}, f32[120,128]{1,0:T(8,1...) custom-call(f32[200,128]{1,0:T(8,128)S(1)} %halo.1.own_ref, ...), custom_call_target="tpu_custom_call" | custom-call | flops 1000000 | bytes 400000 | tf_op jit(solution)/shard_map/force/pallas_call | solution.py:630
  19.4 2.5 %collective-permute-start.3 = (f32[32,128]{1,0:T(8,128)S(1)}, f32[32,128]{1,0:T(8,128)S(1)}, u32[]{:S(2)}, u32[]{:S(2)}) collective-permute-start(f32[32,128]{1,0:T(8,128)S(1)} %get-tuple-element.34), channel_id=1, source_target_pairs={{0,12},{12,0},{24,36},{36,24},{48,60},{60,48},{72,84},{84,72},{96,... | collective-permute-start | bytes 49160 | tf_op jit(solution)/shard_map/ppermute | solution.py:688
  21.9 3.1 %collective-permute-start.4 = (f32[32,128]{1,0:T(8,128)S(1)}, f32[32,128]{1,0:T(8,128)S(1)}, u32[]{:S(2)}, u32[]{:S(2)}) collective-permute-start(f32[32,128]{1,0:T(8,128)S(1)} %get-tuple-element.35), channel_id=1, source_target_pairs={{12,24},{24,12},{36,48},{48,36},{60,72},{72,60},{84,96},{96,84},{1... | collective-permute-start | bytes 49160 | tf_op jit(solution)/shard_map/ppermute | solution.py:688
  25.1 0.9 energy.1
  26.0 3.1 %collective-permute-done.4.second_ref = f32[32,128]{1,0:T(8,128)S(1)} collective-permute-done((f32[32,128]{1,0:T(8,128)S(1)}, f32[32,128]{1,0:T(8,128)S(1)}, u32[]{:S(2)}, u32[]{:S(2)}) %collective-permute-start.4) | collective-permute-done | bytes 16416 | tf_op jit(solution)/shard_map/ppermute | solution.py:688
  29.6 1.9 %collective-permute-start.5 = (f32[32,128]{1,0:T(8,128)S(1)}, f32[32,128]{1,0:T(8,128)S(1)}, u32[]{:S(2)}, u32[]{:S(2)}) collective-permute-start(f32[32,128]{1,0:T(8,128)S(1)} %get-tuple-element.38), channel_id=1, source_target_pairs={{0,12},{12,0},{24,36},{36,24},{48,60},{60,48},{72,84},{84,72},{96,... | collective-permute-start | bytes 49160 | tf_op jit(solution)/shard_map/ppermute | solution.py:688
  31.6 3.1 %collective-permute-start.6 = (f32[32,128]{1,0:T(8,128)S(1)}, f32[32,128]{1,0:T(8,128)S(1)}, u32[]{:S(2)}, u32[]{:S(2)}) collective-permute-start(f32[32,128]{1,0:T(8,128)S(1)} %get-tuple-element.39), channel_id=1, source_target_pairs={{12,24},{24,12},{36,48},{48,36},{60,72},{72,60},{84,96},{96,84},{1... | collective-permute-start | bytes 49160 | tf_op jit(solution)/shard_map/ppermute | solution.py:688
  34.7 4.0 %collective-permute-done.6.second_ref = f32[32,128]{1,0:T(8,128)S(1)} collective-permute-done((f32[32,128]{1,0:T(8,128)S(1)}, f32[32,128]{1,0:T(8,128)S(1)}, u32[]{:S(2)}, u32[]{:S(2)}) %collective-permute-start.6) | collective-permute-done | bytes 16416 | tf_op jit(solution)/shard_map/ppermute | solution.py:688
  39.1 14.6 %all_to_all.17 = f32[64,1,128]{2,1,0:T(1,128)S(1)} all-to-all(f32[64,1,128]{2,1,0:T(1,128)S(1)} %bitcast.8), channel_id=1, replica_groups=mesh['dom'=64,'sub'=12] {'dom'}, dimensions={0} | all-to-all | bytes 65536 | tf_op jit(solution)/shard_map/all_to_all | solution.py:704
  53.8 25.2 %all_to_all.18 = f32[12,1,128]{2,1,0:T(1,128)S(1)} all-to-all(f32[12,1,128]{2,1,0:T(1,128)S(1)} %broadcast_in_dim.25), channel_id=1, replica_groups=mesh['dom'=64,'sub'=12] {'sub'}, dimensions={0} | all-to-all | bytes 12288 | tf_op jit(solution)/shard_map/all_to_all | solution.py:705
  79.0 1.0 %shape1.1 = (f32[120,128]{1,0:T(8,128)S(1)}, f32[120,128]{1,0:T(8,128)S(1)}, f32[120,128]{1,0:T(8,128)S(1)}, f32[32,128]{1,0:T(8,128)S(1)}, f32[32,128]{1,0:T(8,128)S(1)}) custom-call(f32[12,128]{1,0:T(8,128)S(1)} %bitcast.7, f32[120,128]{1,0:T(8,128)S(1)} %get-tuple-element.42.disp_ref, f32[120,128]{1,0:T(8,128)S(1)} %get-tuple-element.43.vel_ref, ...), custom_call_target="tpu_custom_call" | custom-call | flops 1000000 | bytes 400000 | tf_op jit(solution)/shard_map/shape1/pallas_call | solution.py:630
  80.1 4.0 %collective-permute-start.7 = (f32[32,128]{1,0:T(8,128)S(1)}, f32[32,128]{1,0:T(8,128)S(1)}, u32[]{:S(2)}, u32[]{:S(2)}) collective-permute-start(f32[32,128]{1,0:T(8,128)S(1)} %get-tuple-element.52), channel_id=1, source_target_pairs={{0,12},{12,0},{24,36},{36,24},{48,60},{60,48},{72,84},{84,72},{96,... | collective-permute-start | bytes 49160 | tf_op jit(solution)/shard_map/ppermute | solution.py:688
  84.0 4.3 %collective-permute-start.8 = (f32[32,128]{1,0:T(8,128)S(1)}, f32[32,128]{1,0:T(8,128)S(1)}, u32[]{:S(2)}, u32[]{:S(2)}) collective-permute-start(f32[32,128]{1,0:T(8,128)S(1)} %get-tuple-element.53), channel_id=1, source_target_pairs={{12,24},{24,12},{36,48},{48,36},{60,72},{72,60},{84,96},{96,84},{1... | collective-permute-start | bytes 49160 | tf_op jit(solution)/shard_map/ppermute | solution.py:688
  88.3 1.0 newvel.1
  89.3 1.9 %collective-permute-done.8.second_ref = f32[32,128]{1,0:T(8,128)S(1)} collective-permute-done((f32[32,128]{1,0:T(8,128)S(1)}, f32[32,128]{1,0:T(8,128)S(1)}, u32[]{:S(2)}, u32[]{:S(2)}) %collective-permute-start.8) | collective-permute-done | bytes 16416 | tf_op jit(solution)/shard_map/ppermute | solution.py:688
  91.2 0.9 shape2.1
  92.1 1.9 %collective-permute-start.9 = (f32[32,128]{1,0:T(8,128)S(1)}, f32[32,128]{1,0:T(8,128)S(1)}, u32[]{:S(2)}, u32[]{:S(2)}) collective-permute-start(f32[32,128]{1,0:T(8,128)S(1)} %get-tuple-element.56), channel_id=1, source_target_pairs={{12,0},{24,12},{36,24},{48,36},{60,48},{72,60},{84,72},{96,84},{10... | collective-permute-start | bytes 49160 | tf_op jit(solution)/shard_map/ppermute | solution.py:716
  94.5 4.8 %collective-permute-done.9.face_ref = f32[32,128]{1,0:T(8,128)S(1)} collective-permute-done((f32[32,128]{1,0:T(8,128)S(1)}, f32[32,128]{1,0:T(8,128)S(1)}, u32[]{:S(2)}, u32[]{:S(2)}) %collective-permute-start.9) | collective-permute-done | bytes 16416 | tf_op jit(solution)/shard_map/ppermute | solution.py:716
  (67 shorter events, 6.8 us)
Async XLA Ops:
  0.6 6.1 %copy-start.6 = (bf16[450,128]{1,0:T(8,128)(2,1)S(1)}, bf16[450,128]{1,0:T(8,128)(2,1)}, u32[]{:S(2)}) copy-start(bf16[450,128]{1,0:T(8,128)(2,1)} %constant.71.clone.pick_ref) | copy-start | bytes 345604
  2.2 6.7 %collective-permute-start = (f32[6,450]{1,0:T(8,128)S(1)}, f32[6,450]{1,0:T(8,128)S(1)}, u32[]{:S(2)}, u32[]{:S(2)}) collective-permute-start(f32[6,450]{1,0:T(8,128)S(1)} %last.1), channel_id=1, source_target_pairs={{0,12},{12,24},{24,36},{36,48},{48,60},{60,72},{72,84},{84,96},{96... | collective-permute-start | bytes 32408 | tf_op jit(solution)/shard_map/ppermute | solution.py:673
  8.9 9.3 %copy-start.2 = (bf16[384,240]{1,0:T(8,128)(2,1)S(1)}, bf16[384,240]{1,0:T(8,128)(2,1)}, u32[]{:S(2)}) copy-start(bf16[384,240]{1,0:T(8,128)(2,1)} %constant.61.clone.grad_ref) | copy-start | bytes 552964
  8.9 9.3 %copy-start.3 = (bf16[160,384]{1,0:T(8,128)(2,1)S(1)}, bf16[160,384]{1,0:T(8,128)(2,1)}, u32[]{:S(2)}) copy-start(bf16[160,384]{1,0:T(8,128)(2,1)} %constant.62.clone.grad_t_ref) | copy-start | bytes 368644
  8.9 9.3 %copy-start.4 = (f32[128,128]{1,0:T(8,128)S(1)}, f32[128,128]{1,0:T(8,128)}, u32[]{:S(2)}) copy-start(f32[128,128]{1,0:T(8,128)} %constant.67.clone.weight_ref) | copy-start | bytes 196612
  9.3 8.9 %copy-start.18 = (bf16[128,96]{1,0:T(8,128)(2,1)S(1)}, bf16[128,96]{1,0:T(8,128)(2,1)}, u32[]{:S(2)}) copy-start(bf16[128,96]{1,0:T(8,128)(2,1)} %constant.65.clone.psi_ref) | copy-start | bytes 73732
  9.8 7.2 %collective-permute-start.2 = (f32[200,128]{1,0:T(8,128)S(1)}, f32[200,128]{1,0:T(8,128)S(1)}, u32[]{:S(2)}, u32[]{:S(2)}) collective-permute-start(f32[200,128]{1,0:T(8,128)S(1)} %halo.1.own_ref), channel_id=1, source_target_pairs={{1,0},{2,1},{3,2},{4,3},{5,4},{6,5},{7,6},{8,7},{9,8},{10,9},{11,1... | collective-permute-start | bytes 307208 | tf_op jit(solution)/shard_map/ppermute | solution.py:680
  11.1 7.1 %collective-permute-start.1 = (f32[200,128]{1,0:T(8,128)S(1)}, f32[200,128]{1,0:T(8,128)S(1)}, u32[]{:S(2)}, u32[]{:S(2)}) collective-permute-start(f32[200,128]{1,0:T(8,128)S(1)} %halo.1.own_ref), channel_id=1, source_target_pairs={{0,1},{1,2},{2,3},{3,4},{4,5},{5,6},{6,7},{7,8},{8,9},{9,10},{10,1... | collective-permute-start | bytes 307208 | tf_op jit(solution)/shard_map/ppermute | solution.py:679
  15.8 9.2 %copy-start.19 = (bf16[128,48]{1,0:T(8,128)(2,1)S(1)}, bf16[128,48]{1,0:T(8,128)(2,1)}, u32[]{:S(2)}) copy-start(bf16[128,48]{1,0:T(8,128)(2,1)} %constant.77.clone.take_ref) | copy-start | bytes 36868
  18.2 6.8 %copy-start.22 = (bf16[64,128]{1,0:T(8,128)(2,1)S(1)}, bf16[64,128]{1,0:T(8,128)(2,1)}, u32[]{:S(2)}) copy-start(bf16[64,128]{1,0:T(8,128)(2,1)} %constant.66.clone.psi_t_ref) | copy-start | bytes 49156
  19.4 6.6 %collective-permute-start.3 = (f32[32,128]{1,0:T(8,128)S(1)}, f32[32,128]{1,0:T(8,128)S(1)}, u32[]{:S(2)}, u32[]{:S(2)}) collective-permute-start(f32[32,128]{1,0:T(8,128)S(1)} %get-tuple-element.34), channel_id=1, source_target_pairs={{0,12},{12,0},{24,36},{36,24},{48,60},{60,48},{72,84},{84,72},{96,... | collective-permute-start | bytes 49160 | tf_op jit(solution)/shard_map/ppermute | solution.py:688
  21.9 7.2 %collective-permute-start.4 = (f32[32,128]{1,0:T(8,128)S(1)}, f32[32,128]{1,0:T(8,128)S(1)}, u32[]{:S(2)}, u32[]{:S(2)}) collective-permute-start(f32[32,128]{1,0:T(8,128)S(1)} %get-tuple-element.35), channel_id=1, source_target_pairs={{12,24},{24,12},{36,48},{48,36},{60,72},{72,60},{84,96},{96,84},{1... | collective-permute-start | bytes 49160 | tf_op jit(solution)/shard_map/ppermute | solution.py:688
  25.0 4.0 %copy-start.7 = (bf16[128,240]{1,0:T(8,128)(2,1)S(1)}, bf16[128,240]{1,0:T(8,128)(2,1)}, u32[]{:S(2)}) copy-start(bf16[128,240]{1,0:T(8,128)(2,1)} %constant.63.clone.phi_ref) | copy-start | bytes 184324
  25.0 4.0 %copy-start.8 = (f32[40,128]{1,0:T(8,128)S(1)}, f32[40,128]{1,0:T(8,128)}, u32[]{:S(2)}) copy-start(f32[40,128]{1,0:T(8,128)} %constant.75.clone.off_z_ref) | copy-start | bytes 61444
  25.0 4.0 %copy-start.9 = (f32[40,128]{1,0:T(8,128)S(1)}, f32[40,128]{1,0:T(8,128)}, u32[]{:S(2)}) copy-start(f32[40,128]{1,0:T(8,128)} %constant.74.clone.off_x_ref) | copy-start | bytes 61444
  25.0 4.0 %copy-start.15 = (f32[40,128]{1,0:T(8,128)S(1)}, f32[40,128]{1,0:T(8,128)}, u32[]{:S(2)}) copy-start(f32[40,128]{1,0:T(8,128)} %constant.69.clone.own_ref) | copy-start | bytes 61444
  29.6 5.0 %collective-permute-start.5 = (f32[32,128]{1,0:T(8,128)S(1)}, f32[32,128]{1,0:T(8,128)S(1)}, u32[]{:S(2)}, u32[]{:S(2)}) collective-permute-start(f32[32,128]{1,0:T(8,128)S(1)} %get-tuple-element.38), channel_id=1, source_target_pairs={{0,12},{12,0},{24,36},{36,24},{48,60},{60,48},{72,84},{84,72},{96,... | collective-permute-start | bytes 49160 | tf_op jit(solution)/shard_map/ppermute | solution.py:688
  31.6 7.2 %collective-permute-start.6 = (f32[32,128]{1,0:T(8,128)S(1)}, f32[32,128]{1,0:T(8,128)S(1)}, u32[]{:S(2)}, u32[]{:S(2)}) collective-permute-start(f32[32,128]{1,0:T(8,128)S(1)} %get-tuple-element.39), channel_id=1, source_target_pairs={{12,24},{24,12},{36,48},{48,36},{60,72},{72,60},{84,96},{96,84},{1... | collective-permute-start | bytes 49160 | tf_op jit(solution)/shard_map/ppermute | solution.py:688
  79.0 9.3 %copy-start.5 = (bf16[128,450]{1,0:T(8,128)(2,1)S(1)}, bf16[128,450]{1,0:T(8,128)(2,1)}, u32[]{:S(2)}) copy-start(bf16[128,450]{1,0:T(8,128)(2,1)} %constant.72.clone.back_ref) | copy-start | bytes 345604
  80.1 9.3 %collective-permute-start.7 = (f32[32,128]{1,0:T(8,128)S(1)}, f32[32,128]{1,0:T(8,128)S(1)}, u32[]{:S(2)}, u32[]{:S(2)}) collective-permute-start(f32[32,128]{1,0:T(8,128)S(1)} %get-tuple-element.52), channel_id=1, source_target_pairs={{0,12},{12,0},{24,36},{36,24},{48,60},{60,48},{72,84},{84,72},{96,... | collective-permute-start | bytes 49160 | tf_op jit(solution)/shard_map/ppermute | solution.py:688
  84.0 7.2 %collective-permute-start.8 = (f32[32,128]{1,0:T(8,128)S(1)}, f32[32,128]{1,0:T(8,128)S(1)}, u32[]{:S(2)}, u32[]{:S(2)}) collective-permute-start(f32[32,128]{1,0:T(8,128)S(1)} %get-tuple-element.53), channel_id=1, source_target_pairs={{12,24},{24,12},{36,48},{48,36},{60,72},{72,60},{84,96},{96,84},{1... | collective-permute-start | bytes 49160 | tf_op jit(solution)/shard_map/ppermute | solution.py:688
  92.1 7.2 %collective-permute-start.9 = (f32[32,128]{1,0:T(8,128)S(1)}, f32[32,128]{1,0:T(8,128)S(1)}, u32[]{:S(2)}, u32[]{:S(2)}) collective-permute-start(f32[32,128]{1,0:T(8,128)S(1)} %get-tuple-element.56), channel_id=1, source_target_pairs={{12,0},{24,12},{36,24},{48,36},{60,48},{72,60},{84,72},{96,84},{10... | collective-permute-start | bytes 49160 | tf_op jit(solution)/shard_map/ppermute | solution.py:716
  94.1 5.2 %copy-start.10 = (bf16[128,454]{1,0:T(8,128)(2,1)S(1)}, bf16[128,454]{1,0:T(8,128)(2,1)}, u32[]{:S(2)}) copy-start(bf16[128,454]{1,0:T(8,128)(2,1)} %constant.73.clone.face_back_ref) | copy-start | bytes 348676
  94.1 5.2 %copy-start.17 = (f32[16,454]{1,0:T(8,128)S(1)}, f32[16,454]{1,0:T(8,128)}, u32[]{:S(2)}) copy-start(f32[16,454]{1,0:T(8,128)} %constant.70.clone.face_mask_ref) | copy-start | bytes 87172
  (11 other events, 15.8 us)

commit v3 on v2

--- a/solution.py
+++ b/solution.py
@@ -8,6 +8,7 @@
 from jax.experimental import pallas as pl
 from jax.experimental.pallas import tpu as pltpu
 from jax.sharding import PartitionSpec as P
+
 
 EY = 8
 EZ = 6
@@ -148,19 +149,16 @@
     flat = np.arange(450)
     py, pz = flat // 18, flat % 18
     lane = 9 * ((pz + 1) // 3) + py // 3
-    mask = np.zeros((4, ROWS, 450), np.float32)
     own = np.zeros((ROWS, 128), np.float32)
     face_mask = np.zeros((16, 454), np.float32)
     for a in range(4):
         for k in range(450):
             b, c = py[k] % 3, (pz[k] + 1) % 3
             row = node_row(a, b, c)
-            mask[a, row, k] = 1.0
             if a > 0:
                 own[row, lane[k] + LANE_OWN] = 1.0
             else:
                 face_mask[face_row(b, c), k + 4] = 1.0
-    out["mask"] = mask.reshape(4 * ROWS, 450)
     out["own"] = own
     out["face_mask"] = face_mask
     pick = np.zeros((450, 128), np.float32)
@@ -320,23 +318,25 @@
     return flags_ref[row : row + 1, 0:1]
 
 
-def is_even(flags_ref):
-    return jnp.broadcast_to(flag(flags_ref, 0), (32, 128)) > 0.5
+def is_even(flags_ref, row, shape):
+    place = flag(flags_ref, row)
+    rest = place - 2.0 * jnp.floor(place * 0.5)
+    return jnp.broadcast_to(rest, shape) < 0.5
 
 
 def send_faces(nodes, flags_ref, first_ref, second_ref):
-    even = is_even(flags_ref)
+    even = is_even(flags_ref, 0, (32, 128))
     low, high = face_of(nodes, 0), face_of(nodes, 3)
     first_ref[...] = jnp.where(even, high, low)
     second_ref[...] = jnp.where(even, low, high)
 
 
 def shared_sum(nodes, flags_ref, first_ref, second_ref, off_x_ref, off_z_ref):
-    even = is_even(flags_ref)
+    even = is_even(flags_ref, 0, (32, 128))
     first, second = first_ref[...], second_ref[...]
     total = add_faces(nodes, jnp.where(even, second, first), jnp.where(even, first, second))
-    wall = jnp.maximum(off_x_ref[...], flag(flags_ref, 1)) * jnp.maximum(
-        off_z_ref[...], flag(flags_ref, 2)
+    wall = jnp.minimum(off_x_ref[...] + flag(flags_ref, 0), 1.0) * jnp.minimum(
+        off_z_ref[...] + flag(flags_ref, 1), 1.0
     )
     return total * jnp.concatenate([wall, wall, wall], axis=0)
 
@@ -366,41 +366,79 @@
     return [[g[c][m] + 1.0 if c == m else g[c][m] for m in range(3)] for c in range(3)]
 
 
+def add_packed(value, out_ref, at):
+    half = value.shape[0] // 2
+    out_ref[at : at + half, :] = value[:half] + rolled(value[half:], 64)
+
+
+def plane_index(width):
+    row = lax.broadcasted_iota(jnp.int32, (ROWS, width), 0)
+    return jnp.where(
+        row < 8,
+        row // 2,
+        jnp.where(
+            row < 16,
+            (row - 8) // 2,
+            jnp.where(row < 32, (row - 16) // 4, jnp.where(row < 36, row - 32, 9)),
+        ),
+    )
+
+
+def node_mask():
+    row = lax.broadcasted_iota(jnp.int32, (ROWS, 450), 0)
+    odd = row & 1
+    row_code = jnp.where(
+        row < 8,
+        odd + 1,
+        jnp.where(
+            row < 16,
+            3 * odd + 3,
+            jnp.where(row < 32, 3 * ((row >> 1) & 1) + odd + 4, jnp.where(row < 36, 0, 99)),
+        ),
+    )
+    flat = lax.broadcasted_iota(jnp.int32, (ROWS, 450), 1)
+    y = (flat * 3641) >> 16
+    z = flat - 18 * y + 1
+    code = 3 * (y - 3 * ((y * 86) >> 8)) + z - 3 * ((z * 86) >> 8)
+    return row_code == code
+
+
 def last_kernel(disp_ref, vel_ref, out_ref):
     out_ref[0:3, :] = disp_ref[:, 900:1350]
     out_ref[3:6, :] = vel_ref[:, 900:1350]
 
 
-def add_packed(value, out_ref, at):
-    half = value.shape[0] // 2
-    out_ref[at : at + half, :] = value[:half] + rolled(value[half:], 64)
-
-
-def pack_kernel(disp_ref, vel_ref, dens_ref, energy_ref, live_ref, mask_ref, pick_ref, place_ref,
-                out_ref):
-    masks = [mask_ref[ROWS * a : ROWS * a + ROWS] for a in range(1, 4)]
+def pack_kernel(disp_ref, vel_ref, dens_ref, energy_ref, live_ref, pick_ref, place_ref, out_ref):
+    plane = plane_index(450)
+    mask = node_mask() & (plane >= 1)
     blocks = []
     for ref in (disp_ref, vel_ref):
         planes = [ref[:, 450 * x : 450 * x + 450] for x in range(3)]
         for comp in range(3):
+            first, second, third = (jnp.broadcast_to(p[comp : comp + 1], (ROWS, 450)) for p in planes)
             blocks.append(
-                sum(masks[x] * planes[x][comp : comp + 1, :] for x in range(3))
+                jnp.where(
+                    mask, jnp.where(plane == 1, first, jnp.where(plane == 2, second, third)), 0.0
+                )
             )
     add_packed(exact_dot(jnp.concatenate(blocks, axis=0), pick_ref[...]), out_ref, 0)
     row = lax.broadcasted_iota(jnp.int32, (8, 48), 0)
     tail = jnp.pad(energy_ref[24:27], ((0, 5), (0, 0)))
     tail = jnp.where(row == 3, live_ref[...].astype(F32), tail)
-    values = jnp.concatenate(
-        [dens_ref[0:120], jnp.pad(dens_ref[120:125], ((0, 3), (0, 0))), energy_ref[0:24], tail], axis=0
-    )
-    placed = exact_dot(values, place_ref[...])
+    density = jnp.pad(dens_ref[...], ((0, 0), (0, 3))).T
+    placed = exact_dot(
+        jnp.concatenate([density, energy_ref[0:24], tail], axis=0), place_ref[...]
+    )
     add_packed(placed[0:128], out_ref, 120)
     add_packed(placed[128:160], out_ref, 184)
 
 
-def halo_kernel(packed_ref, halo_ref, mask_ref, pick_ref, out_ref):
-    mask = mask_ref[0:ROWS]
-    blocks = [mask * halo_ref[comp : comp + 1, :] for comp in range(6)]
+def halo_kernel(packed_ref, halo_ref, pick_ref, out_ref):
+    mask = node_mask() & (plane_index(450) == 0)
+    blocks = [
+        jnp.where(mask, jnp.broadcast_to(halo_ref[comp : comp + 1, :], (ROWS, 450)), 0.0)
+        for comp in range(6)
+    ]
     nodes = exact_dot(jnp.concatenate(blocks, axis=0), pick_ref[...])
     out_ref[0:120, :] = packed_ref[0:120, :] + (nodes[:120] + rolled(nodes[120:], 64))
     out_ref[120:200, :] = packed_ref[120:200, :]
@@ -422,14 +460,18 @@
     return window(0), window(64)
 
 
-def force_kernel(own_ref, below_ref, above_ref, grad_ref, grad_t_ref, psi_ref, weight_ref,
+def force_kernel(own_ref, first_ref, second_ref, grad_ref, grad_t_ref, psi_ref, weight_ref,
                  flags_ref, force_ref, face1_ref, face2_ref, disp_ref, vel_ref, mass_ref, live_ref,
                  power_ref, wdens_ref, g_ref, flux_ref, point_ref):
-    disp, vel = unpack(own_ref[0:120], below_ref[0:120], above_ref[0:120])
+    even = is_even(flags_ref, 1, (200, 128))
+    first, second = first_ref[...], second_ref[...]
+    below = jnp.where(even, second, first)
+    above = jnp.where(even, first, second)
+    disp, vel = unpack(own_ref[0:120], below[0:120], above[0:120])
     disp_ref[...] = disp
     vel_ref[...] = vel
-    dens_low, dens_high = unpack(own_ref[120:184], below_ref[120:184], above_ref[120:184])
-    energy_low, energy_high = unpack(own_ref[184:200], below_ref[184:200], above_ref[184:200])
+    dens_low, dens_high = unpack(own_ref[120:184], below[120:184], above[120:184])
+    energy_low, energy_high = unpack(own_ref[184:200], below[184:200], above[184:200])
     energy = jnp.concatenate([energy_low, energy_high], axis=0)
     lane = lax.broadcasted_iota(jnp.int32, (1, 128), 1)
     live = jnp.where(lane < 9 * WINDOW, energy[27:28], 0.0)
@@ -578,7 +620,7 @@
     beta = rest / mu0
     gain = 1.0 + beta
     second = rest / (gain * gain * mu1 - 2.0 * gain * alpha * mu2 + alpha * alpha * mu3)
-    step = flag(flags_ref, 3)
+    step = flag(flags_ref, 2)
     newvel = vel_ref[...] + step * (
         (alpha + second * gain) * resid_ref[...] - (alpha * second) * image_ref[...]
     )
@@ -597,22 +639,21 @@
     u = moved_ref[...] - MESH_STEP * gradient
     part = shape_forces(u, live_ref[...], grad_ref, grad_t_ref, weight_ref, g_ref, flux_ref)
     face_ref[...] = face_of(part, 0)
-    base_ref[...] = newvel_ref[...] - (MESH_STEP / flag(flags_ref, 3)) * (gradient + part)
-
-
-def write_kernel(nodes_ref, mask_ref, back_ref, out_ref):
+    base_ref[...] = newvel_ref[...] - (MESH_STEP / flag(flags_ref, 2)) * (gradient + part)
+
+
+def write_kernel(nodes_ref, back_ref, out_ref):
     wide = exact_dot(nodes_ref[...], back_ref[...])
+    plane = plane_index(450)
+    masks = [node_mask() & (plane == a) for a in range(1, 4)]
     for comp in range(3):
         part = wide[ROWS * comp : ROWS * comp + ROWS]
-        planes = [
-            jnp.sum(part * mask_ref[ROWS * a : ROWS * a + ROWS], axis=0, keepdims=True)
-            for a in range(1, 4)
-        ]
+        planes = [jnp.sum(jnp.where(mask, part, 0.0), axis=0, keepdims=True) for mask in masks]
         out_ref[comp : comp + 1, :] = jnp.concatenate(planes, axis=1)
 
 
 def mesh_kernel(base_ref, face_ref, flags_ref, face_mask_ref, face_back_ref, out_ref):
-    scale = -MESH_STEP / flag(flags_ref, 3)
+    scale = -MESH_STEP / flag(flags_ref, 2)
     wide = exact_dot(face_ref[...], face_back_ref[...])
     mask = face_mask_ref[0:8]
     corner = face_mask_ref[8:9]
@@ -623,17 +664,40 @@
         out_ref[comp : comp + 1, 896:1350] = base_ref[comp : comp + 1, 896:1350] + scale * extra
 
 
-def call(kernel, name, outs, scratch=(), flops=1_000_000):
+def copying(kernel, count):
+    def run(*refs):
+        sources, outs = refs[:count], refs[count : -count - 1]
+        copies, sems = refs[-count - 1 : -1], refs[-1]
+        moves = [
+            pltpu.make_async_copy(source, target, sems.at[i])
+            for i, (source, target) in enumerate(zip(sources, copies))
+        ]
+        for move in moves:
+            move.start()
+        for move in moves:
+            move.wait()
+        kernel(*copies, *outs)
+
+    return run
+
+
+def call(kernel, outs, scratch=(), flops=1_000_000, copied=False):
     spec = pl.BlockSpec(memory_space=pltpu.VMEM)
 
     def run(*args):
+        given, body_of = spec, kernel
+        extra = [pltpu.VMEM(shape, F32) for shape in scratch]
+        if copied:
+            given, body_of = pl.BlockSpec(memory_space=pltpu.HBM), copying(kernel, len(args))
+            extra = [pltpu.VMEM(arg.shape, arg.dtype) for arg in args]
+            extra.append(pltpu.SemaphoreType.DMA((len(args),)))
+            args = [pltpu.with_memory_space_constraint(arg, pltpu.HBM) for arg in args]
         return pl.pallas_call(
-            kernel,
+            body_of,
             out_shape=[jax.ShapeDtypeStruct(shape, F32) for shape in outs],
-            in_specs=[spec] * len(args),
+            in_specs=[given] * len(args),
             out_specs=[spec] * len(outs),
-            scratch_shapes=[pltpu.VMEM(shape, F32) for shape in scratch],
-            name=name,
+            scratch_shapes=extra,
             compiler_params=pltpu.CompilerParams(vmem_limit_bytes=16 * 1024 * 1024),
             cost_estimate=pl.CostEstimate(flops=flops, bytes_accessed=400_000, transcendentals=0),
         )(*args)
@@ -652,70 +716,62 @@
     dom, sub = lax.axis_index("dom"), lax.axis_index("sub")
     up = [(i, i + 1) for i in range(n_dom - 1)]
     down = [(i + 1, i) for i in range(n_dom - 1)]
-    pairs_first = [p for i in range(0, n_dom - 1, 2) for p in ((i, i + 1), (i + 1, i))]
-    pairs_second = [p for i in range(1, n_dom - 1, 2) for p in ((i, i + 1), (i + 1, i))]
-    z_up = [(i, i + 1) for i in range(n_sub - 1)]
-    z_down = [(i + 1, i) for i in range(n_sub - 1)]
+
+    def pairs(start, size):
+        return [p for i in range(start, size - 1, 2) for p in ((i, i + 1), (i + 1, i))]
 
     row = lax.broadcasted_iota(jnp.int32, (8, 128), 0)
     flags = jnp.where(
-        row == 0,
-        (1 - dom % 2).astype(F32),
-        jnp.where(
-            row == 1,
-            jnp.minimum(dom, 1).astype(F32),
-            jnp.where(row == 2, jnp.minimum(sub, 1).astype(F32), time_step),
-        ),
+        row == 0, dom.astype(F32), jnp.where(row == 1, sub.astype(F32), time_step)
     )
     walls = (table["off_x"], table["off_z"])
 
-    (last,) = call(last_kernel, "last", [(6, 450)])(displacement, velocity)
+    (last,) = call(last_kernel, [(6, 450)], copied=True)(displacement, velocity)
     halo = lax.ppermute(last, "dom", up)
-    (packed,) = call(pack_kernel, "pack", [(200, 128)])(
-        displacement, velocity, mass_density, energy, live_mask.reshape(1, 48), table["mask"],
-        table["pick"], table["place"],
-    )
-    (own,) = call(halo_kernel, "halo", [(200, 128)])(packed, halo, table["mask"], table["pick"])
-    below = lax.ppermute(own, "sub", z_up)
-    above = lax.ppermute(own, "sub", z_down)
+    (packed,) = call(pack_kernel, [(200, 128)], copied=True)(
+        displacement, velocity, mass_density.T, energy, live_mask.reshape(1, 48), table["pick"],
+        table["place"],
+    )
+    (own,) = call(halo_kernel, [(200, 128)])(packed, halo, table["pick"])
+    below = lax.ppermute(own, "sub", pairs(0, n_sub))
+    above = lax.ppermute(own, "sub", pairs(1, n_sub))
     force, face1, face2, disp, vel, mass, live, power, wdens = call(
-        force_kernel, "force",
+        force_kernel,
         [NODES, FACE, FACE, NODES, NODES, POINTS, (8, 128), POINTS, POINTS],
         [(384, 768), (384, 384), POINTS],
     )(own, below, above, table["grad"], table["grad_t"], table["psi"], table["weight"], flags)
 
     def swap(face1, face2):
-        return lax.ppermute(face1, "dom", pairs_first), lax.ppermute(face2, "dom", pairs_second)
+        second = lax.ppermute(face2, "dom", pairs(1, n_dom))
+        return lax.ppermute(face1, "dom", pairs(0, n_dom)), second
 
     first, second = swap(face1, face2)
-    (energy_rate,) = call(energy_kernel, "energy", [(27, 48)])(
-        power, wdens, table["psi_t"], table["take"]
-    )
+    (energy_rate,) = call(energy_kernel, [(27, 48)])(power, wdens, table["psi_t"], table["take"])
     force, energy_rate = lax.optimization_barrier((force, energy_rate))
     resid, image_part, face1, face2, sums = call(
-        mass_kernel, "mass", [NODES, NODES, FACE, FACE, (8, 128)]
+        mass_kernel, [NODES, NODES, FACE, FACE, (8, 128)]
     )(force, first, second, flags, *walls, mass, table["phi"], table["phi_t"], table["own"],
       table["own_element"])
     first, second = swap(face1, face2)
-    image, local = call(moment_kernel, "moment", [NODES, (n_dom, 128)])(
+    image, local = call(moment_kernel, [NODES, (n_dom, 128)])(
         image_part, first, second, flags, *walls, mass, table["phi"], table["own"],
         table["own_element"], sums,
     )
     slab = jnp.sum(lax.all_to_all(local, "dom", 0, 0, tiled=True), axis=0, keepdims=True)
     moments = lax.all_to_all(jnp.broadcast_to(slab, (n_sub, 128)), "sub", 0, 0, tiled=True)
     newvel, moved, part, face1, face2 = call(
-        first_shape_kernel, "shape1", [NODES, NODES, NODES, FACE, FACE], [(384, 384), (384, 384)]
+        first_shape_kernel, [NODES, NODES, NODES, FACE, FACE], [(384, 384), (384, 384)]
     )(moments, disp, vel, resid, image, live, flags, table["grad"], table["grad_t"], table["weight"])
     first, second = swap(face1, face2)
-    (new_velocity,) = call(write_kernel, "newvel", [(3, 1350)])(newvel, table["mask"], table["back"])
+    (new_velocity,) = call(write_kernel, [(3, 1350)])(newvel, table["back"])
     part, new_velocity = lax.optimization_barrier((part, new_velocity))
     base, face = call(
-        second_shape_kernel, "shape2", [NODES, FACE], [(384, 384), (384, 384)]
+        second_shape_kernel, [NODES, FACE], [(384, 384), (384, 384)]
     )(part, first, second, flags, *walls, newvel, moved, live, table["grad"], table["grad_t"],
       table["weight"])
     from_above = lax.ppermute(face, "dom", down)
-    (mesh_base,) = call(write_kernel, "base", [(3, 1350)])(base, table["mask"], table["back"])
-    (mesh_velocity,) = call(mesh_kernel, "mesh", [(3, 1350)])(
+    (mesh_base,) = call(write_kernel, [(3, 1350)])(base, table["back"])
+    (mesh_velocity,) = call(mesh_kernel, [(3, 1350)])(
         mesh_base, from_above, flags, table["face_mask"], table["face_back"]
     )
     return new_velocity, energy_rate, mesh_velocity
@@ -723,6 +779,7 @@
 
 def solution(mesh):
     both = ("dom", "sub")
+
     return jax.shard_map(
         body,
         mesh=mesh,

time: 101 us -> 99.3 us (0.983)
  starting transfers between devices: 29.6 us -> 34.1 us
  local copies, waits for them, and re-layouts: 4.46 us -> 0.11 us
  Pallas kernels: 8.11 us -> 10.2 us
  blocking collectives: 39.8 us -> 37.8 us
  waiting for transfers between devices: 16.3 us -> 14.7 us
    ppermute x8, starting transfers between devices: 24.8 us -> 29.1 us  [the longest x3 12.2 us: swap(): second = lax.ppermute(face2, 'dom', pairs(1, n_dom))]
    unnamed x52 -> x33, local copies, waits for them, and re-layouts: 4.45 us -> 0.1 us
    all_to_all x1, blocking collectives: 25.2 us -> 22.4 us  [body(): lax.all_to_all(jnp.broadcast_to(slab, (n_sub, 128)), 'sub', 0, 0, tiled=T...]
    pallas_call x12, Pallas kernels: 8.11 us -> 10.2 us  [run(): pl.pallas_call(body_of, out_shape=[jax.ShapeDtypeStruct(shape, F32) for s...]
    ppermute x8, waiting for transfers between devices: 11.4 us -> 9.86 us  [the longest x3 7.25 us: swap(): second = lax.ppermute(face2, 'dom', pairs(1, n_dom))]
  transfers between devices with their start and end apart: 10 -> 10, of which waited for: 6 -> 5; matrix products, arithmetic and copies ran while one was open for 1% -> 0% of each run, Pallas kernels for 3% -> 4%
where the time goes in v3:
time: 99.3 us; the launch traced here: 98.8 us
  blocking collectives  37.8 us (38%)
  starting transfers between devices  34.1 us (34%)
  waiting for transfers between devices  14.7 us (15%)
  Pallas kernels  10.2 us (10%)
  between operations  1.66 us (2%)
    all_to_all x1, blocking collectives, body(): lax.all_to_all(jnp.broadcast_to(slab, (n_sub, 128)), 'sub', 0, 0, tiled=T...  22.4 us
    all_to_all x1, blocking collectives, body(): lax.all_to_all(local, 'dom', 0, 0, tiled=True)  15.5 us
    ppermute x3, starting transfers between devices, swap(): second = lax.ppermute(face2, 'dom', pairs(1, n_dom))  12.2 us
    pallas_call x12, Pallas kernels, run(): pl.pallas_call(body_of, out_shape=[jax.ShapeDtypeStruct(shape, F32) for s...  10.2 us
    ppermute x3, starting transfers between devices, swap(): return (lax.ppermute(face1, 'dom', pairs(0, n_dom)), second)  8.96 us
    ppermute x1, starting transfers between devices, body(): below = lax.ppermute(own, 'sub', pairs(0, n_sub))  7.33 us
    ppermute x3, waiting for transfers between devices, swap(): second = lax.ppermute(face2, 'dom', pairs(1, n_dom))  7.25 us
    ppermute x1, waiting for transfers between devices, body(): from_above = lax.ppermute(face, 'dom', down)  4.83 us
  transfers between devices with their start and end apart: 10, of which 5 were waited for; matrix products, arithmetic and copies ran while one was open for 0% of the time, Pallas kernels for 4%

profile of v3, /device:TPU:57, one launch (start us, length us, event | category | flops | bytes accessed | tf_op | source)
XLA Modules:
  0.0 98.8 jit_solution(272769599132500157)
XLA Ops:
  0.6 0.8 shard_map.239
  1.5 2.9 %collective-permute-start = (f32[6,450]{1,0:T(8,128)S(1)}, f32[6,450]{1,0:T(8,128)S(1)}, u32[]{:S(2)}, u32[]{:S(2)}) collective-permute-start(f32[6,450]{1,0:T(8,128)S(1)} %shard_map.239), channel_id=1, source_target_pairs={{0,12},{12,24},{24,36},{36,48},{48,60},{60,72},{72,84},{84,96},{96... | collective-permute-start | bytes 32408 | tf_op jit(solution)/shard_map/ppermute | solution.py:730
  5.1 1.8 %shard_map.238.packed_ref = f32[200,128]{1,0:T(8,128)S(1)} custom-call(f32[3,1350]{1,0:T(4,128)} %refs_0_.3, f32[3,1350]{1,0:T(4,128)} %refs_1_.3, f32[48,125]{1,0:T(8,128)} %bitcast.10, f32[27,48]{1,0:T(8,128)} %refs_3_.1, s32[1,48]{1,0:T(1,128)} %bitcast.11, bf16[450,128]{1,0:T(8,128)(2,1)} %constant.55.clone.refs_5_.pick_ref, ...), custom_call_target="tpu_custom_call" | custom-call | flops 1000000 | bytes 400000 | tf_op jit(solution)/shard_map/pallas_call | solution.py:695
  8.0 7.3 %collective-permute-start.1 = (f32[200,128]{1,0:T(8,128)S(1)}, f32[200,128]{1,0:T(8,128)S(1)}, u32[]{:S(2)}, u32[]{:S(2)}) collective-permute-start(f32[200,128]{1,0:T(8,128)S(1)} %shard_map.240.own_ref), channel_id=1, source_target_pairs={{0,1},{1,0},{2,3},{3,2},{4,5},{5,4},{6,7},{7,6},{8,9},{9,8},{10,11... | collective-permute-start | bytes 307208 | tf_op jit(solution)/shard_map/ppermute | solution.py:736
  15.5 2.6 %collective-permute-done.1.first_ref = f32[200,128]{1,0:T(8,128)S(1)} collective-permute-done((f32[200,128]{1,0:T(8,128)S(1)}, f32[200,128]{1,0:T(8,128)S(1)}, u32[]{:S(2)}, u32[]{:S(2)}) %collective-permute-start.1) | collective-permute-done | bytes 102432 | tf_op jit(solution)/shard_map/ppermute | solution.py:736
  18.1 1.2 %shard_map.241 = (f32[120,128]{1,0:T(8,128)S(1)}, f32[32,128]{1,0:T(8,128)S(1)}, f32[32,128]{1,0:T(8,128)S(1)}, f32[120,128]{1,0:T(8,128)S(1)}, f32[120,128]{1,0...) custom-call(f32[200,128]{1,0:T(8,128)S(1)} %shard_map.240.own_ref, ...), custom_call_target="tpu_custom_call" | custom-call | flops 1000000 | bytes 400000 | tf_op jit(solution)/shard_map/pallas_call | solution.py:695
  19.3 3.0 %collective-permute-start.3 = (f32[32,128]{1,0:T(8,128)S(1)}, f32[32,128]{1,0:T(8,128)S(1)}, u32[]{:S(2)}, u32[]{:S(2)}) collective-permute-start(f32[32,128]{1,0:T(8,128)S(1)} %get-tuple-element.34), channel_id=1, source_target_pairs={{0,12},{12,0},{24,36},{36,24},{48,60},{60,48},{72,84},{84,72},{96,... | collective-permute-start | bytes 49160 | tf_op jit(solution)/shard_map/ppermute | solution.py:746
  22.3 4.0 %collective-permute-start.4 = (f32[32,128]{1,0:T(8,128)S(1)}, f32[32,128]{1,0:T(8,128)S(1)}, u32[]{:S(2)}, u32[]{:S(2)}) collective-permute-start(f32[32,128]{1,0:T(8,128)S(1)} %get-tuple-element.35), channel_id=1, source_target_pairs={{12,24},{24,12},{36,48},{48,36},{60,72},{72,60},{84,96},{96,84},{1... | collective-permute-start | bytes 49160 | tf_op jit(solution)/shard_map/ppermute | solution.py:745
  26.4 0.9 shard_map.242
  27.3 2.2 %collective-permute-done.4.second_ref = f32[32,128]{1,0:T(8,128)S(1)} collective-permute-done((f32[32,128]{1,0:T(8,128)S(1)}, f32[32,128]{1,0:T(8,128)S(1)}, u32[]{:S(2)}, u32[]{:S(2)}) %collective-permute-start.4) | collective-permute-done | bytes 16416 | tf_op jit(solution)/shard_map/ppermute | solution.py:745
  30.1 1.9 %collective-permute-start.5 = (f32[32,128]{1,0:T(8,128)S(1)}, f32[32,128]{1,0:T(8,128)S(1)}, u32[]{:S(2)}, u32[]{:S(2)}) collective-permute-start(f32[32,128]{1,0:T(8,128)S(1)} %get-tuple-element.38), channel_id=1, source_target_pairs={{0,12},{12,0},{24,36},{36,24},{48,60},{60,48},{72,84},{84,72},{96,... | collective-permute-start | bytes 49160 | tf_op jit(solution)/shard_map/ppermute | solution.py:746
  32.1 4.0 %collective-permute-start.6 = (f32[32,128]{1,0:T(8,128)S(1)}, f32[32,128]{1,0:T(8,128)S(1)}, u32[]{:S(2)}, u32[]{:S(2)}) collective-permute-start(f32[32,128]{1,0:T(8,128)S(1)} %get-tuple-element.39), channel_id=1, source_target_pairs={{12,24},{24,12},{36,48},{48,36},{60,72},{72,60},{84,96},{96,84},{1... | collective-permute-start | bytes 49160 | tf_op jit(solution)/shard_map/ppermute | solution.py:745
  36.0 3.2 %collective-permute-done.6.second_ref = f32[32,128]{1,0:T(8,128)S(1)} collective-permute-done((f32[32,128]{1,0:T(8,128)S(1)}, f32[32,128]{1,0:T(8,128)S(1)}, u32[]{:S(2)}, u32[]{:S(2)}) %collective-permute-start.6) | collective-permute-done | bytes 16416 | tf_op jit(solution)/shard_map/ppermute | solution.py:745
  39.6 15.5 %all_to_all.17 = f32[64,1,128]{2,1,0:T(1,128)S(1)} all-to-all(f32[64,1,128]{2,1,0:T(1,128)S(1)} %bitcast.9), channel_id=1, replica_groups=mesh['dom'=64,'sub'=12] {'dom'}, dimensions={0} | all-to-all | bytes 65536 | tf_op jit(solution)/shard_map/all_to_all | solution.py:760
  55.2 22.4 %all_to_all.18 = f32[12,1,128]{2,1,0:T(1,128)S(1)} all-to-all(f32[12,1,128]{2,1,0:T(1,128)S(1)} %broadcast_in_dim.21), channel_id=1, replica_groups=mesh['dom'=64,'sub'=12] {'sub'}, dimensions={0} | all-to-all | bytes 12288 | tf_op jit(solution)/shard_map/all_to_all | solution.py:761
  77.6 1.0 %shard_map.245 = (f32[120,128]{1,0:T(8,128)S(1)}, f32[120,128]{1,0:T(8,128)S(1)}, f32[120,128]{1,0:T(8,128)S(1)}, f32[32,128]{1,0:T(8,128)S(1)}, f32[32,128]{1,0:T(8,128)S(1)}) custom-call(f32[12,128]{1,0:T(8,128)S(1)} %bitcast.8, f32[120,128]{1,0:T(8,128)S(1)} %get-tuple-element.42.disp_ref, f32[120,128]{1,0:T(8,128)S(1)} %get-tuple-element.43.vel_ref, ...), custom_call_target="tpu_custom_call" | custom-call | flops 1000000 | bytes 400000 | tf_op jit(solution)/shard_map/pallas_call | solution.py:695
  78.6 4.0 %collective-permute-start.7 = (f32[32,128]{1,0:T(8,128)S(1)}, f32[32,128]{1,0:T(8,128)S(1)}, u32[]{:S(2)}, u32[]{:S(2)}) collective-permute-start(f32[32,128]{1,0:T(8,128)S(1)} %get-tuple-element.52), channel_id=1, source_target_pairs={{0,12},{12,0},{24,36},{36,24},{48,60},{60,48},{72,84},{84,72},{96,... | collective-permute-start | bytes 49160 | tf_op jit(solution)/shard_map/ppermute | solution.py:746
  82.6 4.2 %collective-permute-start.8 = (f32[32,128]{1,0:T(8,128)S(1)}, f32[32,128]{1,0:T(8,128)S(1)}, u32[]{:S(2)}, u32[]{:S(2)}) collective-permute-start(f32[32,128]{1,0:T(8,128)S(1)} %get-tuple-element.53), channel_id=1, source_target_pairs={{12,24},{24,12},{36,48},{48,36},{60,72},{72,60},{84,96},{96,84},{1... | collective-permute-start | bytes 49160 | tf_op jit(solution)/shard_map/ppermute | solution.py:745
  86.8 1.0 %shard_map.246 = f32[3,1350]{1,0:T(4,128)} custom-call(f32[120,128]{1,0:T(8,128)S(1)} %get-tuple-element.48.nodes_ref.newvel_ref, bf16[128,450]{1,0:T(8,128)(2,1)S(1)} %copy-done.3), custom_call_target="tpu_custom_call" | custom-call | flops 1000000 | bytes 400000 | tf_op jit(solution)/shard_map/pallas_call | solution.py:695
  87.8 1.9 %collective-permute-done.8.second_ref = f32[32,128]{1,0:T(8,128)S(1)} collective-permute-done((f32[32,128]{1,0:T(8,128)S(1)}, f32[32,128]{1,0:T(8,128)S(1)}, u32[]{:S(2)}, u32[]{:S(2)}) %collective-permute-start.8) | collective-permute-done | bytes 16416 | tf_op jit(solution)/shard_map/ppermute | solution.py:745
  89.7 0.9 shard_map.247
  90.7 2.1 %collective-permute-start.9 = (f32[32,128]{1,0:T(8,128)S(1)}, f32[32,128]{1,0:T(8,128)S(1)}, u32[]{:S(2)}, u32[]{:S(2)}) collective-permute-start(f32[32,128]{1,0:T(8,128)S(1)} %get-tuple-element.56), channel_id=1, source_target_pairs={{12,0},{24,12},{36,24},{48,36},{60,48},{72,60},{84,72},{96,84},{10... | collective-permute-start | bytes 49160 | tf_op jit(solution)/shard_map/ppermute | solution.py:772
  93.1 4.8 %collective-permute-done.9.face_ref = f32[32,128]{1,0:T(8,128)S(1)} collective-permute-done((f32[32,128]{1,0:T(8,128)S(1)}, f32[32,128]{1,0:T(8,128)S(1)}, u32[]{:S(2)}, u32[]{:S(2)}) %collective-permute-start.9) | collective-permute-done | bytes 16416 | tf_op jit(solution)/shard_map/ppermute | solution.py:772
  98.0 0.8 shard_map.249
  (48 shorter events, 2.8 us)
Async XLA Ops:
  1.5 5.4 %collective-permute-start = (f32[6,450]{1,0:T(8,128)S(1)}, f32[6,450]{1,0:T(8,128)S(1)}, u32[]{:S(2)}, u32[]{:S(2)}) collective-permute-start(f32[6,450]{1,0:T(8,128)S(1)} %shard_map.239), channel_id=1, source_target_pairs={{0,12},{12,24},{24,36},{36,48},{48,60},{60,72},{72,84},{84,96},{96... | collective-permute-start | bytes 32408 | tf_op jit(solution)/shard_map/ppermute | solution.py:730
  5.1 13.0 %copy-start.2 = (f32[128,128]{1,0:T(8,128)S(1)}, f32[128,128]{1,0:T(8,128)}, u32[]{:S(2)}) copy-start(f32[128,128]{1,0:T(8,128)} %constant.52.clone.weight_ref) | copy-start | bytes 196612
  5.1 13.0 %copy-start.12 = (bf16[128,96]{1,0:T(8,128)(2,1)S(1)}, bf16[128,96]{1,0:T(8,128)(2,1)}, u32[]{:S(2)}) copy-start(bf16[128,96]{1,0:T(8,128)(2,1)} %constant.50.clone.psi_ref) | copy-start | bytes 73732
  6.9 11.2 %copy-start = (bf16[384,240]{1,0:T(8,128)(2,1)S(1)}, bf16[384,240]{1,0:T(8,128)(2,1)}, u32[]{:S(2)}) copy-start(bf16[384,240]{1,0:T(8,128)(2,1)} %constant.46.clone.grad_ref) | copy-start | bytes 552964
  6.9 11.2 %copy-start.1 = (bf16[160,384]{1,0:T(8,128)(2,1)S(1)}, bf16[160,384]{1,0:T(8,128)(2,1)}, u32[]{:S(2)}) copy-start(bf16[160,384]{1,0:T(8,128)(2,1)} %constant.47.clone.grad_t_ref) | copy-start | bytes 368644
  7.4 8.1 %collective-permute-start.2 = (f32[200,128]{1,0:T(8,128)S(1)}, f32[200,128]{1,0:T(8,128)S(1)}, u32[]{:S(2)}, u32[]{:S(2)}) collective-permute-start(f32[200,128]{1,0:T(8,128)S(1)} %shard_map.240.own_ref), channel_id=1, source_target_pairs={{1,2},{2,1},{3,4},{4,3},{5,6},{6,5},{7,8},{8,7},{9,10},{10,9},{13,... | collective-permute-start | bytes 307208 | tf_op jit(solution)/shard_map/ppermute | solution.py:737
  8.0 10.0 %collective-permute-start.1 = (f32[200,128]{1,0:T(8,128)S(1)}, f32[200,128]{1,0:T(8,128)S(1)}, u32[]{:S(2)}, u32[]{:S(2)}) collective-permute-start(f32[200,128]{1,0:T(8,128)S(1)} %shard_map.240.own_ref), channel_id=1, source_target_pairs={{0,1},{1,0},{2,3},{3,2},{4,5},{5,4},{6,7},{7,6},{8,9},{9,8},{10,11... | collective-permute-start | bytes 307208 | tf_op jit(solution)/shard_map/ppermute | solution.py:736
  15.5 10.9 %copy-start.13 = (bf16[128,48]{1,0:T(8,128)(2,1)S(1)}, bf16[128,48]{1,0:T(8,128)(2,1)}, u32[]{:S(2)}) copy-start(bf16[128,48]{1,0:T(8,128)(2,1)} %constant.61.clone.take_ref) | copy-start | bytes 36868
  18.1 8.2 %copy-start.15 = (bf16[64,128]{1,0:T(8,128)(2,1)S(1)}, bf16[64,128]{1,0:T(8,128)(2,1)}, u32[]{:S(2)}) copy-start(bf16[64,128]{1,0:T(8,128)(2,1)} %constant.51.clone.psi_t_ref) | copy-start | bytes 49156
  19.3 8.0 %collective-permute-start.3 = (f32[32,128]{1,0:T(8,128)S(1)}, f32[32,128]{1,0:T(8,128)S(1)}, u32[]{:S(2)}, u32[]{:S(2)}) collective-permute-start(f32[32,128]{1,0:T(8,128)S(1)} %get-tuple-element.34), channel_id=1, source_target_pairs={{0,12},{12,0},{24,36},{36,24},{48,60},{60,48},{72,84},{84,72},{96,... | collective-permute-start | bytes 49160 | tf_op jit(solution)/shard_map/ppermute | solution.py:746
  22.3 7.2 %collective-permute-start.4 = (f32[32,128]{1,0:T(8,128)S(1)}, f32[32,128]{1,0:T(8,128)S(1)}, u32[]{:S(2)}, u32[]{:S(2)}) collective-permute-start(f32[32,128]{1,0:T(8,128)S(1)} %get-tuple-element.35), channel_id=1, source_target_pairs={{12,24},{24,12},{36,48},{48,36},{60,72},{72,60},{84,96},{96,84},{1... | collective-permute-start | bytes 49160 | tf_op jit(solution)/shard_map/ppermute | solution.py:745
  26.3 3.2 %copy-start.5 = (bf16[128,240]{1,0:T(8,128)(2,1)S(1)}, bf16[128,240]{1,0:T(8,128)(2,1)}, u32[]{:S(2)}) copy-start(bf16[128,240]{1,0:T(8,128)(2,1)} %constant.48.clone.phi_ref) | copy-start | bytes 184324
  26.4 3.2 %copy-start.6 = (f32[40,128]{1,0:T(8,128)S(1)}, f32[40,128]{1,0:T(8,128)}, u32[]{:S(2)}) copy-start(f32[40,128]{1,0:T(8,128)} %constant.59.clone.off_z_ref) | copy-start | bytes 61444
  26.4 3.1 %copy-start.7 = (f32[40,128]{1,0:T(8,128)S(1)}, f32[40,128]{1,0:T(8,128)}, u32[]{:S(2)}) copy-start(f32[40,128]{1,0:T(8,128)} %constant.58.clone.off_x_ref) | copy-start | bytes 61444
  26.4 3.1 %copy-start.9 = (f32[40,128]{1,0:T(8,128)S(1)}, f32[40,128]{1,0:T(8,128)}, u32[]{:S(2)}) copy-start(f32[40,128]{1,0:T(8,128)} %constant.53.clone.own_ref) | copy-start | bytes 61444
  26.4 3.1 %copy-start.10 = (bf16[160,128]{1,0:T(8,128)(2,1)S(1)}, bf16[160,128]{1,0:T(8,128)(2,1)}, u32[]{:S(2)}) copy-start(bf16[160,128]{1,0:T(8,128)(2,1)} %constant.49.clone.phi_t_ref) | copy-start | bytes 122884
  30.1 5.9 %collective-permute-start.5 = (f32[32,128]{1,0:T(8,128)S(1)}, f32[32,128]{1,0:T(8,128)S(1)}, u32[]{:S(2)}, u32[]{:S(2)}) collective-permute-start(f32[32,128]{1,0:T(8,128)S(1)} %get-tuple-element.38), channel_id=1, source_target_pairs={{0,12},{12,0},{24,36},{36,24},{48,60},{60,48},{72,84},{84,72},{96,... | collective-permute-start | bytes 49160 | tf_op jit(solution)/shard_map/ppermute | solution.py:746
  32.1 7.2 %collective-permute-start.6 = (f32[32,128]{1,0:T(8,128)S(1)}, f32[32,128]{1,0:T(8,128)S(1)}, u32[]{:S(2)}, u32[]{:S(2)}) collective-permute-start(f32[32,128]{1,0:T(8,128)S(1)} %get-tuple-element.39), channel_id=1, source_target_pairs={{12,24},{24,12},{36,48},{48,36},{60,72},{72,60},{84,96},{96,84},{1... | collective-permute-start | bytes 49160 | tf_op jit(solution)/shard_map/ppermute | solution.py:745
  77.5 9.3 %copy-start.3 = (bf16[128,450]{1,0:T(8,128)(2,1)S(1)}, bf16[128,450]{1,0:T(8,128)(2,1)}, u32[]{:S(2)}) copy-start(bf16[128,450]{1,0:T(8,128)(2,1)} %constant.56.clone.back_ref) | copy-start | bytes 345604
  78.6 9.3 %collective-permute-start.7 = (f32[32,128]{1,0:T(8,128)S(1)}, f32[32,128]{1,0:T(8,128)S(1)}, u32[]{:S(2)}, u32[]{:S(2)}) collective-permute-start(f32[32,128]{1,0:T(8,128)S(1)} %get-tuple-element.52), channel_id=1, source_target_pairs={{0,12},{12,0},{24,36},{36,24},{48,60},{60,48},{72,84},{84,72},{96,... | collective-permute-start | bytes 49160 | tf_op jit(solution)/shard_map/ppermute | solution.py:746
  82.6 7.2 %collective-permute-start.8 = (f32[32,128]{1,0:T(8,128)S(1)}, f32[32,128]{1,0:T(8,128)S(1)}, u32[]{:S(2)}, u32[]{:S(2)}) collective-permute-start(f32[32,128]{1,0:T(8,128)S(1)} %get-tuple-element.53), channel_id=1, source_target_pairs={{12,24},{24,12},{36,48},{48,36},{60,72},{72,60},{84,96},{96,84},{1... | collective-permute-start | bytes 49160 | tf_op jit(solution)/shard_map/ppermute | solution.py:745
  90.7 7.3 %copy-start.8 = (bf16[128,454]{1,0:T(8,128)(2,1)S(1)}, bf16[128,454]{1,0:T(8,128)(2,1)}, u32[]{:S(2)}) copy-start(bf16[128,454]{1,0:T(8,128)(2,1)} %constant.57.clone.face_back_ref) | copy-start | bytes 348676
  90.7 7.3 %collective-permute-start.9 = (f32[32,128]{1,0:T(8,128)S(1)}, f32[32,128]{1,0:T(8,128)S(1)}, u32[]{:S(2)}, u32[]{:S(2)}) collective-permute-start(f32[32,128]{1,0:T(8,128)S(1)} %get-tuple-element.56), channel_id=1, source_target_pairs={{12,0},{24,12},{36,24},{48,36},{60,48},{72,60},{84,72},{96,84},{10... | collective-permute-start | bytes 49160 | tf_op jit(solution)/shard_map/ppermute | solution.py:772
  92.7 5.2 %copy-start.11 = (f32[16,454]{1,0:T(8,128)S(1)}, f32[16,454]{1,0:T(8,128)}, u32[]{:S(2)}) copy-start(f32[16,454]{1,0:T(8,128)} %constant.54.clone.face_mask_ref) | copy-start | bytes 87172
  (2 other events, 5.0 us)

commit v4 on v3

--- a/solution.py
+++ b/solution.py
@@ -20,6 +20,7 @@
 BELOW = 3
 WINDOW = 13
 LANE_OWN = 9 * BELOW
+BLOCK = 136
 
 
 def node_row(a, b, c):
@@ -149,6 +150,7 @@
     flat = np.arange(450)
     py, pz = flat // 18, flat % 18
     lane = 9 * ((pz + 1) // 3) + py // 3
+    frame = lane - 9 * (pz % 3 == 2)
     own = np.zeros((ROWS, 128), np.float32)
     face_mask = np.zeros((16, 454), np.float32)
     for a in range(4):
@@ -162,7 +164,7 @@
     out["own"] = own
     out["face_mask"] = face_mask
     pick = np.zeros((450, 128), np.float32)
-    pick[flat, lane] = 1.0
+    pick[flat, frame] = 1.0
     out["pick"] = pick.astype(jnp.bfloat16)
     back = np.zeros((128, 450), np.float32)
     back[lane + LANE_OWN, flat] = 1.0
@@ -366,11 +368,6 @@
     return [[g[c][m] + 1.0 if c == m else g[c][m] for m in range(3)] for c in range(3)]
 
 
-def add_packed(value, out_ref, at):
-    half = value.shape[0] // 2
-    out_ref[at : at + half, :] = value[:half] + rolled(value[half:], 64)
-
-
 def plane_index(width):
     row = lax.broadcasted_iota(jnp.int32, (ROWS, width), 0)
     return jnp.where(
@@ -408,7 +405,10 @@
     out_ref[3:6, :] = vel_ref[:, 900:1350]
 
 
-def pack_kernel(disp_ref, vel_ref, dens_ref, energy_ref, live_ref, pick_ref, place_ref, out_ref):
+def pack_kernel(disp_ref, vel_ref, dens_ref, energy_ref, live_ref, pick_ref, place_ref, out_ref,
+                where_ref):
+    dom, sub = lax.axis_index("dom"), lax.axis_index("sub")
+    where_ref[...] = jnp.where(row_index() == 0, dom.astype(F32), sub.astype(F32))
     plane = plane_index(450)
     mask = node_mask() & (plane >= 1)
     blocks = []
@@ -421,58 +421,65 @@
                     mask, jnp.where(plane == 1, first, jnp.where(plane == 2, second, third)), 0.0
                 )
             )
-    add_packed(exact_dot(jnp.concatenate(blocks, axis=0), pick_ref[...]), out_ref, 0)
+    out_ref[0:240, :] = exact_dot(jnp.concatenate(blocks, axis=0), pick_ref[...])
     row = lax.broadcasted_iota(jnp.int32, (8, 48), 0)
     tail = jnp.pad(energy_ref[24:27], ((0, 5), (0, 0)))
     tail = jnp.where(row == 3, live_ref[...].astype(F32), tail)
     density = jnp.pad(dens_ref[...], ((0, 0), (0, 3))).T
-    placed = exact_dot(
+    out_ref[240:400, :] = exact_dot(
         jnp.concatenate([density, energy_ref[0:24], tail], axis=0), place_ref[...]
     )
-    add_packed(placed[0:128], out_ref, 120)
-    add_packed(placed[128:160], out_ref, 184)
-
-
-def halo_kernel(packed_ref, halo_ref, pick_ref, out_ref):
+
+
+def send_columns(value, start):
+    lane = lax.broadcasted_iota(jnp.int32, (BLOCK, 128), 1)
+    value = jnp.concatenate([value, jnp.zeros((3 * BLOCK - 400, 128), F32)], axis=0)
+    parts = [rolled(value[BLOCK * i : BLOCK * i + BLOCK], 36 * i - start) for i in range(3)]
+    return jnp.where(lane < 36, parts[0], jnp.where(lane < 72, parts[1], parts[2]))
+
+
+def halo_kernel(packed_ref, halo_ref, pick_ref, where_ref, own_ref, first_ref, second_ref):
     mask = node_mask() & (plane_index(450) == 0)
     blocks = [
         jnp.where(mask, jnp.broadcast_to(halo_ref[comp : comp + 1, :], (ROWS, 450)), 0.0)
         for comp in range(6)
     ]
     nodes = exact_dot(jnp.concatenate(blocks, axis=0), pick_ref[...])
-    out_ref[0:120, :] = packed_ref[0:120, :] + (nodes[:120] + rolled(nodes[120:], 64))
-    out_ref[120:200, :] = packed_ref[120:200, :]
+    own = jnp.concatenate([packed_ref[0:240] + nodes, packed_ref[240:400]], axis=0)
+    own_ref[...] = own
+    up, down = send_columns(own, 18), send_columns(own, 0)
+    even = is_even(where_ref, 1, (BLOCK, 128))
+    first_ref[...] = jnp.where(even, up, down)
+    second_ref[...] = jnp.where(even, down, up)
 
 
 def unpack(own, below, above):
-    lane = lax.broadcasted_iota(jnp.int32, own.shape, 1)
-    is_own = (lane >= 27) & (lane < 90)
-    is_below = lane < 36
-    is_above = lane >= 81
-
-    def window(by):
-        return (
-            jnp.where(is_own, rolled(own, 27 - by), 0.0)
-            + jnp.where(is_below, rolled(below, -27 - by), 0.0)
-            + jnp.where(is_above, rolled(above, 81 - by), 0.0)
+    lane = lax.broadcasted_iota(jnp.int32, (8, 128), 1)
+    rows = []
+    for at in range(0, 400, 8):
+        block, inner = at // BLOCK, at % BLOCK
+        on_vertex = 9 if at < 240 and at % ROWS in (8, 32) else 0
+        base = 36 * block
+        mine = rolled(own[at : at + 8], 27 + on_vertex)
+        low = rolled(below[inner : inner + 8], on_vertex - 9 - base)
+        high = rolled(above[inner : inner + 8], 81 + on_vertex - base)
+        rows.append(
+            jnp.where(
+                lane < 27 + on_vertex, low, jnp.where(lane < 81 + on_vertex, mine, high)
+            )
         )
-
-    return window(0), window(64)
+    return jnp.concatenate(rows, axis=0)
 
 
 def force_kernel(own_ref, first_ref, second_ref, grad_ref, grad_t_ref, psi_ref, weight_ref,
                  flags_ref, force_ref, face1_ref, face2_ref, disp_ref, vel_ref, mass_ref, live_ref,
                  power_ref, wdens_ref, g_ref, flux_ref, point_ref):
-    even = is_even(flags_ref, 1, (200, 128))
+    even = is_even(flags_ref, 1, (BLOCK, 128))
     first, second = first_ref[...], second_ref[...]
-    below = jnp.where(even, second, first)
-    above = jnp.where(even, first, second)
-    disp, vel = unpack(own_ref[0:120], below[0:120], above[0:120])
+    window = unpack(own_ref[...], jnp.where(even, second, first), jnp.where(even, first, second))
+    disp, vel, energy = window[0:120], window[120:240], window[368:400]
     disp_ref[...] = disp
     vel_ref[...] = vel
-    dens_low, dens_high = unpack(own_ref[120:184], below[120:184], above[120:184])
-    energy_low, energy_high = unpack(own_ref[184:200], below[184:200], above[184:200])
-    energy = jnp.concatenate([energy_low, energy_high], axis=0)
     lane = lax.broadcasted_iota(jnp.int32, (1, 128), 1)
     live = jnp.where(lane < 9 * WINDOW, energy[27:28], 0.0)
     live_ref[...] = jnp.broadcast_to(live, (8, 128))
@@ -489,8 +496,7 @@
         volume = j[0][0] * cof[0][0] + j[0][1] * cof[0][1] + j[0][2] * cof[0][2]
         volume = jnp.where(alive > 0.5, volume, 1.0)
         inverse = 1.0 / volume
-        source = dens_low if chunk < 8 else dens_high
-        mass_density = source[8 * (chunk % 8) : 8 * (chunk % 8) + 8]
+        mass_density = window[240 + 8 * chunk : 248 + 8 * chunk]
         density = mass_density * inverse
         pressure = (5.0 / 3.0 - 1.0) * density * point_ref[at, :]
         spatial = [
@@ -713,33 +719,32 @@
 def body(displacement, velocity, energy, mass_density, live_mask, time_step):
     table = {name: jnp.asarray(value) for name, value in constants().items()}
     n_dom, n_sub = lax.axis_size("dom"), lax.axis_size("sub")
-    dom, sub = lax.axis_index("dom"), lax.axis_index("sub")
     up = [(i, i + 1) for i in range(n_dom - 1)]
     down = [(i + 1, i) for i in range(n_dom - 1)]
 
     def pairs(start, size):
         return [p for i in range(start, size - 1, 2) for p in ((i, i + 1), (i + 1, i))]
 
-    row = lax.broadcasted_iota(jnp.int32, (8, 128), 0)
-    flags = jnp.where(
-        row == 0, dom.astype(F32), jnp.where(row == 1, sub.astype(F32), time_step)
-    )
     walls = (table["off_x"], table["off_z"])
 
     (last,) = call(last_kernel, [(6, 450)], copied=True)(displacement, velocity)
     halo = lax.ppermute(last, "dom", up)
-    (packed,) = call(pack_kernel, [(200, 128)], copied=True)(
+    packed, where = call(pack_kernel, [(400, 128), (8, 128)], copied=True)(
         displacement, velocity, mass_density.T, energy, live_mask.reshape(1, 48), table["pick"],
         table["place"],
     )
-    (own,) = call(halo_kernel, [(200, 128)])(packed, halo, table["pick"])
-    below = lax.ppermute(own, "sub", pairs(0, n_sub))
-    above = lax.ppermute(own, "sub", pairs(1, n_sub))
+    row = lax.broadcasted_iota(jnp.int32, (8, 128), 0)
+    own, z_first, z_second = call(
+        halo_kernel, [(400, 128), (BLOCK, 128), (BLOCK, 128)]
+    )(packed, halo, table["pick"], where)
+    flags = jnp.where(row < 2, where, time_step)
+    first = lax.ppermute(z_first, "sub", pairs(0, n_sub))
+    second = lax.ppermute(z_second, "sub", pairs(1, n_sub))
     force, face1, face2, disp, vel, mass, live, power, wdens = call(
         force_kernel,
         [NODES, FACE, FACE, NODES, NODES, POINTS, (8, 128), POINTS, POINTS],
         [(384, 768), (384, 384), POINTS],
-    )(own, below, above, table["grad"], table["grad_t"], table["psi"], table["weight"], flags)
+    )(own, first, second, table["grad"], table["grad_t"], table["psi"], table["weight"], flags)
 
     def swap(face1, face2):
         second = lax.ppermute(face2, "dom", pairs(1, n_dom))

time: 99.3 us -> 99.1 us (level)
  blocking collectives: 37.8 us -> 42.3 us
  starting transfers between devices: 34.1 us -> 31.2 us
  waiting for transfers between devices: 14.7 us -> 13 us
    all_to_all x1, blocking collectives: 22.4 us -> 26.7 us  [body(): lax.all_to_all(jnp.broadcast_to(slab, (n_sub, 128)), 'sub', 0, 0, tiled=T...]
    ppermute x2, starting transfers between devices: 8 us -> 4.67 us  [the longest x1 4 us: body(): first = lax.ppermute(z_first, 'sub', pairs(0, n_sub))]
    ppermute x2, waiting for transfers between devices: 2.6 us -> 1.37 us  [the longest x1 1.37 us: body(): first = lax.ppermute(z_first, 'sub', pairs(0, n_sub))]
where the time goes in v4:
time: 99.1 us; the launch traced here: 98.6 us
  blocking collectives  42.3 us (43%)
  starting transfers between devices  31.2 us (31%)
  waiting for transfers between devices  13 us (13%)
  Pallas kernels  10.1 us (10%)
  between operations  1.65 us (2%)
    all_to_all x1, blocking collectives, body(): lax.all_to_all(jnp.broadcast_to(slab, (n_sub, 128)), 'sub', 0, 0, tiled=T...  26.7 us
    all_to_all x1, blocking collectives, body(): lax.all_to_all(local, 'dom', 0, 0, tiled=True)  15.7 us
    ppermute x3, starting transfers between devices, swap(): second = lax.ppermute(face2, 'dom', pairs(1, n_dom))  12.6 us
    pallas_call x12, Pallas kernels, run(): pl.pallas_call(body_of, out_shape=[jax.ShapeDtypeStruct(shape, F32) for s...  10.1 us
    ppermute x3, starting transfers between devices, swap(): return (lax.ppermute(face1, 'dom', pairs(0, n_dom)), second)  8.82 us
    ppermute x3, waiting for transfers between devices, swap(): second = lax.ppermute(face2, 'dom', pairs(1, n_dom))  6.81 us
    ppermute x1, waiting for transfers between devices, body(): from_above = lax.ppermute(face, 'dom', down)  4.83 us
    ppermute x1, starting transfers between devices, body(): first = lax.ppermute(z_first, 'sub', pairs(0, n_sub))  4 us
  transfers between devices with their start and end apart: 10, of which 5 were waited for; matrix products, arithmetic and copies ran while one was open for 0% of the time, Pallas kernels for 4%

profile of v4, /device:TPU:57, one launch (start us, length us, event | category | flops | bytes accessed | tf_op | source)
XLA Modules:
  0.0 98.6 jit_solution(8754350459718555557)
XLA Ops:
  0.6 0.8 shard_map.239
  1.5 3.0 %collective-permute-start = (f32[6,450]{1,0:T(8,128)S(1)}, f32[6,450]{1,0:T(8,128)S(1)}, u32[]{:S(2)}, u32[]{:S(2)}) collective-permute-start(f32[6,450]{1,0:T(8,128)S(1)} %shard_map.239), channel_id=1, source_target_pairs={{0,12},{12,24},{24,36},{36,48},{48,60},{60,72},{72,84},{84,96},{96... | collective-permute-start | bytes 32408 | tf_op jit(solution)/shard_map/ppermute | solution.py:731
  5.2 1.7 %shard_map.238 = (f32[400,128]{1,0:T(8,128)S(1)}, f32[8,128]{1,0:T(8,128)S(1)}) custom-call(f32[3,1350]{1,0:T(4,128)} %refs_0_.3, f32[3,1350]{1,0:T(4,128)} %refs_1_.3, f32[48,125]{1,0:T(8,128)} %bitcast.10, f32[27,48]{1,0:T(8,128)} %refs_3_.1, s32[1,48]{1,0:T(1,128)} %bitcast.11, bf16[450,128]{1,0:T(8,128)(2,1)} %constant.47.clone.refs_5_.pick_ref, ...), custom_call_target="tpu_custom_call" | custom-call | flops 1000000 | bytes 400000 | tf_op jit(solution)/shard_map/pallas_call | solution.py:701
  7.4 4.0 %collective-permute-start.1 = (f32[136,128]{1,0:T(8,128)S(1)}, f32[136,128]{1,0:T(8,128)S(1)}, u32[]{:S(2)}, u32[]{:S(2)}) collective-permute-start(f32[136,128]{1,0:T(8,128)S(1)} %get-tuple-element.38), channel_id=1, source_target_pairs={{0,1},{1,0},{2,3},{3,2},{4,5},{5,4},{6,7},{7,6},{8,9},{9,8},{10,11... | collective-permute-start | bytes 208904 | tf_op jit(solution)/shard_map/ppermute | solution.py:741
  12.1 1.4 %collective-permute-done.1.first_ref = f32[136,128]{1,0:T(8,128)S(1)} collective-permute-done((f32[136,128]{1,0:T(8,128)S(1)}, f32[136,128]{1,0:T(8,128)S(1)}, u32[]{:S(2)}, u32[]{:S(2)}) %collective-permute-start.1) | collective-permute-done | bytes 69664 | tf_op jit(solution)/shard_map/ppermute | solution.py:741
  13.6 1.2 %shard_map.241 = (f32[120,128]{1,0:T(8,128)S(1)}, f32[32,128]{1,0:T(8,128)S(1)}, f32[32,128]{1,0:T(8,128)S(1)}, f32[120,128]{1,0:T(8,128)S(1)}, f32[120,128]{1,0...) custom-call(f32[400,128]{1,0:T(8,128)S(1)} %get-tuple-element.37.own, ...), custom_call_target="tpu_custom_call" | custom-call | flops 1000000 | bytes 400000 | tf_op jit(solution)/shard_map/pallas_call | solution.py:701
  14.7 2.9 %collective-permute-start.3 = (f32[32,128]{1,0:T(8,128)S(1)}, f32[32,128]{1,0:T(8,128)S(1)}, u32[]{:S(2)}, u32[]{:S(2)}) collective-permute-start(f32[32,128]{1,0:T(8,128)S(1)} %get-tuple-element.44), channel_id=1, source_target_pairs={{0,12},{12,0},{24,36},{36,24},{48,60},{60,48},{72,84},{84,72},{96,... | collective-permute-start | bytes 49160 | tf_op jit(solution)/shard_map/ppermute | solution.py:751
  17.7 4.2 %collective-permute-start.4 = (f32[32,128]{1,0:T(8,128)S(1)}, f32[32,128]{1,0:T(8,128)S(1)}, u32[]{:S(2)}, u32[]{:S(2)}) collective-permute-start(f32[32,128]{1,0:T(8,128)S(1)} %get-tuple-element.45), channel_id=1, source_target_pairs={{12,24},{24,12},{36,48},{48,36},{60,72},{72,60},{84,96},{96,84},{1... | collective-permute-start | bytes 49160 | tf_op jit(solution)/shard_map/ppermute | solution.py:750
  22.0 0.9 shard_map.242
  22.9 2.0 %collective-permute-done.4.second_ref = f32[32,128]{1,0:T(8,128)S(1)} collective-permute-done((f32[32,128]{1,0:T(8,128)S(1)}, f32[32,128]{1,0:T(8,128)S(1)}, u32[]{:S(2)}, u32[]{:S(2)}) %collective-permute-start.4) | collective-permute-done | bytes 16416 | tf_op jit(solution)/shard_map/ppermute | solution.py:750
  25.5 1.9 %collective-permute-start.5 = (f32[32,128]{1,0:T(8,128)S(1)}, f32[32,128]{1,0:T(8,128)S(1)}, u32[]{:S(2)}, u32[]{:S(2)}) collective-permute-start(f32[32,128]{1,0:T(8,128)S(1)} %get-tuple-element.48), channel_id=1, source_target_pairs={{0,12},{12,0},{24,36},{36,24},{48,60},{60,48},{72,84},{84,72},{96,... | collective-permute-start | bytes 49160 | tf_op jit(solution)/shard_map/ppermute | solution.py:751
  27.4 4.2 %collective-permute-start.6 = (f32[32,128]{1,0:T(8,128)S(1)}, f32[32,128]{1,0:T(8,128)S(1)}, u32[]{:S(2)}, u32[]{:S(2)}) collective-permute-start(f32[32,128]{1,0:T(8,128)S(1)} %get-tuple-element.49), channel_id=1, source_target_pairs={{12,24},{24,12},{36,48},{48,36},{60,72},{72,60},{84,96},{96,84},{1... | collective-permute-start | bytes 49160 | tf_op jit(solution)/shard_map/ppermute | solution.py:750
  31.6 3.0 %collective-permute-done.6.second_ref = f32[32,128]{1,0:T(8,128)S(1)} collective-permute-done((f32[32,128]{1,0:T(8,128)S(1)}, f32[32,128]{1,0:T(8,128)S(1)}, u32[]{:S(2)}, u32[]{:S(2)}) %collective-permute-start.6) | collective-permute-done | bytes 16416 | tf_op jit(solution)/shard_map/ppermute | solution.py:750
  35.0 15.7 %all_to_all.17 = f32[64,1,128]{2,1,0:T(1,128)S(1)} all-to-all(f32[64,1,128]{2,1,0:T(1,128)S(1)} %bitcast.9), channel_id=1, replica_groups=mesh['dom'=64,'sub'=12] {'dom'}, dimensions={0} | all-to-all | bytes 65536 | tf_op jit(solution)/shard_map/all_to_all | solution.py:765
  50.7 26.7 %all_to_all.18 = f32[12,1,128]{2,1,0:T(1,128)S(1)} all-to-all(f32[12,1,128]{2,1,0:T(1,128)S(1)} %broadcast_in_dim.11), channel_id=1, replica_groups=mesh['dom'=64,'sub'=12] {'sub'}, dimensions={0} | all-to-all | bytes 12288 | tf_op jit(solution)/shard_map/all_to_all | solution.py:766
  77.4 1.0 %shard_map.245 = (f32[120,128]{1,0:T(8,128)S(1)}, f32[120,128]{1,0:T(8,128)S(1)}, f32[120,128]{1,0:T(8,128)S(1)}, f32[32,128]{1,0:T(8,128)S(1)}, f32[32,128]{1,0:T(8,128)S(1)}) custom-call(f32[12,128]{1,0:T(8,128)S(1)} %bitcast.8, f32[120,128]{1,0:T(8,128)S(1)} %get-tuple-element.52.disp_ref, f32[120,128]{1,0:T(8,128)S(1)} %get-tuple-element.53.vel_ref, ...), custom_call_target="tpu_custom_call" | custom-call | flops 1000000 | bytes 400000 | tf_op jit(solution)/shard_map/pallas_call | solution.py:701
  78.4 4.0 %collective-permute-start.7 = (f32[32,128]{1,0:T(8,128)S(1)}, f32[32,128]{1,0:T(8,128)S(1)}, u32[]{:S(2)}, u32[]{:S(2)}) collective-permute-start(f32[32,128]{1,0:T(8,128)S(1)} %get-tuple-element.62), channel_id=1, source_target_pairs={{0,12},{12,0},{24,36},{36,24},{48,60},{60,48},{72,84},{84,72},{96,... | collective-permute-start | bytes 49160 | tf_op jit(solution)/shard_map/ppermute | solution.py:751
  82.4 4.3 %collective-permute-start.8 = (f32[32,128]{1,0:T(8,128)S(1)}, f32[32,128]{1,0:T(8,128)S(1)}, u32[]{:S(2)}, u32[]{:S(2)}) collective-permute-start(f32[32,128]{1,0:T(8,128)S(1)} %get-tuple-element.63), channel_id=1, source_target_pairs={{12,24},{24,12},{36,48},{48,36},{60,72},{72,60},{84,96},{96,84},{1... | collective-permute-start | bytes 49160 | tf_op jit(solution)/shard_map/ppermute | solution.py:750
  86.7 1.0 %shard_map.246 = f32[3,1350]{1,0:T(4,128)} custom-call(f32[120,128]{1,0:T(8,128)S(1)} %get-tuple-element.58.nodes_ref.newvel_ref, bf16[128,450]{1,0:T(8,128)(2,1)S(1)} %copy-done.3), custom_call_target="tpu_custom_call" | custom-call | flops 1000000 | bytes 400000 | tf_op jit(solution)/shard_map/pallas_call | solution.py:701
  87.7 1.9 %collective-permute-done.8.second_ref = f32[32,128]{1,0:T(8,128)S(1)} collective-permute-done((f32[32,128]{1,0:T(8,128)S(1)}, f32[32,128]{1,0:T(8,128)S(1)}, u32[]{:S(2)}, u32[]{:S(2)}) %collective-permute-start.8) | collective-permute-done | bytes 16416 | tf_op jit(solution)/shard_map/ppermute | solution.py:750
  89.6 0.9 shard_map.247
  90.5 2.1 %collective-permute-start.9 = (f32[32,128]{1,0:T(8,128)S(1)}, f32[32,128]{1,0:T(8,128)S(1)}, u32[]{:S(2)}, u32[]{:S(2)}) collective-permute-start(f32[32,128]{1,0:T(8,128)S(1)} %get-tuple-element.66), channel_id=1, source_target_pairs={{12,0},{24,12},{36,24},{48,36},{60,48},{72,60},{84,72},{96,84},{10... | collective-permute-start | bytes 49160 | tf_op jit(solution)/shard_map/ppermute | solution.py:777
  93.0 4.8 %collective-permute-done.9.face_ref = f32[32,128]{1,0:T(8,128)S(1)} collective-permute-done((f32[32,128]{1,0:T(8,128)S(1)}, f32[32,128]{1,0:T(8,128)S(1)}, u32[]{:S(2)}, u32[]{:S(2)}) %collective-permute-start.9) | collective-permute-done | bytes 16416 | tf_op jit(solution)/shard_map/ppermute | solution.py:777
  97.8 0.8 shard_map.249
  (47 shorter events, 2.8 us)
Async XLA Ops:
  1.5 5.4 %copy-start.4 = (bf16[450,128]{1,0:T(8,128)(2,1)S(1)}, bf16[450,128]{1,0:T(8,128)(2,1)}, u32[]{:S(2)}) copy-start(bf16[450,128]{1,0:T(8,128)(2,1)} %constant.47.clone.refs_5_.pick_ref) | copy-start | bytes 345604
  1.5 5.4 %collective-permute-start = (f32[6,450]{1,0:T(8,128)S(1)}, f32[6,450]{1,0:T(8,128)S(1)}, u32[]{:S(2)}, u32[]{:S(2)}) collective-permute-start(f32[6,450]{1,0:T(8,128)S(1)} %shard_map.239), channel_id=1, source_target_pairs={{0,12},{12,24},{24,36},{36,48},{48,60},{60,72},{72,84},{84,96},{96... | collective-permute-start | bytes 32408 | tf_op jit(solution)/shard_map/ppermute | solution.py:731
  5.2 8.3 %copy-start.2 = (f32[128,128]{1,0:T(8,128)S(1)}, f32[128,128]{1,0:T(8,128)}, u32[]{:S(2)}) copy-start(f32[128,128]{1,0:T(8,128)} %constant.44.clone.weight_ref) | copy-start | bytes 196612
  6.9 6.6 %copy-start = (bf16[384,240]{1,0:T(8,128)(2,1)S(1)}, bf16[384,240]{1,0:T(8,128)(2,1)}, u32[]{:S(2)}) copy-start(bf16[384,240]{1,0:T(8,128)(2,1)} %constant.38.clone.grad_ref) | copy-start | bytes 552964
  6.9 6.6 %copy-start.1 = (bf16[160,384]{1,0:T(8,128)(2,1)S(1)}, bf16[160,384]{1,0:T(8,128)(2,1)}, u32[]{:S(2)}) copy-start(bf16[160,384]{1,0:T(8,128)(2,1)} %constant.39.clone.grad_t_ref) | copy-start | bytes 368644
  6.9 6.6 %copy-start.12 = (bf16[128,96]{1,0:T(8,128)(2,1)S(1)}, bf16[128,96]{1,0:T(8,128)(2,1)}, u32[]{:S(2)}) copy-start(bf16[128,96]{1,0:T(8,128)(2,1)} %constant.42.clone.psi_ref) | copy-start | bytes 73732
  7.4 6.1 %collective-permute-start.1 = (f32[136,128]{1,0:T(8,128)S(1)}, f32[136,128]{1,0:T(8,128)S(1)}, u32[]{:S(2)}, u32[]{:S(2)}) collective-permute-start(f32[136,128]{1,0:T(8,128)S(1)} %get-tuple-element.38), channel_id=1, source_target_pairs={{0,1},{1,0},{2,3},{3,2},{4,5},{5,4},{6,7},{7,6},{8,9},{9,8},{10,11... | collective-permute-start | bytes 208904 | tf_op jit(solution)/shard_map/ppermute | solution.py:741
  11.4 2.1 %collective-permute-start.2 = (f32[136,128]{1,0:T(8,128)S(1)}, f32[136,128]{1,0:T(8,128)S(1)}, u32[]{:S(2)}, u32[]{:S(2)}) collective-permute-start(f32[136,128]{1,0:T(8,128)S(1)} %get-tuple-element.39), channel_id=1, source_target_pairs={{1,2},{2,1},{3,4},{4,3},{5,6},{6,5},{7,8},{8,7},{9,10},{10,9},{13,... | collective-permute-start | bytes 208904 | tf_op jit(solution)/shard_map/ppermute | solution.py:742
  13.5 8.3 %copy-start.13 = (bf16[128,48]{1,0:T(8,128)(2,1)S(1)}, bf16[128,48]{1,0:T(8,128)(2,1)}, u32[]{:S(2)}) copy-start(bf16[128,48]{1,0:T(8,128)(2,1)} %constant.53.clone.take_ref) | copy-start | bytes 36868
  13.6 8.3 %copy-start.15 = (bf16[64,128]{1,0:T(8,128)(2,1)S(1)}, bf16[64,128]{1,0:T(8,128)(2,1)}, u32[]{:S(2)}) copy-start(bf16[64,128]{1,0:T(8,128)(2,1)} %constant.43.clone.psi_t_ref) | copy-start | bytes 49156
  14.7 8.1 %collective-permute-start.3 = (f32[32,128]{1,0:T(8,128)S(1)}, f32[32,128]{1,0:T(8,128)S(1)}, u32[]{:S(2)}, u32[]{:S(2)}) collective-permute-start(f32[32,128]{1,0:T(8,128)S(1)} %get-tuple-element.44), channel_id=1, source_target_pairs={{0,12},{12,0},{24,36},{36,24},{48,60},{60,48},{72,84},{84,72},{96,... | collective-permute-start | bytes 49160 | tf_op jit(solution)/shard_map/ppermute | solution.py:751
  17.7 7.2 %collective-permute-start.4 = (f32[32,128]{1,0:T(8,128)S(1)}, f32[32,128]{1,0:T(8,128)S(1)}, u32[]{:S(2)}, u32[]{:S(2)}) collective-permute-start(f32[32,128]{1,0:T(8,128)S(1)} %get-tuple-element.45), channel_id=1, source_target_pairs={{12,24},{24,12},{36,48},{48,36},{60,72},{72,60},{84,96},{96,84},{1... | collective-permute-start | bytes 49160 | tf_op jit(solution)/shard_map/ppermute | solution.py:750
  21.9 3.0 %copy-start.5 = (bf16[128,240]{1,0:T(8,128)(2,1)S(1)}, bf16[128,240]{1,0:T(8,128)(2,1)}, u32[]{:S(2)}) copy-start(bf16[128,240]{1,0:T(8,128)(2,1)} %constant.40.clone.phi_ref) | copy-start | bytes 184324
  21.9 2.9 %copy-start.6 = (f32[40,128]{1,0:T(8,128)S(1)}, f32[40,128]{1,0:T(8,128)}, u32[]{:S(2)}) copy-start(f32[40,128]{1,0:T(8,128)} %constant.51.clone.off_z_ref) | copy-start | bytes 61444
  21.9 2.9 %copy-start.7 = (f32[40,128]{1,0:T(8,128)S(1)}, f32[40,128]{1,0:T(8,128)}, u32[]{:S(2)}) copy-start(f32[40,128]{1,0:T(8,128)} %constant.50.clone.off_x_ref) | copy-start | bytes 61444
  21.9 2.9 %copy-start.9 = (f32[40,128]{1,0:T(8,128)S(1)}, f32[40,128]{1,0:T(8,128)}, u32[]{:S(2)}) copy-start(f32[40,128]{1,0:T(8,128)} %constant.45.clone.own_ref) | copy-start | bytes 61444
  25.5 6.1 %collective-permute-start.5 = (f32[32,128]{1,0:T(8,128)S(1)}, f32[32,128]{1,0:T(8,128)S(1)}, u32[]{:S(2)}, u32[]{:S(2)}) collective-permute-start(f32[32,128]{1,0:T(8,128)S(1)} %get-tuple-element.48), channel_id=1, source_target_pairs={{0,12},{12,0},{24,36},{36,24},{48,60},{60,48},{72,84},{84,72},{96,... | collective-permute-start | bytes 49160 | tf_op jit(solution)/shard_map/ppermute | solution.py:751
  27.4 7.2 %collective-permute-start.6 = (f32[32,128]{1,0:T(8,128)S(1)}, f32[32,128]{1,0:T(8,128)S(1)}, u32[]{:S(2)}, u32[]{:S(2)}) collective-permute-start(f32[32,128]{1,0:T(8,128)S(1)} %get-tuple-element.49), channel_id=1, source_target_pairs={{12,24},{24,12},{36,48},{48,36},{60,72},{72,60},{84,96},{96,84},{1... | collective-permute-start | bytes 49160 | tf_op jit(solution)/shard_map/ppermute | solution.py:750
  77.4 9.3 %copy-start.3 = (bf16[128,450]{1,0:T(8,128)(2,1)S(1)}, bf16[128,450]{1,0:T(8,128)(2,1)}, u32[]{:S(2)}) copy-start(bf16[128,450]{1,0:T(8,128)(2,1)} %constant.48.clone.back_ref) | copy-start | bytes 345604
  78.4 9.3 %collective-permute-start.7 = (f32[32,128]{1,0:T(8,128)S(1)}, f32[32,128]{1,0:T(8,128)S(1)}, u32[]{:S(2)}, u32[]{:S(2)}) collective-permute-start(f32[32,128]{1,0:T(8,128)S(1)} %get-tuple-element.62), channel_id=1, source_target_pairs={{0,12},{12,0},{24,36},{36,24},{48,60},{60,48},{72,84},{84,72},{96,... | collective-permute-start | bytes 49160 | tf_op jit(solution)/shard_map/ppermute | solution.py:751
  82.4 7.2 %collective-permute-start.8 = (f32[32,128]{1,0:T(8,128)S(1)}, f32[32,128]{1,0:T(8,128)S(1)}, u32[]{:S(2)}, u32[]{:S(2)}) collective-permute-start(f32[32,128]{1,0:T(8,128)S(1)} %get-tuple-element.63), channel_id=1, source_target_pairs={{12,24},{24,12},{36,48},{48,36},{60,72},{72,60},{84,96},{96,84},{1... | collective-permute-start | bytes 49160 | tf_op jit(solution)/shard_map/ppermute | solution.py:750
  90.5 7.3 %copy-start.8 = (bf16[128,454]{1,0:T(8,128)(2,1)S(1)}, bf16[128,454]{1,0:T(8,128)(2,1)}, u32[]{:S(2)}) copy-start(bf16[128,454]{1,0:T(8,128)(2,1)} %constant.49.clone.face_back_ref) | copy-start | bytes 348676
  90.5 7.3 %collective-permute-start.9 = (f32[32,128]{1,0:T(8,128)S(1)}, f32[32,128]{1,0:T(8,128)S(1)}, u32[]{:S(2)}, u32[]{:S(2)}) collective-permute-start(f32[32,128]{1,0:T(8,128)S(1)} %get-tuple-element.66), channel_id=1, source_target_pairs={{12,0},{24,12},{36,24},{48,36},{60,48},{72,60},{84,72},{96,84},{10... | collective-permute-start | bytes 49160 | tf_op jit(solution)/shard_map/ppermute | solution.py:777
  92.6 5.2 %copy-start.11 = (f32[16,454]{1,0:T(8,128)S(1)}, f32[16,454]{1,0:T(8,128)}, u32[]{:S(2)}) copy-start(f32[16,454]{1,0:T(8,128)} %constant.46.clone.face_mask_ref) | copy-start | bytes 87172
  (2 other events, 5.8 us)

commit v5 on v4

--- a/solution.py
+++ b/solution.py
@@ -31,16 +31,6 @@
     if b > 0:
         return 16 + 4 * a + 2 * (b - 1) + c - 1
     return 32 + a
-
-
-def face_row(b, c):
-    if b == 0 and c > 0:
-        return c - 1
-    if b > 0 and c == 0:
-        return 2 + b - 1
-    if b > 0:
-        return 4 + 2 * (b - 1) + c - 1
-    return 8
 
 
 def local_row(a, b, c):
@@ -152,26 +142,19 @@
     lane = 9 * ((pz + 1) // 3) + py // 3
     frame = lane - 9 * (pz % 3 == 2)
     own = np.zeros((ROWS, 128), np.float32)
-    face_mask = np.zeros((16, 454), np.float32)
     for a in range(4):
         for k in range(450):
             b, c = py[k] % 3, (pz[k] + 1) % 3
             row = node_row(a, b, c)
             if a > 0:
                 own[row, lane[k] + LANE_OWN] = 1.0
-            else:
-                face_mask[face_row(b, c), k + 4] = 1.0
     out["own"] = own
-    out["face_mask"] = face_mask
     pick = np.zeros((450, 128), np.float32)
     pick[flat, frame] = 1.0
     out["pick"] = pick.astype(jnp.bfloat16)
     back = np.zeros((128, 450), np.float32)
     back[lane + LANE_OWN, flat] = 1.0
     out["back"] = back.astype(jnp.bfloat16)
-    face_back = np.zeros((128, 454), np.float32)
-    face_back[lane + LANE_OWN, flat + 4] = 1.0
-    out["face_back"] = face_back.astype(jnp.bfloat16)
     off_x = np.ones((ROWS, 128), np.float32)
     off_z = np.ones((ROWS, 128), np.float32)
     for b in range(3):
@@ -331,6 +314,11 @@
     low, high = face_of(nodes, 0), face_of(nodes, 3)
     first_ref[...] = jnp.where(even, high, low)
     second_ref[...] = jnp.where(even, low, high)
+
+
+def z_wall(flags_ref, off_z_ref):
+    wall = jnp.minimum(off_z_ref[...] + flag(flags_ref, 1), 1.0)
+    return jnp.concatenate([wall, wall, wall], axis=0)
 
 
 def shared_sum(nodes, flags_ref, first_ref, second_ref, off_x_ref, off_z_ref):
@@ -617,8 +605,8 @@
 
 
 def first_shape_kernel(moments_ref, disp_ref, vel_ref, resid_ref, image_ref, live_ref, flags_ref,
-                       grad_ref, grad_t_ref, weight_ref, newvel_ref, moved_ref, part_ref, face1_ref,
-                       face2_ref, g_ref, flux_ref):
+                       off_z_ref, grad_ref, grad_t_ref, weight_ref, newvel_ref, moved_ref, part_ref,
+                       near_ref, far_ref, skip_ref, g_ref, flux_ref):
     moments = jnp.sum(moments_ref[...], axis=0, keepdims=True)
     mu0, mu1, mu2, mu3 = (moments[:, i : i + 1] for i in range(4))
     alpha = mu0 / mu1
@@ -633,23 +621,23 @@
     newvel_ref[...] = newvel
     moved = disp_ref[...] + step * newvel
     moved_ref[...] = moved
-    part = shape_forces(moved, live_ref[...], grad_ref, grad_t_ref, weight_ref, g_ref, flux_ref)
+    live = live_ref[...]
+    part = shape_forces(moved, live, grad_ref, grad_t_ref, weight_ref, g_ref, flux_ref)
     part_ref[...] = part
-    send_faces(part, flags_ref, face1_ref, face2_ref)
-
-
-def second_shape_kernel(part_ref, first_ref, second_ref, flags_ref, off_x_ref, off_z_ref, newvel_ref,
-                        moved_ref, live_ref, grad_ref, grad_t_ref, weight_ref, base_ref, face_ref,
-                        g_ref, flux_ref):
-    gradient = shared_sum(part_ref[...], flags_ref, first_ref, second_ref, off_x_ref, off_z_ref)
-    u = moved_ref[...] - MESH_STEP * gradient
-    part = shape_forces(u, live_ref[...], grad_ref, grad_t_ref, weight_ref, g_ref, flux_ref)
-    face_ref[...] = face_of(part, 0)
-    base_ref[...] = newvel_ref[...] - (MESH_STEP / flag(flags_ref, 2)) * (gradient + part)
-
-
-def write_kernel(nodes_ref, back_ref, out_ref):
-    wide = exact_dot(nodes_ref[...], back_ref[...])
+    next_u = moved - MESH_STEP * part * z_wall(flags_ref, off_z_ref)
+    low = face_of(part, 0)
+    skip_ref[...] = low
+    down = jnp.concatenate([next_u, low, live], axis=0)
+    up = jnp.concatenate(
+        [jnp.zeros((120, 128), F32), face_of(part, 3), jnp.zeros((8, 128), F32)], axis=0
+    )
+    even = is_even(flags_ref, 0, (160, 128))
+    near_ref[...] = jnp.where(even, up, down)
+    far_ref[...] = jnp.where(even, down, up)
+
+
+def write_nodes(nodes, back_ref, out_ref):
+    wide = exact_dot(nodes, back_ref[...])
     plane = plane_index(450)
     masks = [node_mask() & (plane == a) for a in range(1, 4)]
     for comp in range(3):
@@ -658,16 +646,32 @@
         out_ref[comp : comp + 1, :] = jnp.concatenate(planes, axis=1)
 
 
-def mesh_kernel(base_ref, face_ref, flags_ref, face_mask_ref, face_back_ref, out_ref):
-    scale = -MESH_STEP / flag(flags_ref, 2)
-    wide = exact_dot(face_ref[...], face_back_ref[...])
-    mask = face_mask_ref[0:8]
-    corner = face_mask_ref[8:9]
-    out_ref[:, 0:896] = base_ref[:, 0:896]
-    for comp in range(3):
-        extra = jnp.sum(wide[8 * comp : 8 * comp + 8] * mask, axis=0, keepdims=True)
-        extra = extra + wide[24 + comp : 25 + comp] * corner
-        out_ref[comp : comp + 1, 896:1350] = base_ref[comp : comp + 1, 896:1350] + scale * extra
+def write_kernel(nodes_ref, back_ref, out_ref):
+    write_nodes(nodes_ref[...], back_ref, out_ref)
+
+
+def second_shape_kernel(part_ref, near_ref, far_ref, skip_ref, flags_ref, off_x_ref, off_z_ref,
+                        newvel_ref, moved_ref, live_ref, grad_ref, grad_t_ref, weight_ref, back_ref,
+                        out_ref, g_ref, flux_ref, next_g_ref, next_flux_ref):
+    even = is_even(flags_ref, 0, (160, 128))
+    near, far = near_ref[...], far_ref[...]
+    upper, lower = jnp.where(even, near, far), jnp.where(even, far, near)
+    wall = z_wall(flags_ref, off_z_ref)
+    off_x = off_x_ref[...]
+    x_wall = jnp.minimum(off_x + flag(flags_ref, 0), 1.0)
+    total = add_faces(part_ref[...], lower[120:152], upper[120:152])
+    gradient = total * wall * jnp.concatenate([x_wall, x_wall, x_wall], axis=0)
+    u = moved_ref[...] - MESH_STEP * gradient
+    zero = jnp.zeros((120, 128), F32)
+    next_u = upper[0:120] * jnp.concatenate([off_x, off_x, off_x], axis=0)
+    next_u = next_u + wall * add_faces(zero, face_of(u, 3), -MESH_STEP * skip_ref[...])
+    part = shape_forces(u, live_ref[...], grad_ref, grad_t_ref, weight_ref, g_ref, flux_ref)
+    next_part = shape_forces(
+        next_u, upper[152:160], grad_ref, grad_t_ref, weight_ref, next_g_ref, next_flux_ref
+    )
+    second = add_faces(part, jnp.zeros((32, 128), F32), face_of(next_part, 0))
+    nodes = newvel_ref[...] - (MESH_STEP / flag(flags_ref, 2)) * (gradient + second)
+    write_nodes(nodes, back_ref, out_ref)
 
 
 def copying(kernel, count):
@@ -720,7 +724,6 @@
     table = {name: jnp.asarray(value) for name, value in constants().items()}
     n_dom, n_sub = lax.axis_size("dom"), lax.axis_size("sub")
     up = [(i, i + 1) for i in range(n_dom - 1)]
-    down = [(i + 1, i) for i in range(n_dom - 1)]
 
     def pairs(start, size):
         return [p for i in range(start, size - 1, 2) for p in ((i, i + 1), (i + 1, i))]
@@ -764,21 +767,20 @@
     )
     slab = jnp.sum(lax.all_to_all(local, "dom", 0, 0, tiled=True), axis=0, keepdims=True)
     moments = lax.all_to_all(jnp.broadcast_to(slab, (n_sub, 128)), "sub", 0, 0, tiled=True)
-    newvel, moved, part, face1, face2 = call(
-        first_shape_kernel, [NODES, NODES, NODES, FACE, FACE], [(384, 384), (384, 384)]
-    )(moments, disp, vel, resid, image, live, flags, table["grad"], table["grad_t"], table["weight"])
-    first, second = swap(face1, face2)
+    newvel, moved, part, near, far, skip = call(
+        first_shape_kernel, [NODES, NODES, NODES, (160, 128), (160, 128), FACE],
+        [(384, 384), (384, 384)],
+    )(moments, disp, vel, resid, image, live, flags, table["off_z"], table["grad"], table["grad_t"],
+      table["weight"])
+    near = lax.ppermute(near, "dom", pairs(0, n_dom))
+    far = lax.ppermute(far, "dom", pairs(1, n_dom))
+    skip = lax.ppermute(skip, "dom", [(i + 2, i) for i in range(n_dom - 2)])
     (new_velocity,) = call(write_kernel, [(3, 1350)])(newvel, table["back"])
     part, new_velocity = lax.optimization_barrier((part, new_velocity))
-    base, face = call(
-        second_shape_kernel, [NODES, FACE], [(384, 384), (384, 384)]
-    )(part, first, second, flags, *walls, newvel, moved, live, table["grad"], table["grad_t"],
-      table["weight"])
-    from_above = lax.ppermute(face, "dom", down)
-    (mesh_base,) = call(write_kernel, [(3, 1350)])(base, table["back"])
-    (mesh_velocity,) = call(mesh_kernel, [(3, 1350)])(
-        mesh_base, from_above, flags, table["face_mask"], table["face_back"]
-    )
+    (mesh_velocity,) = call(
+        second_shape_kernel, [(3, 1350)], [(384, 384)] * 4
+    )(part, near, far, skip, flags, *walls, newvel, moved, live, table["grad"], table["grad_t"],
+      table["weight"], table["back"])
     return new_velocity, energy_rate, mesh_velocity
 
 

time: 99.1 us -> 96.2 us (0.971)
  waiting for transfers between devices: 13 us -> 9.95 us
    ppermute x1 -> x3, starting transfers between devices: 2.05 us -> 10.2 us  [the longest x1 4.26 us: body(): far = lax.ppermute(far, 'dom', pairs(1, n_dom))]
    ppermute x3 -> x2, starting transfers between devices: 12.6 us -> 8.38 us  [swap(): second = lax.ppermute(face2, 'dom', pairs(1, n_dom))]
    ppermute x3 -> x2, starting transfers between devices: 8.82 us -> 4.83 us  [swap(): return (lax.ppermute(face1, 'dom', pairs(0, n_dom)), second)]
    ppermute x3 -> x2, waiting for transfers between devices: 6.81 us -> 4.92 us  [swap(): second = lax.ppermute(face2, 'dom', pairs(1, n_dom))]
    ppermute x1 -> x3, waiting for transfers between devices: 4.83 us -> 3.65 us  [the longest x1 3.65 us: body(): skip = lax.ppermute(skip, 'dom', [(i + 2, i) for i in range(n_dom - 2)])]
    pallas_call x12 -> x10, Pallas kernels: 10.1 us -> 10.5 us  [run(): pl.pallas_call(body_of, out_shape=[jax.ShapeDtypeStruct(shape, F32) for s...]
  transfers between devices with their start and end apart: 10 -> 10, of which waited for: 5 -> 4; matrix products, arithmetic and copies ran while one was open for 0% -> 0% of each run, Pallas kernels for 4% -> 4%
where the time goes in v5:
time: 96.2 us; the launch traced here: 95.7 us
  blocking collectives  42.3 us (44%)
  starting transfers between devices  31.1 us (32%)
  Pallas kernels  10.5 us (11%)
  waiting for transfers between devices  9.95 us (10%)
  between operations  1.62 us (2%)
    all_to_all x1, blocking collectives, body(): lax.all_to_all(jnp.broadcast_to(slab, (n_sub, 128)), 'sub', 0, 0, tiled=T...  26.7 us
    all_to_all x1, blocking collectives, body(): lax.all_to_all(local, 'dom', 0, 0, tiled=True)  15.7 us
    pallas_call x10, Pallas kernels, run(): pl.pallas_call(body_of, out_shape=[jax.ShapeDtypeStruct(shape, F32) for s...  10.5 us
    ppermute x2, starting transfers between devices, swap(): second = lax.ppermute(face2, 'dom', pairs(1, n_dom))  8.38 us
    ppermute x2, waiting for transfers between devices, swap(): second = lax.ppermute(face2, 'dom', pairs(1, n_dom))  4.92 us
    ppermute x2, starting transfers between devices, swap(): return (lax.ppermute(face1, 'dom', pairs(0, n_dom)), second)  4.83 us
    ppermute x1, starting transfers between devices, body(): far = lax.ppermute(far, 'dom', pairs(1, n_dom))  4.26 us
    ppermute x1, starting transfers between devices, body(): first = lax.ppermute(z_first, 'sub', pairs(0, n_sub))  4 us
  transfers between devices with their start and end apart: 10, of which 4 were waited for; matrix products, arithmetic and copies ran while one was open for 0% of the time, Pallas kernels for 4%

profile of v5, /device:TPU:57, one launch (start us, length us, event | category | flops | bytes accessed | tf_op | source)
XLA Modules:
  0.0 95.7 jit_solution(7337852099553682393)
XLA Ops:
  0.6 0.8 shard_map.221
  1.5 3.0 %collective-permute-start = (f32[6,450]{1,0:T(8,128)S(1)}, f32[6,450]{1,0:T(8,128)S(1)}, u32[]{:S(2)}, u32[]{:S(2)}) collective-permute-start(f32[6,450]{1,0:T(8,128)S(1)} %shard_map.221), channel_id=1, source_target_pairs={{0,12},{12,24},{24,36},{36,48},{48,60},{60,72},{72,84},{84,96},{96... | collective-permute-start | bytes 32408 | tf_op jit(solution)/shard_map/ppermute | solution.py:734
  5.2 1.7 %shard_map.220 = (f32[400,128]{1,0:T(8,128)S(1)}, f32[8,128]{1,0:T(8,128)S(1)}) custom-call(f32[3,1350]{1,0:T(4,128)} %refs_0_.3, f32[3,1350]{1,0:T(4,128)} %refs_1_.3, f32[48,125]{1,0:T(8,128)} %bitcast.10, f32[27,48]{1,0:T(8,128)} %refs_3_.1, s32[1,48]{1,0:T(1,128)} %bitcast.11, bf16[450,128]{1,0:T(8,128)(2,1)} %constant.42.clone.refs_5_.pick_ref, ...), custom_call_target="tpu_custom_call" | custom-call | flops 1000000 | bytes 400000 | tf_op jit(solution)/shard_map/pallas_call | solution.py:705
  7.4 4.0 %collective-permute-start.1 = (f32[136,128]{1,0:T(8,128)S(1)}, f32[136,128]{1,0:T(8,128)S(1)}, u32[]{:S(2)}, u32[]{:S(2)}) collective-permute-start(f32[136,128]{1,0:T(8,128)S(1)} %get-tuple-element.37), channel_id=1, source_target_pairs={{0,1},{1,0},{2,3},{3,2},{4,5},{5,4},{6,7},{7,6},{8,9},{9,8},{10,11... | collective-permute-start | bytes 208904 | tf_op jit(solution)/shard_map/ppermute | solution.py:744
  11.4 0.7 collective-permute-start.2
  12.1 1.4 %collective-permute-done.1.first_ref = f32[136,128]{1,0:T(8,128)S(1)} collective-permute-done((f32[136,128]{1,0:T(8,128)S(1)}, f32[136,128]{1,0:T(8,128)S(1)}, u32[]{:S(2)}, u32[]{:S(2)}) %collective-permute-start.1) | collective-permute-done | bytes 69664 | tf_op jit(solution)/shard_map/ppermute | solution.py:744
  13.6 1.2 %shard_map.223 = (f32[120,128]{1,0:T(8,128)S(1)}, f32[32,128]{1,0:T(8,128)S(1)}, f32[32,128]{1,0:T(8,128)S(1)}, f32[120,128]{1,0:T(8,128)S(1)}, f32[120,128]{1,0...) custom-call(f32[400,128]{1,0:T(8,128)S(1)} %get-tuple-element.36.own, ...), custom_call_target="tpu_custom_call" | custom-call | flops 1000000 | bytes 400000 | tf_op jit(solution)/shard_map/pallas_call | solution.py:705
  14.7 2.9 %collective-permute-start.3 = (f32[32,128]{1,0:T(8,128)S(1)}, f32[32,128]{1,0:T(8,128)S(1)}, u32[]{:S(2)}, u32[]{:S(2)}) collective-permute-start(f32[32,128]{1,0:T(8,128)S(1)} %get-tuple-element.43), channel_id=1, source_target_pairs={{0,12},{12,0},{24,36},{36,24},{48,60},{60,48},{72,84},{84,72},{96,... | collective-permute-start | bytes 49160 | tf_op jit(solution)/shard_map/ppermute | solution.py:754
  17.7 4.2 %collective-permute-start.4 = (f32[32,128]{1,0:T(8,128)S(1)}, f32[32,128]{1,0:T(8,128)S(1)}, u32[]{:S(2)}, u32[]{:S(2)}) collective-permute-start(f32[32,128]{1,0:T(8,128)S(1)} %get-tuple-element.44), channel_id=1, source_target_pairs={{12,24},{24,12},{36,48},{48,36},{60,72},{72,60},{84,96},{96,84},{1... | collective-permute-start | bytes 49160 | tf_op jit(solution)/shard_map/ppermute | solution.py:753
  22.0 0.9 shard_map.224
  22.9 2.0 %collective-permute-done.4.second_ref = f32[32,128]{1,0:T(8,128)S(1)} collective-permute-done((f32[32,128]{1,0:T(8,128)S(1)}, f32[32,128]{1,0:T(8,128)S(1)}, u32[]{:S(2)}, u32[]{:S(2)}) %collective-permute-start.4) | collective-permute-done | bytes 16416 | tf_op jit(solution)/shard_map/ppermute | solution.py:753
  24.9 0.6 shard_map.225
  25.5 1.9 %collective-permute-start.5 = (f32[32,128]{1,0:T(8,128)S(1)}, f32[32,128]{1,0:T(8,128)S(1)}, u32[]{:S(2)}, u32[]{:S(2)}) collective-permute-start(f32[32,128]{1,0:T(8,128)S(1)} %get-tuple-element.47), channel_id=1, source_target_pairs={{0,12},{12,0},{24,36},{36,24},{48,60},{60,48},{72,84},{84,72},{96,... | collective-permute-start | bytes 49160 | tf_op jit(solution)/shard_map/ppermute | solution.py:754
  27.4 4.2 %collective-permute-start.6 = (f32[32,128]{1,0:T(8,128)S(1)}, f32[32,128]{1,0:T(8,128)S(1)}, u32[]{:S(2)}, u32[]{:S(2)}) collective-permute-start(f32[32,128]{1,0:T(8,128)S(1)} %get-tuple-element.48), channel_id=1, source_target_pairs={{12,24},{24,12},{36,48},{48,36},{60,72},{72,60},{84,96},{96,84},{1... | collective-permute-start | bytes 49160 | tf_op jit(solution)/shard_map/ppermute | solution.py:753
  31.6 3.0 %collective-permute-done.6.second_ref = f32[32,128]{1,0:T(8,128)S(1)} collective-permute-done((f32[32,128]{1,0:T(8,128)S(1)}, f32[32,128]{1,0:T(8,128)S(1)}, u32[]{:S(2)}, u32[]{:S(2)}) %collective-permute-start.6) | collective-permute-done | bytes 16416 | tf_op jit(solution)/shard_map/ppermute | solution.py:753
  35.0 15.7 %all_to_all.17 = f32[64,1,128]{2,1,0:T(1,128)S(1)} all-to-all(f32[64,1,128]{2,1,0:T(1,128)S(1)} %bitcast.8), channel_id=1, replica_groups=mesh['dom'=64,'sub'=12] {'dom'}, dimensions={0} | all-to-all | bytes 65536 | tf_op jit(solution)/shard_map/all_to_all | solution.py:768
  50.7 26.7 %all_to_all.18 = f32[12,1,128]{2,1,0:T(1,128)S(1)} all-to-all(f32[12,1,128]{2,1,0:T(1,128)S(1)} %broadcast_in_dim.11), channel_id=1, replica_groups=mesh['dom'=64,'sub'=12] {'sub'}, dimensions={0} | all-to-all | bytes 12288 | tf_op jit(solution)/shard_map/all_to_all | solution.py:769
  77.4 1.0 %shard_map.227 = (f32[120,128]{1,0:T(8,128)S(1)}, f32[120,128]{1,0:T(8,128)S(1)}, f32[120,128]{1,0:T(8,128)S(1)}, f32[160,128]{1,0:T(8,128)S(1)}, f32[160,128]{1,0:T(8,128)S(1)}, /*index=5*/f32[32,128]{1,0:T(8,128)S(1)}) custom-call(f32[12,128]{1,0:T(8,128)S(1)} %bitcast.9, f32[120,128]{1,0:T(8,128)S(1)} %get-tuple-element.51.disp_ref, ...), custom_call_target="tpu_custom_call" | custom-call | flops 1000000 | bytes 400000 | tf_op jit(solution)/shard_map/pallas_call | solution.py:705
  78.4 4.0 %collective-permute-start.7 = (f32[160,128]{1,0:T(8,128)S(1)}, f32[160,128]{1,0:T(8,128)S(1)}, u32[]{:S(2)}, u32[]{:S(2)}) collective-permute-start(f32[160,128]{1,0:T(8,128)S(1)} %get-tuple-element.61), channel_id=1, source_target_pairs={{0,12},{12,0},{24,36},{36,24},{48,60},{60,48},{72,84},{84,72},{96,... | collective-permute-start | bytes 245768 | tf_op jit(solution)/shard_map/ppermute | solution.py:775
  82.4 4.3 %collective-permute-start.8 = (f32[160,128]{1,0:T(8,128)S(1)}, f32[160,128]{1,0:T(8,128)S(1)}, u32[]{:S(2)}, u32[]{:S(2)}) collective-permute-start(f32[160,128]{1,0:T(8,128)S(1)} %get-tuple-element.62), channel_id=1, source_target_pairs={{12,24},{24,12},{36,48},{48,36},{60,72},{72,60},{84,96},{96,84},{1... | collective-permute-start | bytes 245768 | tf_op jit(solution)/shard_map/ppermute | solution.py:776
  86.7 1.9 %collective-permute-start.9 = (f32[32,128]{1,0:T(8,128)S(1)}, f32[32,128]{1,0:T(8,128)S(1)}, u32[]{:S(2)}, u32[]{:S(2)}) collective-permute-start(f32[32,128]{1,0:T(8,128)S(1)} %get-tuple-element.63), channel_id=1, source_target_pairs={{24,0},{36,12},{48,24},{60,36},{72,48},{84,60},{96,72},{108,84},{1... | collective-permute-start | bytes 49160 | tf_op jit(solution)/shard_map/ppermute | solution.py:777
  88.6 1.0 %shard_map.228 = f32[3,1350]{1,0:T(4,128)} custom-call(f32[120,128]{1,0:T(8,128)S(1)} %get-tuple-element.57.nodes_ref.newvel_ref, bf16[128,450]{1,0:T(8,128)(2,1)S(1)} %copy-done.3), custom_call_target="tpu_custom_call" | custom-call | flops 1000000 | bytes 400000 | tf_op jit(solution)/shard_map/pallas_call | solution.py:705
  89.6 3.6 %collective-permute-done.9.skip_ref = f32[32,128]{1,0:T(8,128)S(1)} collective-permute-done((f32[32,128]{1,0:T(8,128)S(1)}, f32[32,128]{1,0:T(8,128)S(1)}, u32[]{:S(2)}, u32[]{:S(2)}) %collective-permute-start.9) | collective-permute-done | bytes 16416 | tf_op jit(solution)/shard_map/ppermute | solution.py:777
  93.3 2.4 %shard_map.229 = f32[3,1350]{1,0:T(4,128)} custom-call(f32[120,128]{1,0:T(8,128)S(1)} %get-tuple-element.60.part_ref, f32[160,128]{1,0:T(8,128)S(1)} %collective-permute-done.7.near_ref, f32[160,128]{1,0:T(8,128)S(1)} %collective-permute-done.8.far_ref, f32[32,128]{1,0:T(8,128)S(1)} %collective-permute-done.9.skip_ref, ...), custom_call_target="tpu_custom_call" | custom-call | flops 1000000 | bytes 400000 | tf_op jit(solution)/shard_map/pallas_call | solution.py:705
  (41 shorter events, 1.1 us)
Async XLA Ops:
  1.5 5.4 %copy-start.4 = (bf16[450,128]{1,0:T(8,128)(2,1)S(1)}, bf16[450,128]{1,0:T(8,128)(2,1)}, u32[]{:S(2)}) copy-start(bf16[450,128]{1,0:T(8,128)(2,1)} %constant.42.clone.refs_5_.pick_ref) | copy-start | bytes 345604
  1.5 5.4 %collective-permute-start = (f32[6,450]{1,0:T(8,128)S(1)}, f32[6,450]{1,0:T(8,128)S(1)}, u32[]{:S(2)}, u32[]{:S(2)}) collective-permute-start(f32[6,450]{1,0:T(8,128)S(1)} %shard_map.221), channel_id=1, source_target_pairs={{0,12},{12,24},{24,36},{36,48},{48,60},{60,72},{72,84},{84,96},{96... | collective-permute-start | bytes 32408 | tf_op jit(solution)/shard_map/ppermute | solution.py:734
  5.2 8.3 %copy-start.2 = (f32[128,128]{1,0:T(8,128)S(1)}, f32[128,128]{1,0:T(8,128)}, u32[]{:S(2)}) copy-start(f32[128,128]{1,0:T(8,128)} %constant.40.clone.weight_ref) | copy-start | bytes 196612
  6.9 6.6 %copy-start = (bf16[384,240]{1,0:T(8,128)(2,1)S(1)}, bf16[384,240]{1,0:T(8,128)(2,1)}, u32[]{:S(2)}) copy-start(bf16[384,240]{1,0:T(8,128)(2,1)} %constant.34.clone.grad_ref) | copy-start | bytes 552964
  6.9 6.6 %copy-start.1 = (bf16[160,384]{1,0:T(8,128)(2,1)S(1)}, bf16[160,384]{1,0:T(8,128)(2,1)}, u32[]{:S(2)}) copy-start(bf16[160,384]{1,0:T(8,128)(2,1)} %constant.35.clone.grad_t_ref) | copy-start | bytes 368644
  6.9 6.6 %copy-start.10 = (bf16[128,96]{1,0:T(8,128)(2,1)S(1)}, bf16[128,96]{1,0:T(8,128)(2,1)}, u32[]{:S(2)}) copy-start(bf16[128,96]{1,0:T(8,128)(2,1)} %constant.38.clone.psi_ref) | copy-start | bytes 73732
  7.4 6.1 %collective-permute-start.1 = (f32[136,128]{1,0:T(8,128)S(1)}, f32[136,128]{1,0:T(8,128)S(1)}, u32[]{:S(2)}, u32[]{:S(2)}) collective-permute-start(f32[136,128]{1,0:T(8,128)S(1)} %get-tuple-element.37), channel_id=1, source_target_pairs={{0,1},{1,0},{2,3},{3,2},{4,5},{5,4},{6,7},{7,6},{8,9},{9,8},{10,11... | collective-permute-start | bytes 208904 | tf_op jit(solution)/shard_map/ppermute | solution.py:744
  11.4 2.1 %collective-permute-start.2 = (f32[136,128]{1,0:T(8,128)S(1)}, f32[136,128]{1,0:T(8,128)S(1)}, u32[]{:S(2)}, u32[]{:S(2)}) collective-permute-start(f32[136,128]{1,0:T(8,128)S(1)} %get-tuple-element.38), channel_id=1, source_target_pairs={{1,2},{2,1},{3,4},{4,3},{5,6},{6,5},{7,8},{8,7},{9,10},{10,9},{13,... | collective-permute-start | bytes 208904 | tf_op jit(solution)/shard_map/ppermute | solution.py:745
  13.5 8.3 %copy-start.11 = (bf16[128,48]{1,0:T(8,128)(2,1)S(1)}, bf16[128,48]{1,0:T(8,128)(2,1)}, u32[]{:S(2)}) copy-start(bf16[128,48]{1,0:T(8,128)(2,1)} %constant.47.clone.take_ref) | copy-start | bytes 36868
  13.6 8.3 %copy-start.13 = (bf16[64,128]{1,0:T(8,128)(2,1)S(1)}, bf16[64,128]{1,0:T(8,128)(2,1)}, u32[]{:S(2)}) copy-start(bf16[64,128]{1,0:T(8,128)(2,1)} %constant.39.clone.psi_t_ref) | copy-start | bytes 49156
  14.7 8.1 %collective-permute-start.3 = (f32[32,128]{1,0:T(8,128)S(1)}, f32[32,128]{1,0:T(8,128)S(1)}, u32[]{:S(2)}, u32[]{:S(2)}) collective-permute-start(f32[32,128]{1,0:T(8,128)S(1)} %get-tuple-element.43), channel_id=1, source_target_pairs={{0,12},{12,0},{24,36},{36,24},{48,60},{60,48},{72,84},{84,72},{96,... | collective-permute-start | bytes 49160 | tf_op jit(solution)/shard_map/ppermute | solution.py:754
  17.7 7.2 %collective-permute-start.4 = (f32[32,128]{1,0:T(8,128)S(1)}, f32[32,128]{1,0:T(8,128)S(1)}, u32[]{:S(2)}, u32[]{:S(2)}) collective-permute-start(f32[32,128]{1,0:T(8,128)S(1)} %get-tuple-element.44), channel_id=1, source_target_pairs={{12,24},{24,12},{36,48},{48,36},{60,72},{72,60},{84,96},{96,84},{1... | collective-permute-start | bytes 49160 | tf_op jit(solution)/shard_map/ppermute | solution.py:753
  21.9 3.0 %copy-start.5 = (f32[40,128]{1,0:T(8,128)S(1)}, f32[40,128]{1,0:T(8,128)}, u32[]{:S(2)}) copy-start(f32[40,128]{1,0:T(8,128)} %constant.45.clone.off_z_ref) | copy-start | bytes 61444
  21.9 2.9 %copy-start.6 = (bf16[128,240]{1,0:T(8,128)(2,1)S(1)}, bf16[128,240]{1,0:T(8,128)(2,1)}, u32[]{:S(2)}) copy-start(bf16[128,240]{1,0:T(8,128)(2,1)} %constant.36.clone.phi_ref) | copy-start | bytes 184324
  21.9 2.9 %copy-start.7 = (f32[40,128]{1,0:T(8,128)S(1)}, f32[40,128]{1,0:T(8,128)}, u32[]{:S(2)}) copy-start(f32[40,128]{1,0:T(8,128)} %constant.44.clone.off_x_ref) | copy-start | bytes 61444
  21.9 2.9 %copy-start.8 = (f32[40,128]{1,0:T(8,128)S(1)}, f32[40,128]{1,0:T(8,128)}, u32[]{:S(2)}) copy-start(f32[40,128]{1,0:T(8,128)} %constant.41.clone.own_ref) | copy-start | bytes 61444
  21.9 2.9 %copy-start.9 = (bf16[160,128]{1,0:T(8,128)(2,1)S(1)}, bf16[160,128]{1,0:T(8,128)(2,1)}, u32[]{:S(2)}) copy-start(bf16[160,128]{1,0:T(8,128)(2,1)} %constant.37.clone.phi_t_ref) | copy-start | bytes 122884
  22.0 2.9 %copy-start.12 = (f32[8,128]{1,0:T(8,128)S(1)}, f32[8,128]{1,0:T(8,128)}, u32[]{:S(2)}) copy-start(f32[8,128]{1,0:T(8,128)} %constant.48.clone.own_element_ref) | copy-start | bytes 12292
  25.5 6.1 %collective-permute-start.5 = (f32[32,128]{1,0:T(8,128)S(1)}, f32[32,128]{1,0:T(8,128)S(1)}, u32[]{:S(2)}, u32[]{:S(2)}) collective-permute-start(f32[32,128]{1,0:T(8,128)S(1)} %get-tuple-element.47), channel_id=1, source_target_pairs={{0,12},{12,0},{24,36},{36,24},{48,60},{60,48},{72,84},{84,72},{96,... | collective-permute-start | bytes 49160 | tf_op jit(solution)/shard_map/ppermute | solution.py:754
  27.4 7.2 %collective-permute-start.6 = (f32[32,128]{1,0:T(8,128)S(1)}, f32[32,128]{1,0:T(8,128)S(1)}, u32[]{:S(2)}, u32[]{:S(2)}) collective-permute-start(f32[32,128]{1,0:T(8,128)S(1)} %get-tuple-element.48), channel_id=1, source_target_pairs={{12,24},{24,12},{36,48},{48,36},{60,72},{72,60},{84,96},{96,84},{1... | collective-permute-start | bytes 49160 | tf_op jit(solution)/shard_map/ppermute | solution.py:753
  77.4 11.2 %copy-start.3 = (bf16[128,450]{1,0:T(8,128)(2,1)S(1)}, bf16[128,450]{1,0:T(8,128)(2,1)}, u32[]{:S(2)}) copy-start(bf16[128,450]{1,0:T(8,128)(2,1)} %constant.43.clone.back_ref) | copy-start | bytes 345604
  78.4 14.9 %collective-permute-start.7 = (f32[160,128]{1,0:T(8,128)S(1)}, f32[160,128]{1,0:T(8,128)S(1)}, u32[]{:S(2)}, u32[]{:S(2)}) collective-permute-start(f32[160,128]{1,0:T(8,128)S(1)} %get-tuple-element.61), channel_id=1, source_target_pairs={{0,12},{12,0},{24,36},{36,24},{48,60},{60,48},{72,84},{84,72},{96,... | collective-permute-start | bytes 245768 | tf_op jit(solution)/shard_map/ppermute | solution.py:775
  82.4 10.9 %collective-permute-start.8 = (f32[160,128]{1,0:T(8,128)S(1)}, f32[160,128]{1,0:T(8,128)S(1)}, u32[]{:S(2)}, u32[]{:S(2)}) collective-permute-start(f32[160,128]{1,0:T(8,128)S(1)} %get-tuple-element.62), channel_id=1, source_target_pairs={{12,24},{24,12},{36,48},{48,36},{60,72},{72,60},{84,96},{96,84},{1... | collective-permute-start | bytes 245768 | tf_op jit(solution)/shard_map/ppermute | solution.py:776
  86.7 6.6 %collective-permute-start.9 = (f32[32,128]{1,0:T(8,128)S(1)}, f32[32,128]{1,0:T(8,128)S(1)}, u32[]{:S(2)}, u32[]{:S(2)}) collective-permute-start(f32[32,128]{1,0:T(8,128)S(1)} %get-tuple-element.63), channel_id=1, source_target_pairs={{24,0},{36,12},{48,24},{60,36},{72,48},{84,60},{96,72},{108,84},{1... | collective-permute-start | bytes 49160 | tf_op jit(solution)/shard_map/ppermute | solution.py:777

commit v6 on v5

--- a/solution.py
+++ b/solution.py
@@ -309,26 +309,9 @@
     return jnp.broadcast_to(rest, shape) < 0.5
 
 
-def send_faces(nodes, flags_ref, first_ref, second_ref):
-    even = is_even(flags_ref, 0, (32, 128))
-    low, high = face_of(nodes, 0), face_of(nodes, 3)
-    first_ref[...] = jnp.where(even, high, low)
-    second_ref[...] = jnp.where(even, low, high)
-
-
 def z_wall(flags_ref, off_z_ref):
     wall = jnp.minimum(off_z_ref[...] + flag(flags_ref, 1), 1.0)
     return jnp.concatenate([wall, wall, wall], axis=0)
-
-
-def shared_sum(nodes, flags_ref, first_ref, second_ref, off_x_ref, off_z_ref):
-    even = is_even(flags_ref, 0, (32, 128))
-    first, second = first_ref[...], second_ref[...]
-    total = add_faces(nodes, jnp.where(even, second, first), jnp.where(even, first, second))
-    wall = jnp.minimum(off_x_ref[...] + flag(flags_ref, 0), 1.0) * jnp.minimum(
-        off_z_ref[...] + flag(flags_ref, 1), 1.0
-    )
-    return total * jnp.concatenate([wall, wall, wall], axis=0)
 
 
 def cofactors(j):
@@ -460,7 +443,7 @@
 
 
 def force_kernel(own_ref, first_ref, second_ref, grad_ref, grad_t_ref, psi_ref, weight_ref,
-                 flags_ref, force_ref, face1_ref, face2_ref, disp_ref, vel_ref, mass_ref, live_ref,
+                 flags_ref, message_ref, low_ref, high_ref, disp_ref, vel_ref, live_ref,
                  power_ref, wdens_ref, g_ref, flux_ref, point_ref):
     even = is_even(flags_ref, 1, (BLOCK, 128))
     first, second = first_ref[...], second_ref[...]
@@ -515,10 +498,11 @@
         power_ref[at, :] = live_weight * volume * power
         wdens = weight * mass_density
         wdens_ref[at, :] = wdens
-        mass_ref[at, :] = wdens * alive
+        message_ref[120 + 8 * chunk : 128 + 8 * chunk, :] = wdens * alive
     force = from_local(transposed_dot(grad_t_ref[...], flux_ref[...]))
-    force_ref[...] = force
-    send_faces(force, flags_ref, face1_ref, face2_ref)
+    message_ref[0:120, :] = force
+    low_ref[...] = face_of(force, 0)
+    high_ref[...] = face_of(force, 3)
 
 
 def energy_kernel(power_ref, wdens_ref, psi_t_ref, take_ref, out_ref):
@@ -550,33 +534,48 @@
     return total_of(nodes * nodes * jnp.concatenate([own, own, own], axis=0))
 
 
-def mass_kernel(part_ref, first_ref, second_ref, flags_ref, off_x_ref, off_z_ref, mass_ref, phi_ref,
-                phi_t_ref, own_ref, own_element_ref, resid_ref, image_ref, face1_ref, face2_ref,
-                sums_ref):
-    resid = shared_sum(part_ref[...], flags_ref, first_ref, second_ref, off_x_ref, off_z_ref)
+def mass_image(points, mass, phi_t_ref):
+    return from_local(
+        transposed_dot(phi_t_ref[...], points * jnp.concatenate([mass, mass, mass], axis=1))
+    )
+
+
+def krylov_kernel(message_ref, near_ref, far_ref, skip_up_ref, skip_down_ref, flags_ref, off_x_ref,
+                  off_z_ref, phi_ref, phi_t_ref, own_ref, own_element_ref, resid_ref, image_ref,
+                  out_ref):
+    even = is_even(flags_ref, 0, (248, 128))
+    near, far = near_ref[...], far_ref[...]
+    upper, lower = jnp.where(even, near, far), jnp.where(even, far, near)
+    force, mass = message_ref[0:120], message_ref[120:248]
+    wall = z_wall(flags_ref, off_z_ref)
+    dom = flag(flags_ref, 0)
+
+    def walls(place):
+        x_wall = jnp.minimum(off_x_ref[...] + jnp.maximum(place, 0.0), 1.0)
+        return wall * jnp.concatenate([x_wall, x_wall, x_wall], axis=0)
+
+    own_walls = walls(dom)
+    resid = add_faces(force, face_of(lower, 3), face_of(upper, 0)) * own_walls
+    resid_low = add_faces(lower[0:120], skip_up_ref[...], face_of(force, 0)) * walls(dom - 1.0)
+    resid_up = add_faces(upper[0:120], face_of(force, 3), skip_down_ref[...]) * wall
     resid_ref[...] = resid
     points = mass_points(resid, phi_ref)
-    mass = mass_ref[...]
-    image = from_local(
-        transposed_dot(phi_t_ref[...], points * jnp.concatenate([mass, mass, mass], axis=1))
-    )
+    part = mass_image(points, mass, phi_t_ref)
+    part_low = mass_image(mass_points(resid_low, phi_ref), lower[120:248], phi_t_ref)
+    part_up = mass_image(mass_points(resid_up, phi_ref), upper[120:248], phi_t_ref)
+    image = add_faces(part, face_of(part_low, 3), face_of(part_up, 0)) * own_walls
     image_ref[...] = image
-    send_faces(image, flags_ref, face1_ref, face2_ref)
-    norm = norm_of(resid, own_ref[...])
-    energy = point_energy(points, mass, own_element_ref[0:1])
-    lane = lax.broadcasted_iota(jnp.int32, (8, 128), 1)
-    sums_ref[...] = jnp.where(lane == 0, norm, jnp.where(lane == 1, energy, 0.0))
-
-
-def moment_kernel(part_ref, first_ref, second_ref, flags_ref, off_x_ref, off_z_ref, mass_ref, phi_ref,
-                  own_ref, own_element_ref, sums_ref, image_ref, out_ref):
-    image = shared_sum(part_ref[...], flags_ref, first_ref, second_ref, off_x_ref, off_z_ref)
-    image_ref[...] = image
-    points = mass_points(image, phi_ref)
-    norm = norm_of(image, own_ref[...])
-    energy = point_energy(points, mass_ref[...], own_element_ref[0:1])
+    own, own_element = own_ref[...], own_element_ref[0:1]
+    moments = (
+        norm_of(resid, own),
+        point_energy(points, mass, own_element),
+        norm_of(image, own),
+        point_energy(mass_points(image, phi_ref), mass, own_element),
+    )
     lane = lax.broadcasted_iota(jnp.int32, (1, 128), 1)
-    row = sums_ref[0:1] + jnp.where(lane == 2, norm, jnp.where(lane == 3, energy, 0.0))
+    row = jnp.zeros((1, 128), F32)
+    for i, moment in enumerate(moments):
+        row = jnp.where(lane == i, moment, row)
     out_ref[...] = jnp.broadcast_to(row, out_ref.shape)
 
 
@@ -743,27 +742,20 @@
     flags = jnp.where(row < 2, where, time_step)
     first = lax.ppermute(z_first, "sub", pairs(0, n_sub))
     second = lax.ppermute(z_second, "sub", pairs(1, n_sub))
-    force, face1, face2, disp, vel, mass, live, power, wdens = call(
+    message, low, high, disp, vel, live, power, wdens = call(
         force_kernel,
-        [NODES, FACE, FACE, NODES, NODES, POINTS, (8, 128), POINTS, POINTS],
+        [(248, 128), FACE, FACE, NODES, NODES, (8, 128), POINTS, POINTS],
         [(384, 768), (384, 384), POINTS],
     )(own, first, second, table["grad"], table["grad_t"], table["psi"], table["weight"], flags)
-
-    def swap(face1, face2):
-        second = lax.ppermute(face2, "dom", pairs(1, n_dom))
-        return lax.ppermute(face1, "dom", pairs(0, n_dom)), second
-
-    first, second = swap(face1, face2)
+    far = lax.ppermute(message, "dom", pairs(1, n_dom))
+    skip_up = lax.ppermute(high, "dom", [(i, i + 2) for i in range(n_dom - 2)])
+    skip_down = lax.ppermute(low, "dom", [(i + 2, i) for i in range(n_dom - 2)])
+    near = lax.ppermute(message, "dom", pairs(0, n_dom))
     (energy_rate,) = call(energy_kernel, [(27, 48)])(power, wdens, table["psi_t"], table["take"])
-    force, energy_rate = lax.optimization_barrier((force, energy_rate))
-    resid, image_part, face1, face2, sums = call(
-        mass_kernel, [NODES, NODES, FACE, FACE, (8, 128)]
-    )(force, first, second, flags, *walls, mass, table["phi"], table["phi_t"], table["own"],
-      table["own_element"])
-    first, second = swap(face1, face2)
-    image, local = call(moment_kernel, [NODES, (n_dom, 128)])(
-        image_part, first, second, flags, *walls, mass, table["phi"], table["own"],
-        table["own_element"], sums,
+    message, energy_rate = lax.optimization_barrier((message, energy_rate))
+    resid, image, local = call(krylov_kernel, [NODES, NODES, (n_dom, 128)])(
+        message, near, far, skip_up, skip_down, flags, *walls, table["phi"], table["phi_t"],
+        table["own"], table["own_element"],
     )
     slab = jnp.sum(lax.all_to_all(local, "dom", 0, 0, tiled=True), axis=0, keepdims=True)
     moments = lax.all_to_all(jnp.broadcast_to(slab, (n_sub, 128)), "sub", 0, 0, tiled=True)

time: 96.2 us -> 93.5 us (0.972)
  waiting for transfers between devices: 9.95 us -> 7.92 us
    ppermute x4, waiting for transfers between devices: 4.92 us -> 2.9 us  [the longest x1 2.89 us: body(): skip_down = lax.ppermute(low, 'dom', [(i + 2, i) for i in range(n_dom - 2)])]
    pallas_call x10 -> x9, Pallas kernels: 10.5 us -> 10.9 us  [run(): pl.pallas_call(body_of, out_shape=[jax.ShapeDtypeStruct(shape, F32) for s...]
  transfers between devices with their start and end apart: 10 -> 10, of which waited for: 4 -> 3; matrix products, arithmetic and copies ran while one was open for 0% -> 0% of each run, Pallas kernels for 4% -> 4%
where the time goes in v6:
time: 93.5 us; the launch traced here: 93 us
  blocking collectives  42.1 us (45%)
  starting transfers between devices  30.2 us (32%)
  Pallas kernels  10.9 us (12%)
  waiting for transfers between devices  7.92 us (8%)
  between operations  1.62 us (2%)
    all_to_all x1, blocking collectives, body(): lax.all_to_all(jnp.broadcast_to(slab, (n_sub, 128)), 'sub', 0, 0, tiled=T...  26.6 us
    all_to_all x1, blocking collectives, body(): lax.all_to_all(local, 'dom', 0, 0, tiled=True)  15.5 us
    pallas_call x9, Pallas kernels, run(): pl.pallas_call(body_of, out_shape=[jax.ShapeDtypeStruct(shape, F32) for s...  10.9 us
    ppermute x1, starting transfers between devices, body(): far = lax.ppermute(message, 'dom', pairs(1, n_dom))  5.18 us
    ppermute x1, starting transfers between devices, body(): far = lax.ppermute(far, 'dom', pairs(1, n_dom))  4.25 us
    ppermute x1, starting transfers between devices, body(): first = lax.ppermute(z_first, 'sub', pairs(0, n_sub))  4 us
    ppermute x1, starting transfers between devices, body(): near = lax.ppermute(near, 'dom', pairs(0, n_dom))  3.99 us
    ppermute x1, waiting for transfers between devices, body(): skip = lax.ppermute(skip, 'dom', [(i + 2, i) for i in range(n_dom - 2)])  3.65 us
  transfers between devices with their start and end apart: 10, of which 3 were waited for; matrix products, arithmetic and copies ran while one was open for 0% of the time, Pallas kernels for 4%

profile of v6, /device:TPU:57, one launch (start us, length us, event | category | flops | bytes accessed | tf_op | source)
XLA Modules:
  0.0 93.0 jit_solution(14986015346208829013)
XLA Ops:
  0.6 0.8 shard_map.221
  1.5 3.0 %collective-permute-start = (f32[6,450]{1,0:T(8,128)S(1)}, f32[6,450]{1,0:T(8,128)S(1)}, u32[]{:S(2)}, u32[]{:S(2)}) collective-permute-start(f32[6,450]{1,0:T(8,128)S(1)} %shard_map.221), channel_id=1, source_target_pairs={{0,12},{12,24},{24,36},{36,48},{48,60},{60,72},{72,84},{84,96},{96... | collective-permute-start | bytes 32408 | tf_op jit(solution)/shard_map/ppermute | solution.py:733
  5.2 1.7 %shard_map.220 = (f32[400,128]{1,0:T(8,128)S(1)}, f32[8,128]{1,0:T(8,128)S(1)}) custom-call(f32[3,1350]{1,0:T(4,128)} %refs_0_.3, f32[3,1350]{1,0:T(4,128)} %refs_1_.3, f32[48,125]{1,0:T(8,128)} %bitcast.10, f32[27,48]{1,0:T(8,128)} %refs_3_.1, s32[1,48]{1,0:T(1,128)} %bitcast.11, bf16[450,128]{1,0:T(8,128)(2,1)} %constant.42.clone.refs_5_.pick_ref, ...), custom_call_target="tpu_custom_call" | custom-call | flops 1000000 | bytes 400000 | tf_op jit(solution)/shard_map/pallas_call | solution.py:704
  6.9 0.4 shard_map.222
  7.4 4.0 %collective-permute-start.1 = (f32[136,128]{1,0:T(8,128)S(1)}, f32[136,128]{1,0:T(8,128)S(1)}, u32[]{:S(2)}, u32[]{:S(2)}) collective-permute-start(f32[136,128]{1,0:T(8,128)S(1)} %get-tuple-element.32), channel_id=1, source_target_pairs={{0,1},{1,0},{2,3},{3,2},{4,5},{5,4},{6,7},{7,6},{8,9},{9,8},{10,11... | collective-permute-start | bytes 208904 | tf_op jit(solution)/shard_map/ppermute | solution.py:743
  11.4 0.7 collective-permute-start.2
  12.1 1.4 %collective-permute-done.1.first_ref = f32[136,128]{1,0:T(8,128)S(1)} collective-permute-done((f32[136,128]{1,0:T(8,128)S(1)}, f32[136,128]{1,0:T(8,128)S(1)}, u32[]{:S(2)}, u32[]{:S(2)}) %collective-permute-start.1) | collective-permute-done | bytes 69664 | tf_op jit(solution)/shard_map/ppermute | solution.py:743
  13.6 1.2 %shard_map.223 = (f32[248,128]{1,0:T(8,128)S(1)}, f32[32,128]{1,0:T(8,128)S(1)}, f32[32,128]{1,0:T(8,128)S(1)}, f32[120,128]{1,0:T(8,128)S(1)}, f32[120,128]{1,0...) custom-call(f32[400,128]{1,0:T(8,128)S(1)} %get-tuple-element.31.own_ref, ...), custom_call_target="tpu_custom_call" | custom-call | flops 1000000 | bytes 400000 | tf_op jit(solution)/shard_map/pallas_call | solution.py:704
  14.7 5.2 %collective-permute-start.4 = (f32[248,128]{1,0:T(8,128)S(1)}, f32[248,128]{1,0:T(8,128)S(1)}, u32[]{:S(2)}, u32[]{:S(2)}) collective-permute-start(f32[248,128]{1,0:T(8,128)S(1)} %get-tuple-element.37.message_ref), channel_id=1, source_target_pairs={{12,24},{24,12},{36,48},{48,36},{60,72},{72,60},{84,96},{96,84},{1... | collective-permute-start | bytes 380936 | tf_op jit(solution)/shard_map/ppermute | solution.py:750
  19.9 1.9 %collective-permute-start.3 = (f32[248,128]{1,0:T(8,128)S(1)}, f32[248,128]{1,0:T(8,128)S(1)}, u32[]{:S(2)}, u32[]{:S(2)}) collective-permute-start(f32[248,128]{1,0:T(8,128)S(1)} %get-tuple-element.37.message_ref), channel_id=1, source_target_pairs={{0,12},{12,0},{24,36},{36,24},{48,60},{60,48},{72,84},{84,72},{96,... | collective-permute-start | bytes 380936 | tf_op jit(solution)/shard_map/ppermute | solution.py:753
  21.9 2.6 %collective-permute-start.5 = (f32[32,128]{1,0:T(8,128)S(1)}, f32[32,128]{1,0:T(8,128)S(1)}, u32[]{:S(2)}, u32[]{:S(2)}) collective-permute-start(f32[32,128]{1,0:T(8,128)S(1)} %get-tuple-element.38), channel_id=1, source_target_pairs={{0,24},{12,36},{24,48},{36,60},{48,72},{60,84},{72,96},{84,108},{9... | collective-permute-start | bytes 49160 | tf_op jit(solution)/shard_map/ppermute | solution.py:751
  24.5 2.7 %collective-permute-start.6 = (f32[32,128]{1,0:T(8,128)S(1)}, f32[32,128]{1,0:T(8,128)S(1)}, u32[]{:S(2)}, u32[]{:S(2)}) collective-permute-start(f32[32,128]{1,0:T(8,128)S(1)} %get-tuple-element.39), channel_id=1, source_target_pairs={{24,0},{36,12},{48,24},{60,36},{72,48},{84,60},{96,72},{108,84},{1... | collective-permute-start | bytes 49160 | tf_op jit(solution)/shard_map/ppermute | solution.py:752
  27.2 0.9 shard_map.224
  28.2 2.9 %collective-permute-done.6.skip_down_ref = f32[32,128]{1,0:T(8,128)S(1)} collective-permute-done((f32[32,128]{1,0:T(8,128)S(1)}, f32[32,128]{1,0:T(8,128)S(1)}, u32[]{:S(2)}, u32[]{:S(2)}) %collective-permute-start.6) | collective-permute-done | bytes 16416 | tf_op jit(solution)/shard_map/ppermute | solution.py:752
  31.1 1.4 %shard_map.225 = (f32[120,128]{1,0:T(8,128)S(1)}, f32[120,128]{1,0:T(8,128)S(1)}, f32[64,128]{1,0:T(8,128)S(1)}) custom-call(f32[248,128]{1,0:T(8,128)S(1)} %get-tuple-element.37.message_ref, f32[248,128]{1,0:T(8,128)S(1)} %collective-permute-done.3.near_ref, f32[248,128]{1,0:T(8,128)S(1)} %collective-permute-done.4.far_ref, ...), custom_call_target="tpu_custom_call" | custom-call | flops 1000000 | bytes 400000 | tf_op jit(solution)/shard_map/pallas_call | solution.py:704
  32.5 15.5 %all_to_all.17 = f32[64,1,128]{2,1,0:T(1,128)S(1)} all-to-all(f32[64,1,128]{2,1,0:T(1,128)S(1)} %bitcast.8), channel_id=1, replica_groups=mesh['dom'=64,'sub'=12] {'dom'}, dimensions={0} | all-to-all | bytes 65536 | tf_op jit(solution)/shard_map/all_to_all | solution.py:760
  48.1 26.6 %all_to_all.18 = f32[12,1,128]{2,1,0:T(1,128)S(1)} all-to-all(f32[12,1,128]{2,1,0:T(1,128)S(1)} %broadcast_in_dim.11), channel_id=1, replica_groups=mesh['dom'=64,'sub'=12] {'sub'}, dimensions={0} | all-to-all | bytes 12288 | tf_op jit(solution)/shard_map/all_to_all | solution.py:761
  74.7 1.0 %shard_map.226 = (f32[120,128]{1,0:T(8,128)S(1)}, f32[120,128]{1,0:T(8,128)S(1)}, f32[120,128]{1,0:T(8,128)S(1)}, f32[160,128]{1,0:T(8,128)S(1)}, f32[160,128]{1,0:T(8,128)S(1)}, /*index=5*/f32[32,128]{1,0:T(8,128)S(1)}) custom-call(f32[12,128]{1,0:T(8,128)S(1)} %bitcast.9, f32[120,128]{1,0:T(8,128)S(1)} %get-tuple-element.41.disp_ref, ...), custom_call_target="tpu_custom_call" | custom-call | flops 1000000 | bytes 400000 | tf_op jit(solution)/shard_map/pallas_call | solution.py:704
  75.7 4.0 %collective-permute-start.7 = (f32[160,128]{1,0:T(8,128)S(1)}, f32[160,128]{1,0:T(8,128)S(1)}, u32[]{:S(2)}, u32[]{:S(2)}) collective-permute-start(f32[160,128]{1,0:T(8,128)S(1)} %get-tuple-element.51), channel_id=1, source_target_pairs={{0,12},{12,0},{24,36},{36,24},{48,60},{60,48},{72,84},{84,72},{96,... | collective-permute-start | bytes 245768 | tf_op jit(solution)/shard_map/ppermute | solution.py:767
  79.7 4.3 %collective-permute-start.8 = (f32[160,128]{1,0:T(8,128)S(1)}, f32[160,128]{1,0:T(8,128)S(1)}, u32[]{:S(2)}, u32[]{:S(2)}) collective-permute-start(f32[160,128]{1,0:T(8,128)S(1)} %get-tuple-element.52), channel_id=1, source_target_pairs={{12,24},{24,12},{36,48},{48,36},{60,72},{72,60},{84,96},{96,84},{1... | collective-permute-start | bytes 245768 | tf_op jit(solution)/shard_map/ppermute | solution.py:768
  84.0 1.9 %collective-permute-start.9 = (f32[32,128]{1,0:T(8,128)S(1)}, f32[32,128]{1,0:T(8,128)S(1)}, u32[]{:S(2)}, u32[]{:S(2)}) collective-permute-start(f32[32,128]{1,0:T(8,128)S(1)} %get-tuple-element.53), channel_id=1, source_target_pairs={{24,0},{36,12},{48,24},{60,36},{72,48},{84,60},{96,72},{108,84},{1... | collective-permute-start | bytes 49160 | tf_op jit(solution)/shard_map/ppermute | solution.py:769
  85.9 1.0 %shard_map.227 = f32[3,1350]{1,0:T(4,128)} custom-call(f32[120,128]{1,0:T(8,128)S(1)} %get-tuple-element.47.nodes_ref.newvel_ref, bf16[128,450]{1,0:T(8,128)(2,1)S(1)} %copy-done.3), custom_call_target="tpu_custom_call" | custom-call | flops 1000000 | bytes 400000 | tf_op jit(solution)/shard_map/pallas_call | solution.py:704
  86.9 3.6 %collective-permute-done.9.skip_ref = f32[32,128]{1,0:T(8,128)S(1)} collective-permute-done((f32[32,128]{1,0:T(8,128)S(1)}, f32[32,128]{1,0:T(8,128)S(1)}, u32[]{:S(2)}, u32[]{:S(2)}) %collective-permute-start.9) | collective-permute-done | bytes 16416 | tf_op jit(solution)/shard_map/ppermute | solution.py:769
  90.6 2.4 %shard_map.228 = f32[3,1350]{1,0:T(4,128)} custom-call(f32[120,128]{1,0:T(8,128)S(1)} %get-tuple-element.50.part_ref, f32[160,128]{1,0:T(8,128)S(1)} %collective-permute-done.7.near_ref, f32[160,128]{1,0:T(8,128)S(1)} %collective-permute-done.8.far_ref, f32[32,128]{1,0:T(8,128)S(1)} %collective-permute-done.9.skip_ref, ...), custom_call_target="tpu_custom_call" | custom-call | flops 1000000 | bytes 400000 | tf_op jit(solution)/shard_map/pallas_call | solution.py:704
  (40 shorter events, 0.3 us)
Async XLA Ops:
  1.5 5.4 %copy-start.4 = (bf16[450,128]{1,0:T(8,128)(2,1)S(1)}, bf16[450,128]{1,0:T(8,128)(2,1)}, u32[]{:S(2)}) copy-start(bf16[450,128]{1,0:T(8,128)(2,1)} %constant.42.clone.refs_5_.pick_ref) | copy-start | bytes 345604
  1.5 5.4 %collective-permute-start = (f32[6,450]{1,0:T(8,128)S(1)}, f32[6,450]{1,0:T(8,128)S(1)}, u32[]{:S(2)}, u32[]{:S(2)}) collective-permute-start(f32[6,450]{1,0:T(8,128)S(1)} %shard_map.221), channel_id=1, source_target_pairs={{0,12},{12,24},{24,36},{36,48},{48,60},{60,72},{72,84},{84,96},{96... | collective-permute-start | bytes 32408 | tf_op jit(solution)/shard_map/ppermute | solution.py:733
  5.2 8.3 %copy-start.2 = (f32[128,128]{1,0:T(8,128)S(1)}, f32[128,128]{1,0:T(8,128)}, u32[]{:S(2)}) copy-start(f32[128,128]{1,0:T(8,128)} %constant.40.clone.weight_ref) | copy-start | bytes 196612
  6.9 6.6 %copy-start = (bf16[384,240]{1,0:T(8,128)(2,1)S(1)}, bf16[384,240]{1,0:T(8,128)(2,1)}, u32[]{:S(2)}) copy-start(bf16[384,240]{1,0:T(8,128)(2,1)} %constant.34.clone.grad_ref) | copy-start | bytes 552964
  6.9 6.6 %copy-start.1 = (bf16[160,384]{1,0:T(8,128)(2,1)S(1)}, bf16[160,384]{1,0:T(8,128)(2,1)}, u32[]{:S(2)}) copy-start(bf16[160,384]{1,0:T(8,128)(2,1)} %constant.35.clone.grad_t_ref) | copy-start | bytes 368644
  6.9 6.6 %copy-start.9 = (bf16[128,96]{1,0:T(8,128)(2,1)S(1)}, bf16[128,96]{1,0:T(8,128)(2,1)}, u32[]{:S(2)}) copy-start(bf16[128,96]{1,0:T(8,128)(2,1)} %constant.38.clone.psi_ref) | copy-start | bytes 73732
  7.4 6.1 %collective-permute-start.1 = (f32[136,128]{1,0:T(8,128)S(1)}, f32[136,128]{1,0:T(8,128)S(1)}, u32[]{:S(2)}, u32[]{:S(2)}) collective-permute-start(f32[136,128]{1,0:T(8,128)S(1)} %get-tuple-element.32), channel_id=1, source_target_pairs={{0,1},{1,0},{2,3},{3,2},{4,5},{5,4},{6,7},{7,6},{8,9},{9,8},{10,11... | collective-permute-start | bytes 208904 | tf_op jit(solution)/shard_map/ppermute | solution.py:743
  11.4 2.1 %collective-permute-start.2 = (f32[136,128]{1,0:T(8,128)S(1)}, f32[136,128]{1,0:T(8,128)S(1)}, u32[]{:S(2)}, u32[]{:S(2)}) collective-permute-start(f32[136,128]{1,0:T(8,128)S(1)} %get-tuple-element.33), channel_id=1, source_target_pairs={{1,2},{2,1},{3,4},{4,3},{5,6},{6,5},{7,8},{8,7},{9,10},{10,9},{13,... | collective-permute-start | bytes 208904 | tf_op jit(solution)/shard_map/ppermute | solution.py:744
  13.5 13.6 %copy-start.10 = (bf16[128,48]{1,0:T(8,128)(2,1)S(1)}, bf16[128,48]{1,0:T(8,128)(2,1)}, u32[]{:S(2)}) copy-start(bf16[128,48]{1,0:T(8,128)(2,1)} %constant.47.clone.take_ref) | copy-start | bytes 36868
  13.6 13.6 %copy-start.12 = (bf16[64,128]{1,0:T(8,128)(2,1)S(1)}, bf16[64,128]{1,0:T(8,128)(2,1)}, u32[]{:S(2)}) copy-start(bf16[64,128]{1,0:T(8,128)(2,1)} %constant.39.clone.psi_t_ref) | copy-start | bytes 49156
  14.7 16.3 %collective-permute-start.4 = (f32[248,128]{1,0:T(8,128)S(1)}, f32[248,128]{1,0:T(8,128)S(1)}, u32[]{:S(2)}, u32[]{:S(2)}) collective-permute-start(f32[248,128]{1,0:T(8,128)S(1)} %get-tuple-element.37.message_ref), channel_id=1, source_target_pairs={{12,24},{24,12},{36,48},{48,36},{60,72},{72,60},{84,96},{96,84},{1... | collective-permute-start | bytes 380936 | tf_op jit(solution)/shard_map/ppermute | solution.py:750
  19.9 11.1 %collective-permute-start.3 = (f32[248,128]{1,0:T(8,128)S(1)}, f32[248,128]{1,0:T(8,128)S(1)}, u32[]{:S(2)}, u32[]{:S(2)}) collective-permute-start(f32[248,128]{1,0:T(8,128)S(1)} %get-tuple-element.37.message_ref), channel_id=1, source_target_pairs={{0,12},{12,0},{24,36},{36,24},{48,60},{60,48},{72,84},{84,72},{96,... | collective-permute-start | bytes 380936 | tf_op jit(solution)/shard_map/ppermute | solution.py:753
  21.9 6.3 %collective-permute-start.5 = (f32[32,128]{1,0:T(8,128)S(1)}, f32[32,128]{1,0:T(8,128)S(1)}, u32[]{:S(2)}, u32[]{:S(2)}) collective-permute-start(f32[32,128]{1,0:T(8,128)S(1)} %get-tuple-element.38), channel_id=1, source_target_pairs={{0,24},{12,36},{24,48},{36,60},{48,72},{60,84},{72,96},{84,108},{9... | collective-permute-start | bytes 49160 | tf_op jit(solution)/shard_map/ppermute | solution.py:751
  24.5 6.6 %collective-permute-start.6 = (f32[32,128]{1,0:T(8,128)S(1)}, f32[32,128]{1,0:T(8,128)S(1)}, u32[]{:S(2)}, u32[]{:S(2)}) collective-permute-start(f32[32,128]{1,0:T(8,128)S(1)} %get-tuple-element.39), channel_id=1, source_target_pairs={{24,0},{36,12},{48,24},{60,36},{72,48},{84,60},{96,72},{108,84},{1... | collective-permute-start | bytes 49160 | tf_op jit(solution)/shard_map/ppermute | solution.py:752
  27.2 3.9 %copy-start.5 = (f32[40,128]{1,0:T(8,128)S(1)}, f32[40,128]{1,0:T(8,128)}, u32[]{:S(2)}) copy-start(f32[40,128]{1,0:T(8,128)} %constant.45.clone.off_z_ref) | copy-start | bytes 61444
  27.2 3.9 %copy-start.6 = (f32[40,128]{1,0:T(8,128)S(1)}, f32[40,128]{1,0:T(8,128)}, u32[]{:S(2)}) copy-start(f32[40,128]{1,0:T(8,128)} %constant.44.clone.off_x_ref) | copy-start | bytes 61444
  27.2 3.9 %copy-start.7 = (bf16[128,240]{1,0:T(8,128)(2,1)S(1)}, bf16[128,240]{1,0:T(8,128)(2,1)}, u32[]{:S(2)}) copy-start(bf16[128,240]{1,0:T(8,128)(2,1)} %constant.36.clone.phi_ref) | copy-start | bytes 184324
  27.2 3.9 %copy-start.8 = (bf16[160,128]{1,0:T(8,128)(2,1)S(1)}, bf16[160,128]{1,0:T(8,128)(2,1)}, u32[]{:S(2)}) copy-start(bf16[160,128]{1,0:T(8,128)(2,1)} %constant.37.clone.phi_t_ref) | copy-start | bytes 122884
  27.2 3.9 %copy-start.11 = (f32[40,128]{1,0:T(8,128)S(1)}, f32[40,128]{1,0:T(8,128)}, u32[]{:S(2)}) copy-start(f32[40,128]{1,0:T(8,128)} %constant.41.clone.own_ref) | copy-start | bytes 61444
  27.2 3.9 %copy-start.13 = (f32[8,128]{1,0:T(8,128)S(1)}, f32[8,128]{1,0:T(8,128)}, u32[]{:S(2)}) copy-start(f32[8,128]{1,0:T(8,128)} %constant.48.clone.own_element_ref) | copy-start | bytes 12292
  74.7 11.2 %copy-start.3 = (bf16[128,450]{1,0:T(8,128)(2,1)S(1)}, bf16[128,450]{1,0:T(8,128)(2,1)}, u32[]{:S(2)}) copy-start(bf16[128,450]{1,0:T(8,128)(2,1)} %constant.43.clone.back_ref) | copy-start | bytes 345604
  75.7 14.9 %collective-permute-start.7 = (f32[160,128]{1,0:T(8,128)S(1)}, f32[160,128]{1,0:T(8,128)S(1)}, u32[]{:S(2)}, u32[]{:S(2)}) collective-permute-start(f32[160,128]{1,0:T(8,128)S(1)} %get-tuple-element.51), channel_id=1, source_target_pairs={{0,12},{12,0},{24,36},{36,24},{48,60},{60,48},{72,84},{84,72},{96,... | collective-permute-start | bytes 245768 | tf_op jit(solution)/shard_map/ppermute | solution.py:767
  79.7 10.9 %collective-permute-start.8 = (f32[160,128]{1,0:T(8,128)S(1)}, f32[160,128]{1,0:T(8,128)S(1)}, u32[]{:S(2)}, u32[]{:S(2)}) collective-permute-start(f32[160,128]{1,0:T(8,128)S(1)} %get-tuple-element.52), channel_id=1, source_target_pairs={{12,24},{24,12},{36,48},{48,36},{60,72},{72,60},{84,96},{96,84},{1... | collective-permute-start | bytes 245768 | tf_op jit(solution)/shard_map/ppermute | solution.py:768
  84.0 6.6 %collective-permute-start.9 = (f32[32,128]{1,0:T(8,128)S(1)}, f32[32,128]{1,0:T(8,128)S(1)}, u32[]{:S(2)}, u32[]{:S(2)}) collective-permute-start(f32[32,128]{1,0:T(8,128)S(1)} %get-tuple-element.53), channel_id=1, source_target_pairs={{24,0},{36,12},{48,24},{60,36},{72,48},{84,60},{96,72},{108,84},{1... | collective-permute-start | bytes 49160 | tf_op jit(solution)/shard_map/ppermute | solution.py:769

commit v7 on v6

--- a/solution.py
+++ b/solution.py
@@ -309,6 +309,12 @@
     return jnp.broadcast_to(rest, shape) < 0.5
 
 
+def leads_pair(flags_ref):
+    place = flag(flags_ref, 0)
+    rest = place - 4.0 * jnp.floor(place * 0.25)
+    return jnp.broadcast_to(rest, (32, 128)) < 1.5
+
+
 def z_wall(flags_ref, off_z_ref):
     wall = jnp.minimum(off_z_ref[...] + flag(flags_ref, 1), 1.0)
     return jnp.concatenate([wall, wall, wall], axis=0)
@@ -443,7 +449,7 @@
 
 
 def force_kernel(own_ref, first_ref, second_ref, grad_ref, grad_t_ref, psi_ref, weight_ref,
-                 flags_ref, message_ref, low_ref, high_ref, disp_ref, vel_ref, live_ref,
+                 flags_ref, message_ref, skip1_ref, skip2_ref, disp_ref, vel_ref, live_ref,
                  power_ref, wdens_ref, g_ref, flux_ref, point_ref):
     even = is_even(flags_ref, 1, (BLOCK, 128))
     first, second = first_ref[...], second_ref[...]
@@ -501,8 +507,10 @@
         message_ref[120 + 8 * chunk : 128 + 8 * chunk, :] = wdens * alive
     force = from_local(transposed_dot(grad_t_ref[...], flux_ref[...]))
     message_ref[0:120, :] = force
-    low_ref[...] = face_of(force, 0)
-    high_ref[...] = face_of(force, 3)
+    low, high = face_of(force, 0), face_of(force, 3)
+    leads = leads_pair(flags_ref)
+    skip1_ref[...] = jnp.where(leads, high, low)
+    skip2_ref[...] = jnp.where(leads, low, high)
 
 
 def energy_kernel(power_ref, wdens_ref, psi_t_ref, take_ref, out_ref):
@@ -540,13 +548,16 @@
     )
 
 
-def krylov_kernel(message_ref, near_ref, far_ref, skip_up_ref, skip_down_ref, flags_ref, off_x_ref,
+def krylov_kernel(message_ref, near_ref, far_ref, skip1_ref, skip2_ref, flags_ref, off_x_ref,
                   off_z_ref, phi_ref, phi_t_ref, own_ref, own_element_ref, resid_ref, image_ref,
                   out_ref):
     even = is_even(flags_ref, 0, (248, 128))
     near, far = near_ref[...], far_ref[...]
     upper, lower = jnp.where(even, near, far), jnp.where(even, far, near)
     force, mass = message_ref[0:120], message_ref[120:248]
+    leads = leads_pair(flags_ref)
+    skip_down = jnp.where(leads, skip1_ref[...], skip2_ref[...])
+    skip_up = jnp.where(leads, skip2_ref[...], skip1_ref[...])
     wall = z_wall(flags_ref, off_z_ref)
     dom = flag(flags_ref, 0)
 
@@ -556,8 +567,8 @@
 
     own_walls = walls(dom)
     resid = add_faces(force, face_of(lower, 3), face_of(upper, 0)) * own_walls
-    resid_low = add_faces(lower[0:120], skip_up_ref[...], face_of(force, 0)) * walls(dom - 1.0)
-    resid_up = add_faces(upper[0:120], face_of(force, 3), skip_down_ref[...]) * wall
+    resid_low = add_faces(lower[0:120], skip_up, face_of(force, 0)) * walls(dom - 1.0)
+    resid_up = add_faces(upper[0:120], face_of(force, 3), skip_down) * wall
     resid_ref[...] = resid
     points = mass_points(resid, phi_ref)
     part = mass_image(points, mass, phi_t_ref)
@@ -742,19 +753,24 @@
     flags = jnp.where(row < 2, where, time_step)
     first = lax.ppermute(z_first, "sub", pairs(0, n_sub))
     second = lax.ppermute(z_second, "sub", pairs(1, n_sub))
-    message, low, high, disp, vel, live, power, wdens = call(
+    message, skip1, skip2, disp, vel, live, power, wdens = call(
         force_kernel,
         [(248, 128), FACE, FACE, NODES, NODES, (8, 128), POINTS, POINTS],
         [(384, 768), (384, 384), POINTS],
     )(own, first, second, table["grad"], table["grad_t"], table["psi"], table["weight"], flags)
     far = lax.ppermute(message, "dom", pairs(1, n_dom))
-    skip_up = lax.ppermute(high, "dom", [(i, i + 2) for i in range(n_dom - 2)])
-    skip_down = lax.ppermute(low, "dom", [(i + 2, i) for i in range(n_dom - 2)])
+
+    def two_apart(phase):
+        starts = [i for i in range(n_dom - 2) if (i % 4) // 2 == phase]
+        return [p for i in starts for p in ((i, i + 2), (i + 2, i))]
+
+    skip2 = lax.ppermute(skip2, "dom", two_apart(1))
+    skip1 = lax.ppermute(skip1, "dom", two_apart(0))
     near = lax.ppermute(message, "dom", pairs(0, n_dom))
     (energy_rate,) = call(energy_kernel, [(27, 48)])(power, wdens, table["psi_t"], table["take"])
     message, energy_rate = lax.optimization_barrier((message, energy_rate))
     resid, image, local = call(krylov_kernel, [NODES, NODES, (n_dom, 128)])(
-        message, near, far, skip_up, skip_down, flags, *walls, table["phi"], table["phi_t"],
+        message, near, far, skip1, skip2, flags, *walls, table["phi"], table["phi_t"],
         table["own"], table["own_element"],
     )
     slab = jnp.sum(lax.all_to_all(local, "dom", 0, 0, tiled=True), axis=0, keepdims=True)

time: 93.5 us -> 93.5 us (level)
  no operation moved by 1% of the time
where the time goes in v7:
time: 93.5 us; the launch traced here: 93 us
  blocking collectives  42.8 us (46%)
  starting transfers between devices  29.7 us (32%)
  Pallas kernels  10.9 us (12%)
  waiting for transfers between devices  7.76 us (8%)
  between operations  1.62 us (2%)
    all_to_all x1, blocking collectives, body(): lax.all_to_all(jnp.broadcast_to(slab, (n_sub, 128)), 'sub', 0, 0, tiled=T...  26.7 us
    all_to_all x1, blocking collectives, body(): lax.all_to_all(local, 'dom', 0, 0, tiled=True)  16.1 us
    pallas_call x9, Pallas kernels, run(): pl.pallas_call(body_of, out_shape=[jax.ShapeDtypeStruct(shape, F32) for s...  10.9 us
    ppermute x1, starting transfers between devices, body(): far = lax.ppermute(message, 'dom', pairs(1, n_dom))  5.18 us
    ppermute x1, starting transfers between devices, body(): far = lax.ppermute(far, 'dom', pairs(1, n_dom))  4.25 us
    ppermute x1, starting transfers between devices, body(): first = lax.ppermute(z_first, 'sub', pairs(0, n_sub))  4 us
    ppermute x1, starting transfers between devices, body(): near = lax.ppermute(near, 'dom', pairs(0, n_dom))  3.99 us
    ppermute x1, waiting for transfers between devices, body(): skip = lax.ppermute(skip, 'dom', [(i + 2, i) for i in range(n_dom - 2)])  3.65 us
  transfers between devices with their start and end apart: 10, of which 3 were waited for; matrix products, arithmetic and copies ran while one was open for 0% of the time, Pallas kernels for 4%

profile of v7, /device:TPU:57, one launch (start us, length us, event | category | flops | bytes accessed | tf_op | source)
XLA Modules:
  0.0 93.0 jit_solution(417674539396406608)
XLA Ops:
  0.6 0.8 shard_map.221
  1.5 3.0 %collective-permute-start = (f32[6,450]{1,0:T(8,128)S(1)}, f32[6,450]{1,0:T(8,128)S(1)}, u32[]{:S(2)}, u32[]{:S(2)}) collective-permute-start(f32[6,450]{1,0:T(8,128)S(1)} %shard_map.221), channel_id=1, source_target_pairs={{0,12},{12,24},{24,36},{36,48},{48,60},{60,72},{72,84},{84,96},{96... | collective-permute-start | bytes 32408 | tf_op jit(solution)/shard_map/ppermute | solution.py:744
  5.2 1.7 %shard_map.220 = (f32[400,128]{1,0:T(8,128)S(1)}, f32[8,128]{1,0:T(8,128)S(1)}) custom-call(f32[3,1350]{1,0:T(4,128)} %refs_0_.3, f32[3,1350]{1,0:T(4,128)} %refs_1_.3, f32[48,125]{1,0:T(8,128)} %bitcast.10, f32[27,48]{1,0:T(8,128)} %refs_3_.1, s32[1,48]{1,0:T(1,128)} %bitcast.11, bf16[450,128]{1,0:T(8,128)(2,1)} %constant.42.clone.refs_5_.pick_ref, ...), custom_call_target="tpu_custom_call" | custom-call | flops 1000000 | bytes 400000 | tf_op jit(solution)/shard_map/pallas_call | solution.py:715
  6.9 0.4 shard_map.222
  7.4 4.0 %collective-permute-start.1 = (f32[136,128]{1,0:T(8,128)S(1)}, f32[136,128]{1,0:T(8,128)S(1)}, u32[]{:S(2)}, u32[]{:S(2)}) collective-permute-start(f32[136,128]{1,0:T(8,128)S(1)} %get-tuple-element.32), channel_id=1, source_target_pairs={{0,1},{1,0},{2,3},{3,2},{4,5},{5,4},{6,7},{7,6},{8,9},{9,8},{10,11... | collective-permute-start | bytes 208904 | tf_op jit(solution)/shard_map/ppermute | solution.py:754
  11.4 0.7 collective-permute-start.2
  12.1 1.4 %collective-permute-done.1.first_ref = f32[136,128]{1,0:T(8,128)S(1)} collective-permute-done((f32[136,128]{1,0:T(8,128)S(1)}, f32[136,128]{1,0:T(8,128)S(1)}, u32[]{:S(2)}, u32[]{:S(2)}) %collective-permute-start.1) | collective-permute-done | bytes 69664 | tf_op jit(solution)/shard_map/ppermute | solution.py:754
  13.6 1.2 %shard_map.223 = (f32[248,128]{1,0:T(8,128)S(1)}, f32[32,128]{1,0:T(8,128)S(1)}, f32[32,128]{1,0:T(8,128)S(1)}, f32[120,128]{1,0:T(8,128)S(1)}, f32[120,128]{1,0...) custom-call(f32[400,128]{1,0:T(8,128)S(1)} %get-tuple-element.31.own_ref, ...), custom_call_target="tpu_custom_call" | custom-call | flops 1000000 | bytes 400000 | tf_op jit(solution)/shard_map/pallas_call | solution.py:715
  14.7 5.2 %collective-permute-start.4 = (f32[248,128]{1,0:T(8,128)S(1)}, f32[248,128]{1,0:T(8,128)S(1)}, u32[]{:S(2)}, u32[]{:S(2)}) collective-permute-start(f32[248,128]{1,0:T(8,128)S(1)} %get-tuple-element.37.message_ref), channel_id=1, source_target_pairs={{12,24},{24,12},{36,48},{48,36},{60,72},{72,60},{84,96},{96,84},{1... | collective-permute-start | bytes 380936 | tf_op jit(solution)/shard_map/ppermute | solution.py:761
  19.9 1.9 %collective-permute-start.3 = (f32[248,128]{1,0:T(8,128)S(1)}, f32[248,128]{1,0:T(8,128)S(1)}, u32[]{:S(2)}, u32[]{:S(2)}) collective-permute-start(f32[248,128]{1,0:T(8,128)S(1)} %get-tuple-element.37.message_ref), channel_id=1, source_target_pairs={{0,12},{12,0},{24,36},{36,24},{48,60},{60,48},{72,84},{84,72},{96,... | collective-permute-start | bytes 380936 | tf_op jit(solution)/shard_map/ppermute | solution.py:769
  21.9 1.9 %collective-permute-start.5 = (f32[32,128]{1,0:T(8,128)S(1)}, f32[32,128]{1,0:T(8,128)S(1)}, u32[]{:S(2)}, u32[]{:S(2)}) collective-permute-start(f32[32,128]{1,0:T(8,128)S(1)} %get-tuple-element.38), channel_id=1, source_target_pairs={{0,24},{24,0},{12,36},{36,12},{48,72},{72,48},{60,84},{84,60},{96,... | collective-permute-start | bytes 49160 | tf_op jit(solution)/shard_map/ppermute | solution.py:768
  23.8 2.9 %collective-permute-start.6 = (f32[32,128]{1,0:T(8,128)S(1)}, f32[32,128]{1,0:T(8,128)S(1)}, u32[]{:S(2)}, u32[]{:S(2)}) collective-permute-start(f32[32,128]{1,0:T(8,128)S(1)} %get-tuple-element.39), channel_id=1, source_target_pairs={{24,48},{48,24},{36,60},{60,36},{72,96},{96,72},{84,108},{108,84},... | collective-permute-start | bytes 49160 | tf_op jit(solution)/shard_map/ppermute | solution.py:767
  26.7 0.9 shard_map.224
  27.7 2.7 %collective-permute-done.6.skip2_ref = f32[32,128]{1,0:T(8,128)S(1)} collective-permute-done((f32[32,128]{1,0:T(8,128)S(1)}, f32[32,128]{1,0:T(8,128)S(1)}, u32[]{:S(2)}, u32[]{:S(2)}) %collective-permute-start.6) | collective-permute-done | bytes 16416 | tf_op jit(solution)/shard_map/ppermute | solution.py:767
  30.4 1.4 %shard_map.225 = (f32[120,128]{1,0:T(8,128)S(1)}, f32[120,128]{1,0:T(8,128)S(1)}, f32[64,128]{1,0:T(8,128)S(1)}) custom-call(f32[248,128]{1,0:T(8,128)S(1)} %get-tuple-element.37.message_ref, f32[248,128]{1,0:T(8,128)S(1)} %collective-permute-done.3.near_ref, f32[248,128]{1,0:T(8,128)S(1)} %collective-permute-done.4.far_ref, ...), custom_call_target="tpu_custom_call" | custom-call | flops 1000000 | bytes 400000 | tf_op jit(solution)/shard_map/pallas_call | solution.py:715
  31.9 16.1 %all_to_all.17 = f32[64,1,128]{2,1,0:T(1,128)S(1)} all-to-all(f32[64,1,128]{2,1,0:T(1,128)S(1)} %bitcast.8), channel_id=1, replica_groups=mesh['dom'=64,'sub'=12] {'dom'}, dimensions={0} | all-to-all | bytes 65536 | tf_op jit(solution)/shard_map/all_to_all | solution.py:776
  48.1 26.7 %all_to_all.18 = f32[12,1,128]{2,1,0:T(1,128)S(1)} all-to-all(f32[12,1,128]{2,1,0:T(1,128)S(1)} %broadcast_in_dim.11), channel_id=1, replica_groups=mesh['dom'=64,'sub'=12] {'sub'}, dimensions={0} | all-to-all | bytes 12288 | tf_op jit(solution)/shard_map/all_to_all | solution.py:777
  74.7 1.0 %shard_map.226 = (f32[120,128]{1,0:T(8,128)S(1)}, f32[120,128]{1,0:T(8,128)S(1)}, f32[120,128]{1,0:T(8,128)S(1)}, f32[160,128]{1,0:T(8,128)S(1)}, f32[160,128]{1,0:T(8,128)S(1)}, /*index=5*/f32[32,128]{1,0:T(8,128)S(1)}) custom-call(f32[12,128]{1,0:T(8,128)S(1)} %bitcast.9, f32[120,128]{1,0:T(8,128)S(1)} %get-tuple-element.41.disp_ref, ...), custom_call_target="tpu_custom_call" | custom-call | flops 1000000 | bytes 400000 | tf_op jit(solution)/shard_map/pallas_call | solution.py:715
  75.7 4.0 %collective-permute-start.7 = (f32[160,128]{1,0:T(8,128)S(1)}, f32[160,128]{1,0:T(8,128)S(1)}, u32[]{:S(2)}, u32[]{:S(2)}) collective-permute-start(f32[160,128]{1,0:T(8,128)S(1)} %get-tuple-element.51), channel_id=1, source_target_pairs={{0,12},{12,0},{24,36},{36,24},{48,60},{60,48},{72,84},{84,72},{96,... | collective-permute-start | bytes 245768 | tf_op jit(solution)/shard_map/ppermute | solution.py:783
  79.7 4.3 %collective-permute-start.8 = (f32[160,128]{1,0:T(8,128)S(1)}, f32[160,128]{1,0:T(8,128)S(1)}, u32[]{:S(2)}, u32[]{:S(2)}) collective-permute-start(f32[160,128]{1,0:T(8,128)S(1)} %get-tuple-element.52), channel_id=1, source_target_pairs={{12,24},{24,12},{36,48},{48,36},{60,72},{72,60},{84,96},{96,84},{1... | collective-permute-start | bytes 245768 | tf_op jit(solution)/shard_map/ppermute | solution.py:784
  84.0 1.9 %collective-permute-start.9 = (f32[32,128]{1,0:T(8,128)S(1)}, f32[32,128]{1,0:T(8,128)S(1)}, u32[]{:S(2)}, u32[]{:S(2)}) collective-permute-start(f32[32,128]{1,0:T(8,128)S(1)} %get-tuple-element.53), channel_id=1, source_target_pairs={{24,0},{36,12},{48,24},{60,36},{72,48},{84,60},{96,72},{108,84},{1... | collective-permute-start | bytes 49160 | tf_op jit(solution)/shard_map/ppermute | solution.py:785
  85.9 1.0 %shard_map.227 = f32[3,1350]{1,0:T(4,128)} custom-call(f32[120,128]{1,0:T(8,128)S(1)} %get-tuple-element.47.nodes_ref.newvel_ref, bf16[128,450]{1,0:T(8,128)(2,1)S(1)} %copy-done.3), custom_call_target="tpu_custom_call" | custom-call | flops 1000000 | bytes 400000 | tf_op jit(solution)/shard_map/pallas_call | solution.py:715
  86.9 3.6 %collective-permute-done.9.skip_ref = f32[32,128]{1,0:T(8,128)S(1)} collective-permute-done((f32[32,128]{1,0:T(8,128)S(1)}, f32[32,128]{1,0:T(8,128)S(1)}, u32[]{:S(2)}, u32[]{:S(2)}) %collective-permute-start.9) | collective-permute-done | bytes 16416 | tf_op jit(solution)/shard_map/ppermute | solution.py:785
  90.6 2.4 %shard_map.228 = f32[3,1350]{1,0:T(4,128)} custom-call(f32[120,128]{1,0:T(8,128)S(1)} %get-tuple-element.50.part_ref, f32[160,128]{1,0:T(8,128)S(1)} %collective-permute-done.7.near_ref, f32[160,128]{1,0:T(8,128)S(1)} %collective-permute-done.8.far_ref, f32[32,128]{1,0:T(8,128)S(1)} %collective-permute-done.9.skip_ref, ...), custom_call_target="tpu_custom_call" | custom-call | flops 1000000 | bytes 400000 | tf_op jit(solution)/shard_map/pallas_call | solution.py:715
  (40 shorter events, 0.3 us)
Async XLA Ops:
  1.5 5.4 %copy-start.4 = (bf16[450,128]{1,0:T(8,128)(2,1)S(1)}, bf16[450,128]{1,0:T(8,128)(2,1)}, u32[]{:S(2)}) copy-start(bf16[450,128]{1,0:T(8,128)(2,1)} %constant.42.clone.refs_5_.pick_ref) | copy-start | bytes 345604
  1.5 5.4 %collective-permute-start = (f32[6,450]{1,0:T(8,128)S(1)}, f32[6,450]{1,0:T(8,128)S(1)}, u32[]{:S(2)}, u32[]{:S(2)}) collective-permute-start(f32[6,450]{1,0:T(8,128)S(1)} %shard_map.221), channel_id=1, source_target_pairs={{0,12},{12,24},{24,36},{36,48},{48,60},{60,72},{72,84},{84,96},{96... | collective-permute-start | bytes 32408 | tf_op jit(solution)/shard_map/ppermute | solution.py:744
  5.2 8.3 %copy-start.2 = (f32[128,128]{1,0:T(8,128)S(1)}, f32[128,128]{1,0:T(8,128)}, u32[]{:S(2)}) copy-start(f32[128,128]{1,0:T(8,128)} %constant.40.clone.weight_ref) | copy-start | bytes 196612
  6.9 6.6 %copy-start = (bf16[384,240]{1,0:T(8,128)(2,1)S(1)}, bf16[384,240]{1,0:T(8,128)(2,1)}, u32[]{:S(2)}) copy-start(bf16[384,240]{1,0:T(8,128)(2,1)} %constant.34.clone.grad_ref) | copy-start | bytes 552964
  6.9 6.6 %copy-start.1 = (bf16[160,384]{1,0:T(8,128)(2,1)S(1)}, bf16[160,384]{1,0:T(8,128)(2,1)}, u32[]{:S(2)}) copy-start(bf16[160,384]{1,0:T(8,128)(2,1)} %constant.35.clone.grad_t_ref) | copy-start | bytes 368644
  6.9 6.6 %copy-start.9 = (bf16[128,96]{1,0:T(8,128)(2,1)S(1)}, bf16[128,96]{1,0:T(8,128)(2,1)}, u32[]{:S(2)}) copy-start(bf16[128,96]{1,0:T(8,128)(2,1)} %constant.38.clone.psi_ref) | copy-start | bytes 73732
  7.4 6.1 %collective-permute-start.1 = (f32[136,128]{1,0:T(8,128)S(1)}, f32[136,128]{1,0:T(8,128)S(1)}, u32[]{:S(2)}, u32[]{:S(2)}) collective-permute-start(f32[136,128]{1,0:T(8,128)S(1)} %get-tuple-element.32), channel_id=1, source_target_pairs={{0,1},{1,0},{2,3},{3,2},{4,5},{5,4},{6,7},{7,6},{8,9},{9,8},{10,11... | collective-permute-start | bytes 208904 | tf_op jit(solution)/shard_map/ppermute | solution.py:754
  11.4 2.1 %collective-permute-start.2 = (f32[136,128]{1,0:T(8,128)S(1)}, f32[136,128]{1,0:T(8,128)S(1)}, u32[]{:S(2)}, u32[]{:S(2)}) collective-permute-start(f32[136,128]{1,0:T(8,128)S(1)} %get-tuple-element.33), channel_id=1, source_target_pairs={{1,2},{2,1},{3,4},{4,3},{5,6},{6,5},{7,8},{8,7},{9,10},{10,9},{13,... | collective-permute-start | bytes 208904 | tf_op jit(solution)/shard_map/ppermute | solution.py:755
  13.5 13.1 %copy-start.10 = (bf16[128,48]{1,0:T(8,128)(2,1)S(1)}, bf16[128,48]{1,0:T(8,128)(2,1)}, u32[]{:S(2)}) copy-start(bf16[128,48]{1,0:T(8,128)(2,1)} %constant.47.clone.take_ref) | copy-start | bytes 36868
  13.6 13.1 %copy-start.12 = (bf16[64,128]{1,0:T(8,128)(2,1)S(1)}, bf16[64,128]{1,0:T(8,128)(2,1)}, u32[]{:S(2)}) copy-start(bf16[64,128]{1,0:T(8,128)(2,1)} %constant.39.clone.psi_t_ref) | copy-start | bytes 49156
  14.7 15.6 %collective-permute-start.4 = (f32[248,128]{1,0:T(8,128)S(1)}, f32[248,128]{1,0:T(8,128)S(1)}, u32[]{:S(2)}, u32[]{:S(2)}) collective-permute-start(f32[248,128]{1,0:T(8,128)S(1)} %get-tuple-element.37.message_ref), channel_id=1, source_target_pairs={{12,24},{24,12},{36,48},{48,36},{60,72},{72,60},{84,96},{96,84},{1... | collective-permute-start | bytes 380936 | tf_op jit(solution)/shard_map/ppermute | solution.py:761
  19.9 10.5 %collective-permute-start.3 = (f32[248,128]{1,0:T(8,128)S(1)}, f32[248,128]{1,0:T(8,128)S(1)}, u32[]{:S(2)}, u32[]{:S(2)}) collective-permute-start(f32[248,128]{1,0:T(8,128)S(1)} %get-tuple-element.37.message_ref), channel_id=1, source_target_pairs={{0,12},{12,0},{24,36},{36,24},{48,60},{60,48},{72,84},{84,72},{96,... | collective-permute-start | bytes 380936 | tf_op jit(solution)/shard_map/ppermute | solution.py:769
  21.9 5.8 %collective-permute-start.5 = (f32[32,128]{1,0:T(8,128)S(1)}, f32[32,128]{1,0:T(8,128)S(1)}, u32[]{:S(2)}, u32[]{:S(2)}) collective-permute-start(f32[32,128]{1,0:T(8,128)S(1)} %get-tuple-element.38), channel_id=1, source_target_pairs={{0,24},{24,0},{12,36},{36,12},{48,72},{72,48},{60,84},{84,60},{96,... | collective-permute-start | bytes 49160 | tf_op jit(solution)/shard_map/ppermute | solution.py:768
  23.8 6.6 %collective-permute-start.6 = (f32[32,128]{1,0:T(8,128)S(1)}, f32[32,128]{1,0:T(8,128)S(1)}, u32[]{:S(2)}, u32[]{:S(2)}) collective-permute-start(f32[32,128]{1,0:T(8,128)S(1)} %get-tuple-element.39), channel_id=1, source_target_pairs={{24,48},{48,24},{36,60},{60,36},{72,96},{96,72},{84,108},{108,84},... | collective-permute-start | bytes 49160 | tf_op jit(solution)/shard_map/ppermute | solution.py:767
  26.7 3.7 %copy-start.5 = (f32[40,128]{1,0:T(8,128)S(1)}, f32[40,128]{1,0:T(8,128)}, u32[]{:S(2)}) copy-start(f32[40,128]{1,0:T(8,128)} %constant.45.clone.off_z_ref) | copy-start | bytes 61444
  26.7 3.7 %copy-start.6 = (f32[40,128]{1,0:T(8,128)S(1)}, f32[40,128]{1,0:T(8,128)}, u32[]{:S(2)}) copy-start(f32[40,128]{1,0:T(8,128)} %constant.44.clone.off_x_ref) | copy-start | bytes 61444
  26.7 3.7 %copy-start.7 = (bf16[128,240]{1,0:T(8,128)(2,1)S(1)}, bf16[128,240]{1,0:T(8,128)(2,1)}, u32[]{:S(2)}) copy-start(bf16[128,240]{1,0:T(8,128)(2,1)} %constant.36.clone.phi_ref) | copy-start | bytes 184324
  26.7 3.7 %copy-start.8 = (bf16[160,128]{1,0:T(8,128)(2,1)S(1)}, bf16[160,128]{1,0:T(8,128)(2,1)}, u32[]{:S(2)}) copy-start(bf16[160,128]{1,0:T(8,128)(2,1)} %constant.37.clone.phi_t_ref) | copy-start | bytes 122884
  26.7 3.7 %copy-start.11 = (f32[40,128]{1,0:T(8,128)S(1)}, f32[40,128]{1,0:T(8,128)}, u32[]{:S(2)}) copy-start(f32[40,128]{1,0:T(8,128)} %constant.41.clone.own_ref) | copy-start | bytes 61444
  26.7 3.7 %copy-start.13 = (f32[8,128]{1,0:T(8,128)S(1)}, f32[8,128]{1,0:T(8,128)}, u32[]{:S(2)}) copy-start(f32[8,128]{1,0:T(8,128)} %constant.48.clone.own_element_ref) | copy-start | bytes 12292
  74.7 11.2 %copy-start.3 = (bf16[128,450]{1,0:T(8,128)(2,1)S(1)}, bf16[128,450]{1,0:T(8,128)(2,1)}, u32[]{:S(2)}) copy-start(bf16[128,450]{1,0:T(8,128)(2,1)} %constant.43.clone.back_ref) | copy-start | bytes 345604
  75.7 14.9 %collective-permute-start.7 = (f32[160,128]{1,0:T(8,128)S(1)}, f32[160,128]{1,0:T(8,128)S(1)}, u32[]{:S(2)}, u32[]{:S(2)}) collective-permute-start(f32[160,128]{1,0:T(8,128)S(1)} %get-tuple-element.51), channel_id=1, source_target_pairs={{0,12},{12,0},{24,36},{36,24},{48,60},{60,48},{72,84},{84,72},{96,... | collective-permute-start | bytes 245768 | tf_op jit(solution)/shard_map/ppermute | solution.py:783
  79.7 10.9 %collective-permute-start.8 = (f32[160,128]{1,0:T(8,128)S(1)}, f32[160,128]{1,0:T(8,128)S(1)}, u32[]{:S(2)}, u32[]{:S(2)}) collective-permute-start(f32[160,128]{1,0:T(8,128)S(1)} %get-tuple-element.52), channel_id=1, source_target_pairs={{12,24},{24,12},{36,48},{48,36},{60,72},{72,60},{84,96},{96,84},{1... | collective-permute-start | bytes 245768 | tf_op jit(solution)/shard_map/ppermute | solution.py:784
  84.0 6.6 %collective-permute-start.9 = (f32[32,128]{1,0:T(8,128)S(1)}, f32[32,128]{1,0:T(8,128)S(1)}, u32[]{:S(2)}, u32[]{:S(2)}) collective-permute-start(f32[32,128]{1,0:T(8,128)S(1)} %get-tuple-element.53), channel_id=1, source_target_pairs={{24,0},{36,12},{48,24},{60,36},{72,48},{84,60},{96,72},{108,84},{1... | collective-permute-start | bytes 49160 | tf_op jit(solution)/shard_map/ppermute | solution.py:785

commit v8 on v7

--- a/solution.py
+++ b/solution.py
@@ -769,12 +769,12 @@
     near = lax.ppermute(message, "dom", pairs(0, n_dom))
     (energy_rate,) = call(energy_kernel, [(27, 48)])(power, wdens, table["psi_t"], table["take"])
     message, energy_rate = lax.optimization_barrier((message, energy_rate))
-    resid, image, local = call(krylov_kernel, [NODES, NODES, (n_dom, 128)])(
+    resid, image, local = call(krylov_kernel, [NODES, NODES, (n_sub, 128)])(
         message, near, far, skip1, skip2, flags, *walls, table["phi"], table["phi_t"],
         table["own"], table["own_element"],
     )
-    slab = jnp.sum(lax.all_to_all(local, "dom", 0, 0, tiled=True), axis=0, keepdims=True)
-    moments = lax.all_to_all(jnp.broadcast_to(slab, (n_sub, 128)), "sub", 0, 0, tiled=True)
+    column = jnp.sum(lax.all_to_all(local, "sub", 0, 0, tiled=True), axis=0, keepdims=True)
+    moments = lax.all_to_all(jnp.broadcast_to(column, (n_dom, 128)), "dom", 0, 0, tiled=True)
     newvel, moved, part, near, far, skip = call(
         first_shape_kernel, [NODES, NODES, NODES, (160, 128), (160, 128), FACE],
         [(384, 384), (384, 384)],

time: 93.5 us -> 93.5 us (level)
  blocking collectives: 42.8 us -> 44.2 us
  starting transfers between devices: 29.7 us -> 28.3 us
    all_to_all x2, blocking collectives: 42.8 us -> 44.2 us  [the longest x1 26.6 us: body(): lax.all_to_all(local, 'sub', 0, 0, tiled=True)]
    ppermute x1, starting transfers between devices: 3.99 us -> 2.56 us  [body(): near = lax.ppermute(near, 'dom', pairs(0, n_dom))]
where the time goes in v8:
time: 93.5 us; the launch traced here: 93 us
  blocking collectives  44.2 us (47%)
  starting transfers between devices  28.3 us (30%)
  Pallas kernels  10.9 us (12%)
  waiting for transfers between devices  7.76 us (8%)
  between operations  1.62 us (2%)
    all_to_all x1, blocking collectives, body(): lax.all_to_all(local, 'sub', 0, 0, tiled=True)  26.6 us
    all_to_all x1, blocking collectives, body(): lax.all_to_all(jnp.broadcast_to(column, (n_dom, 128)), 'dom', 0, 0, tiled...  17.6 us
    pallas_call x9, Pallas kernels, run(): pl.pallas_call(body_of, out_shape=[jax.ShapeDtypeStruct(shape, F32) for s...  10.9 us
    ppermute x1, starting transfers between devices, body(): far = lax.ppermute(message, 'dom', pairs(1, n_dom))  5.18 us
    ppermute x1, starting transfers between devices, body(): far = lax.ppermute(far, 'dom', pairs(1, n_dom))  4.26 us
    ppermute x1, starting transfers between devices, body(): first = lax.ppermute(z_first, 'sub', pairs(0, n_sub))  4 us
    ppermute x1, waiting for transfers between devices, body(): skip = lax.ppermute(skip, 'dom', [(i + 2, i) for i in range(n_dom - 2)])  3.65 us
    ppermute x1, starting transfers between devices, body(): halo = lax.ppermute(last, 'dom', up)  3.02 us
  transfers between devices with their start and end apart: 10, of which 3 were waited for; matrix products, arithmetic and copies ran while one was open for 0% of the time, Pallas kernels for 4%

profile of v8, /device:TPU:57, one launch (start us, length us, event | category | flops | bytes accessed | tf_op | source)
XLA Modules:
  0.0 93.0 jit_solution(11710152823682021016)
XLA Ops:
  0.6 0.8 shard_map.221
  1.5 3.0 %collective-permute-start = (f32[6,450]{1,0:T(8,128)S(1)}, f32[6,450]{1,0:T(8,128)S(1)}, u32[]{:S(2)}, u32[]{:S(2)}) collective-permute-start(f32[6,450]{1,0:T(8,128)S(1)} %shard_map.221), channel_id=1, source_target_pairs={{0,12},{12,24},{24,36},{36,48},{48,60},{60,72},{72,84},{84,96},{96... | collective-permute-start | bytes 32408 | tf_op jit(solution)/shard_map/ppermute | solution.py:744
  5.2 1.7 %shard_map.220 = (f32[400,128]{1,0:T(8,128)S(1)}, f32[8,128]{1,0:T(8,128)S(1)}) custom-call(f32[3,1350]{1,0:T(4,128)} %refs_0_.3, f32[3,1350]{1,0:T(4,128)} %refs_1_.3, f32[48,125]{1,0:T(8,128)} %bitcast.6, f32[27,48]{1,0:T(8,128)} %refs_3_.1, s32[1,48]{1,0:T(1,128)} %bitcast.7, bf16[450,128]{1,0:T(8,128)(2,1)} %constant.42.clone.refs_5_.pick_ref, ...), custom_call_target="tpu_custom_call" | custom-call | flops 1000000 | bytes 400000 | tf_op jit(solution)/shard_map/pallas_call | solution.py:715
  6.9 0.4 shard_map.222
  7.4 4.0 %collective-permute-start.1 = (f32[136,128]{1,0:T(8,128)S(1)}, f32[136,128]{1,0:T(8,128)S(1)}, u32[]{:S(2)}, u32[]{:S(2)}) collective-permute-start(f32[136,128]{1,0:T(8,128)S(1)} %get-tuple-element.32), channel_id=1, source_target_pairs={{0,1},{1,0},{2,3},{3,2},{4,5},{5,4},{6,7},{7,6},{8,9},{9,8},{10,11... | collective-permute-start | bytes 208904 | tf_op jit(solution)/shard_map/ppermute | solution.py:754
  11.4 0.7 collective-permute-start.2
  12.1 1.4 %collective-permute-done.1.first_ref = f32[136,128]{1,0:T(8,128)S(1)} collective-permute-done((f32[136,128]{1,0:T(8,128)S(1)}, f32[136,128]{1,0:T(8,128)S(1)}, u32[]{:S(2)}, u32[]{:S(2)}) %collective-permute-start.1) | collective-permute-done | bytes 69664 | tf_op jit(solution)/shard_map/ppermute | solution.py:754
  13.6 1.2 %shard_map.223 = (f32[248,128]{1,0:T(8,128)S(1)}, f32[32,128]{1,0:T(8,128)S(1)}, f32[32,128]{1,0:T(8,128)S(1)}, f32[120,128]{1,0:T(8,128)S(1)}, f32[120,128]{1,0...) custom-call(f32[400,128]{1,0:T(8,128)S(1)} %get-tuple-element.31.own_ref, ...), custom_call_target="tpu_custom_call" | custom-call | flops 1000000 | bytes 400000 | tf_op jit(solution)/shard_map/pallas_call | solution.py:715
  14.7 5.2 %collective-permute-start.4 = (f32[248,128]{1,0:T(8,128)S(1)}, f32[248,128]{1,0:T(8,128)S(1)}, u32[]{:S(2)}, u32[]{:S(2)}) collective-permute-start(f32[248,128]{1,0:T(8,128)S(1)} %get-tuple-element.37.message_ref), channel_id=1, source_target_pairs={{12,24},{24,12},{36,48},{48,36},{60,72},{72,60},{84,96},{96,84},{1... | collective-permute-start | bytes 380936 | tf_op jit(solution)/shard_map/ppermute | solution.py:761
  19.9 1.9 %collective-permute-start.3 = (f32[248,128]{1,0:T(8,128)S(1)}, f32[248,128]{1,0:T(8,128)S(1)}, u32[]{:S(2)}, u32[]{:S(2)}) collective-permute-start(f32[248,128]{1,0:T(8,128)S(1)} %get-tuple-element.37.message_ref), channel_id=1, source_target_pairs={{0,12},{12,0},{24,36},{36,24},{48,60},{60,48},{72,84},{84,72},{96,... | collective-permute-start | bytes 380936 | tf_op jit(solution)/shard_map/ppermute | solution.py:769
  21.9 1.9 %collective-permute-start.5 = (f32[32,128]{1,0:T(8,128)S(1)}, f32[32,128]{1,0:T(8,128)S(1)}, u32[]{:S(2)}, u32[]{:S(2)}) collective-permute-start(f32[32,128]{1,0:T(8,128)S(1)} %get-tuple-element.38), channel_id=1, source_target_pairs={{0,24},{24,0},{12,36},{36,12},{48,72},{72,48},{60,84},{84,60},{96,... | collective-permute-start | bytes 49160 | tf_op jit(solution)/shard_map/ppermute | solution.py:768
  23.8 2.9 %collective-permute-start.6 = (f32[32,128]{1,0:T(8,128)S(1)}, f32[32,128]{1,0:T(8,128)S(1)}, u32[]{:S(2)}, u32[]{:S(2)}) collective-permute-start(f32[32,128]{1,0:T(8,128)S(1)} %get-tuple-element.39), channel_id=1, source_target_pairs={{24,48},{48,24},{36,60},{60,36},{72,96},{96,72},{84,108},{108,84},... | collective-permute-start | bytes 49160 | tf_op jit(solution)/shard_map/ppermute | solution.py:767
  26.7 0.9 shard_map.224
  27.7 2.7 %collective-permute-done.6.skip2_ref = f32[32,128]{1,0:T(8,128)S(1)} collective-permute-done((f32[32,128]{1,0:T(8,128)S(1)}, f32[32,128]{1,0:T(8,128)S(1)}, u32[]{:S(2)}, u32[]{:S(2)}) %collective-permute-start.6) | collective-permute-done | bytes 16416 | tf_op jit(solution)/shard_map/ppermute | solution.py:767
  30.4 1.4 %shard_map.225 = (f32[120,128]{1,0:T(8,128)S(1)}, f32[120,128]{1,0:T(8,128)S(1)}, f32[12,128]{1,0:T(8,128)S(1)}) custom-call(f32[248,128]{1,0:T(8,128)S(1)} %get-tuple-element.37.message_ref, f32[248,128]{1,0:T(8,128)S(1)} %collective-permute-done.3.near_ref, f32[248,128]{1,0:T(8,128)S(1)} %collective-permute-done.4.far_ref, ...), custom_call_target="tpu_custom_call" | custom-call | flops 1000000 | bytes 400000 | tf_op jit(solution)/shard_map/pallas_call | solution.py:715
  31.9 26.6 %all_to_all.17 = f32[12,1,128]{2,1,0:T(1,128)S(1)} all-to-all(f32[12,1,128]{2,1,0:T(1,128)S(1)} %copy.24), channel_id=1, replica_groups=mesh['dom'=64,'sub'=12] {'sub'}, dimensions={0} | all-to-all | bytes 12288 | tf_op jit(solution)/shard_map/all_to_all | solution.py:776
  58.6 17.6 %all_to_all.18 = f32[64,1,128]{2,1,0:T(1,128)S(1)} all-to-all(f32[64,1,128]{2,1,0:T(1,128)S(1)} %broadcast_in_dim.11), channel_id=1, replica_groups=mesh['dom'=64,'sub'=12] {'dom'}, dimensions={0} | all-to-all | bytes 65536 | tf_op jit(solution)/shard_map/all_to_all | solution.py:777
  76.1 1.0 %shard_map.226 = (f32[120,128]{1,0:T(8,128)S(1)}, f32[120,128]{1,0:T(8,128)S(1)}, f32[120,128]{1,0:T(8,128)S(1)}, f32[160,128]{1,0:T(8,128)S(1)}, f32[160,128]{1,0:T(8,128)S(1)}, /*index=5*/f32[32,128]{1,0:T(8,128)S(1)}) custom-call(f32[64,128]{1,0:T(8,128)S(1)} %bitcast.4, f32[120,128]{1,0:T(8,128)S(1)} %get-tuple-element.41.disp_ref, ...), custom_call_target="tpu_custom_call" | custom-call | flops 1000000 | bytes 400000 | tf_op jit(solution)/shard_map/pallas_call | solution.py:715
  77.2 2.6 %collective-permute-start.7 = (f32[160,128]{1,0:T(8,128)S(1)}, f32[160,128]{1,0:T(8,128)S(1)}, u32[]{:S(2)}, u32[]{:S(2)}) collective-permute-start(f32[160,128]{1,0:T(8,128)S(1)} %get-tuple-element.51), channel_id=1, source_target_pairs={{0,12},{12,0},{24,36},{36,24},{48,60},{60,48},{72,84},{84,72},{96,... | collective-permute-start | bytes 245768 | tf_op jit(solution)/shard_map/ppermute | solution.py:783
  79.7 4.3 %collective-permute-start.8 = (f32[160,128]{1,0:T(8,128)S(1)}, f32[160,128]{1,0:T(8,128)S(1)}, u32[]{:S(2)}, u32[]{:S(2)}) collective-permute-start(f32[160,128]{1,0:T(8,128)S(1)} %get-tuple-element.52), channel_id=1, source_target_pairs={{12,24},{24,12},{36,48},{48,36},{60,72},{72,60},{84,96},{96,84},{1... | collective-permute-start | bytes 245768 | tf_op jit(solution)/shard_map/ppermute | solution.py:784
  84.0 1.9 %collective-permute-start.9 = (f32[32,128]{1,0:T(8,128)S(1)}, f32[32,128]{1,0:T(8,128)S(1)}, u32[]{:S(2)}, u32[]{:S(2)}) collective-permute-start(f32[32,128]{1,0:T(8,128)S(1)} %get-tuple-element.53), channel_id=1, source_target_pairs={{24,0},{36,12},{48,24},{60,36},{72,48},{84,60},{96,72},{108,84},{1... | collective-permute-start | bytes 49160 | tf_op jit(solution)/shard_map/ppermute | solution.py:785
  85.9 1.0 %shard_map.227 = f32[3,1350]{1,0:T(4,128)} custom-call(f32[120,128]{1,0:T(8,128)S(1)} %get-tuple-element.47.nodes_ref.newvel_ref, bf16[128,450]{1,0:T(8,128)(2,1)S(1)} %copy-done.3), custom_call_target="tpu_custom_call" | custom-call | flops 1000000 | bytes 400000 | tf_op jit(solution)/shard_map/pallas_call | solution.py:715
  86.9 3.6 %collective-permute-done.9.skip_ref = f32[32,128]{1,0:T(8,128)S(1)} collective-permute-done((f32[32,128]{1,0:T(8,128)S(1)}, f32[32,128]{1,0:T(8,128)S(1)}, u32[]{:S(2)}, u32[]{:S(2)}) %collective-permute-start.9) | collective-permute-done | bytes 16416 | tf_op jit(solution)/shard_map/ppermute | solution.py:785
  90.6 2.4 %shard_map.228 = f32[3,1350]{1,0:T(4,128)} custom-call(f32[120,128]{1,0:T(8,128)S(1)} %get-tuple-element.50.part_ref, f32[160,128]{1,0:T(8,128)S(1)} %collective-permute-done.7.near_ref, f32[160,128]{1,0:T(8,128)S(1)} %collective-permute-done.8.far_ref, f32[32,128]{1,0:T(8,128)S(1)} %collective-permute-done.9.skip_ref, ...), custom_call_target="tpu_custom_call" | custom-call | flops 1000000 | bytes 400000 | tf_op jit(solution)/shard_map/pallas_call | solution.py:715
  (40 shorter events, 0.3 us)
Async XLA Ops:
  1.5 5.4 %copy-start.4 = (bf16[450,128]{1,0:T(8,128)(2,1)S(1)}, bf16[450,128]{1,0:T(8,128)(2,1)}, u32[]{:S(2)}) copy-start(bf16[450,128]{1,0:T(8,128)(2,1)} %constant.42.clone.refs_5_.pick_ref) | copy-start | bytes 345604
  1.5 5.4 %collective-permute-start = (f32[6,450]{1,0:T(8,128)S(1)}, f32[6,450]{1,0:T(8,128)S(1)}, u32[]{:S(2)}, u32[]{:S(2)}) collective-permute-start(f32[6,450]{1,0:T(8,128)S(1)} %shard_map.221), channel_id=1, source_target_pairs={{0,12},{12,24},{24,36},{36,48},{48,60},{60,72},{72,84},{84,96},{96... | collective-permute-start | bytes 32408 | tf_op jit(solution)/shard_map/ppermute | solution.py:744
  5.2 8.3 %copy-start.2 = (f32[128,128]{1,0:T(8,128)S(1)}, f32[128,128]{1,0:T(8,128)}, u32[]{:S(2)}) copy-start(f32[128,128]{1,0:T(8,128)} %constant.40.clone.weight_ref) | copy-start | bytes 196612
  6.9 6.6 %copy-start = (bf16[384,240]{1,0:T(8,128)(2,1)S(1)}, bf16[384,240]{1,0:T(8,128)(2,1)}, u32[]{:S(2)}) copy-start(bf16[384,240]{1,0:T(8,128)(2,1)} %constant.34.clone.grad_ref) | copy-start | bytes 552964
  6.9 6.6 %copy-start.1 = (bf16[160,384]{1,0:T(8,128)(2,1)S(1)}, bf16[160,384]{1,0:T(8,128)(2,1)}, u32[]{:S(2)}) copy-start(bf16[160,384]{1,0:T(8,128)(2,1)} %constant.35.clone.grad_t_ref) | copy-start | bytes 368644
  6.9 6.6 %copy-start.9 = (bf16[128,96]{1,0:T(8,128)(2,1)S(1)}, bf16[128,96]{1,0:T(8,128)(2,1)}, u32[]{:S(2)}) copy-start(bf16[128,96]{1,0:T(8,128)(2,1)} %constant.38.clone.psi_ref) | copy-start | bytes 73732
  7.4 6.1 %collective-permute-start.1 = (f32[136,128]{1,0:T(8,128)S(1)}, f32[136,128]{1,0:T(8,128)S(1)}, u32[]{:S(2)}, u32[]{:S(2)}) collective-permute-start(f32[136,128]{1,0:T(8,128)S(1)} %get-tuple-element.32), channel_id=1, source_target_pairs={{0,1},{1,0},{2,3},{3,2},{4,5},{5,4},{6,7},{7,6},{8,9},{9,8},{10,11... | collective-permute-start | bytes 208904 | tf_op jit(solution)/shard_map/ppermute | solution.py:754
  11.4 2.1 %collective-permute-start.2 = (f32[136,128]{1,0:T(8,128)S(1)}, f32[136,128]{1,0:T(8,128)S(1)}, u32[]{:S(2)}, u32[]{:S(2)}) collective-permute-start(f32[136,128]{1,0:T(8,128)S(1)} %get-tuple-element.33), channel_id=1, source_target_pairs={{1,2},{2,1},{3,4},{4,3},{5,6},{6,5},{7,8},{8,7},{9,10},{10,9},{13,... | collective-permute-start | bytes 208904 | tf_op jit(solution)/shard_map/ppermute | solution.py:755
  13.5 13.1 %copy-start.10 = (bf16[128,48]{1,0:T(8,128)(2,1)S(1)}, bf16[128,48]{1,0:T(8,128)(2,1)}, u32[]{:S(2)}) copy-start(bf16[128,48]{1,0:T(8,128)(2,1)} %constant.47.clone.take_ref) | copy-start | bytes 36868
  13.6 13.1 %copy-start.12 = (bf16[64,128]{1,0:T(8,128)(2,1)S(1)}, bf16[64,128]{1,0:T(8,128)(2,1)}, u32[]{:S(2)}) copy-start(bf16[64,128]{1,0:T(8,128)(2,1)} %constant.39.clone.psi_t_ref) | copy-start | bytes 49156
  14.7 15.6 %collective-permute-start.4 = (f32[248,128]{1,0:T(8,128)S(1)}, f32[248,128]{1,0:T(8,128)S(1)}, u32[]{:S(2)}, u32[]{:S(2)}) collective-permute-start(f32[248,128]{1,0:T(8,128)S(1)} %get-tuple-element.37.message_ref), channel_id=1, source_target_pairs={{12,24},{24,12},{36,48},{48,36},{60,72},{72,60},{84,96},{96,84},{1... | collective-permute-start | bytes 380936 | tf_op jit(solution)/shard_map/ppermute | solution.py:761
  19.9 10.5 %collective-permute-start.3 = (f32[248,128]{1,0:T(8,128)S(1)}, f32[248,128]{1,0:T(8,128)S(1)}, u32[]{:S(2)}, u32[]{:S(2)}) collective-permute-start(f32[248,128]{1,0:T(8,128)S(1)} %get-tuple-element.37.message_ref), channel_id=1, source_target_pairs={{0,12},{12,0},{24,36},{36,24},{48,60},{60,48},{72,84},{84,72},{96,... | collective-permute-start | bytes 380936 | tf_op jit(solution)/shard_map/ppermute | solution.py:769
  21.9 5.8 %collective-permute-start.5 = (f32[32,128]{1,0:T(8,128)S(1)}, f32[32,128]{1,0:T(8,128)S(1)}, u32[]{:S(2)}, u32[]{:S(2)}) collective-permute-start(f32[32,128]{1,0:T(8,128)S(1)} %get-tuple-element.38), channel_id=1, source_target_pairs={{0,24},{24,0},{12,36},{36,12},{48,72},{72,48},{60,84},{84,60},{96,... | collective-permute-start | bytes 49160 | tf_op jit(solution)/shard_map/ppermute | solution.py:768
  23.8 6.6 %collective-permute-start.6 = (f32[32,128]{1,0:T(8,128)S(1)}, f32[32,128]{1,0:T(8,128)S(1)}, u32[]{:S(2)}, u32[]{:S(2)}) collective-permute-start(f32[32,128]{1,0:T(8,128)S(1)} %get-tuple-element.39), channel_id=1, source_target_pairs={{24,48},{48,24},{36,60},{60,36},{72,96},{96,72},{84,108},{108,84},... | collective-permute-start | bytes 49160 | tf_op jit(solution)/shard_map/ppermute | solution.py:767
  26.7 3.7 %copy-start.5 = (f32[40,128]{1,0:T(8,128)S(1)}, f32[40,128]{1,0:T(8,128)}, u32[]{:S(2)}) copy-start(f32[40,128]{1,0:T(8,128)} %constant.45.clone.off_z_ref) | copy-start | bytes 61444
  26.7 3.7 %copy-start.6 = (f32[40,128]{1,0:T(8,128)S(1)}, f32[40,128]{1,0:T(8,128)}, u32[]{:S(2)}) copy-start(f32[40,128]{1,0:T(8,128)} %constant.44.clone.off_x_ref) | copy-start | bytes 61444
  26.7 3.7 %copy-start.7 = (bf16[128,240]{1,0:T(8,128)(2,1)S(1)}, bf16[128,240]{1,0:T(8,128)(2,1)}, u32[]{:S(2)}) copy-start(bf16[128,240]{1,0:T(8,128)(2,1)} %constant.36.clone.phi_ref) | copy-start | bytes 184324
  26.7 3.7 %copy-start.8 = (bf16[160,128]{1,0:T(8,128)(2,1)S(1)}, bf16[160,128]{1,0:T(8,128)(2,1)}, u32[]{:S(2)}) copy-start(bf16[160,128]{1,0:T(8,128)(2,1)} %constant.37.clone.phi_t_ref) | copy-start | bytes 122884
  26.7 3.7 %copy-start.11 = (f32[40,128]{1,0:T(8,128)S(1)}, f32[40,128]{1,0:T(8,128)}, u32[]{:S(2)}) copy-start(f32[40,128]{1,0:T(8,128)} %constant.41.clone.own_ref) | copy-start | bytes 61444
  26.7 3.7 %copy-start.13 = (f32[8,128]{1,0:T(8,128)S(1)}, f32[8,128]{1,0:T(8,128)}, u32[]{:S(2)}) copy-start(f32[8,128]{1,0:T(8,128)} %constant.48.clone.own_element_ref) | copy-start | bytes 12292
  76.1 9.8 %copy-start.3 = (bf16[128,450]{1,0:T(8,128)(2,1)S(1)}, bf16[128,450]{1,0:T(8,128)(2,1)}, u32[]{:S(2)}) copy-start(bf16[128,450]{1,0:T(8,128)(2,1)} %constant.43.clone.back_ref) | copy-start | bytes 345604
  77.2 13.4 %collective-permute-start.7 = (f32[160,128]{1,0:T(8,128)S(1)}, f32[160,128]{1,0:T(8,128)S(1)}, u32[]{:S(2)}, u32[]{:S(2)}) collective-permute-start(f32[160,128]{1,0:T(8,128)S(1)} %get-tuple-element.51), channel_id=1, source_target_pairs={{0,12},{12,0},{24,36},{36,24},{48,60},{60,48},{72,84},{84,72},{96,... | collective-permute-start | bytes 245768 | tf_op jit(solution)/shard_map/ppermute | solution.py:783
  79.7 10.9 %collective-permute-start.8 = (f32[160,128]{1,0:T(8,128)S(1)}, f32[160,128]{1,0:T(8,128)S(1)}, u32[]{:S(2)}, u32[]{:S(2)}) collective-permute-start(f32[160,128]{1,0:T(8,128)S(1)} %get-tuple-element.52), channel_id=1, source_target_pairs={{12,24},{24,12},{36,48},{48,36},{60,72},{72,60},{84,96},{96,84},{1... | collective-permute-start | bytes 245768 | tf_op jit(solution)/shard_map/ppermute | solution.py:784
  84.0 6.6 %collective-permute-start.9 = (f32[32,128]{1,0:T(8,128)S(1)}, f32[32,128]{1,0:T(8,128)S(1)}, u32[]{:S(2)}, u32[]{:S(2)}) collective-permute-start(f32[32,128]{1,0:T(8,128)S(1)} %get-tuple-element.53), channel_id=1, source_target_pairs={{24,0},{36,12},{48,24},{60,36},{72,48},{84,60},{96,72},{108,84},{1... | collective-permute-start | bytes 49160 | tf_op jit(solution)/shard_map/ppermute | solution.py:785
